TPU v7x, 8 devices: a whole 2x2x1 slice. The times are simulated.
8 devices in a mesh: dp: 1 (over z), tp: 2 (over y), cp: 4 (over x, core).
Axes of the slice: x: 2, y: 2, z: 1, core: 2. Of those that a mesh axis runs over, the one named last changes fastest.
Arguments:
- x_in: bfloat16 [4096, 2048], P(('dp', 'cp', 'tp'))
- w_query: bfloat16 [2048, 32, 64], P(None, 'tp')
- w_key: bfloat16 [2048, 8, 64], P(None, 'tp')
- w_value: bfloat16 [2048, 8, 64], P(None, 'tp')
- w_out: bfloat16 [32, 64, 2048], P('tp')
- d_out: bfloat16 [4096, 2048], P(('dp', 'cp', 'tp'))
Outputs:
- output 1: bfloat16 [4096, 2048], P(('dp', 'cp', 'tp'))
- output 2: bfloat16 [4096, 2048], P(('dp', 'cp', 'tp'))
- output 3: bfloat16 [4, 2048, 32, 64], P(('dp', 'cp'), None, 'tp')
- output 4: bfloat16 [4, 2048, 8, 64], P(('dp', 'cp'), None, 'tp')
- output 5: bfloat16 [4, 2048, 8, 64], P(('dp', 'cp'), None, 'tp')
- output 6: bfloat16 [4, 32, 64, 2048], P(('dp', 'cp'), 'tp')
All inputs are finite; a program needn't handle non-finite values.
Results may differ from a plain program's by a relative error of at most 0.0112094.
Values are sent between devices in bfloat16 or wider.
A program may use at most 1 GiB of HBM per device.

v0:
```python
import jax
import jax.numpy as jnp
from jax import lax
from jax.sharding import PartitionSpec as P

ROW_SPEC = P(("dp", "cp", "tp"), None)
HEAD_SPEC = P(None, "tp", None)
OUT_W_SPEC = P("tp", None, None)
GRAD_SPEC = P(("dp", "cp"), None, "tp", None)
GRAD_OUT_SPEC = P(("dp", "cp"), "tp", None, None)
COLS_CONTRACT = (((1,), (1,)), ((), ()))
ROWS_CONTRACT = (((0,), (0,)), ((), ()))


def causal_where(pos_pair, values, fill):
    q_pos, k_pos = pos_pair
    return jnp.where(q_pos[:, None, None, None] >= k_pos[None, None, None, :], values, fill)


def attend_update(softmax_state, q_rows, k_blk, v_blk, pos_pair):
    row_max, row_sum, out_acc = softmax_state
    attn_scale = q_rows.shape[-1] ** -0.5
    scores = jnp.einsum("qhgd,khd->qhgk", q_rows, k_blk, preferred_element_type=jnp.float32) * attn_scale
    if pos_pair is not None:
        scores = causal_where(pos_pair, scores, -jnp.inf)
    new_max = jnp.maximum(row_max, jnp.max(scores, axis=-1))
    prob_mat = jnp.exp(scores - new_max[..., None])
    factor = jnp.exp(row_max - new_max)
    new_sum = row_sum * factor + jnp.sum(prob_mat, axis=-1)
    pv_part = jnp.einsum("qhgk,khd->qhgd", prob_mat.astype(jnp.bfloat16), v_blk, preferred_element_type=jnp.float32)
    return new_max, new_sum, out_acc * factor[..., None] + pv_part


def grad_update(q_rows, do_rows, lse_rows, dot_rows, k_blk, v_blk, pos_pair):
    attn_scale = q_rows.shape[-1] ** -0.5
    scores = jnp.einsum("qhgd,khd->qhgk", q_rows, k_blk, preferred_element_type=jnp.float32) * attn_scale
    prob_mat = jnp.exp(scores - lse_rows[..., None])
    if pos_pair is not None:
        prob_mat = causal_where(pos_pair, prob_mat, 0.0)
    d_probs = jnp.einsum("qhgd,khd->qhgk", do_rows, v_blk, preferred_element_type=jnp.float32)
    d_scores = (prob_mat * (d_probs - dot_rows[..., None])).astype(jnp.bfloat16)
    dv_part = jnp.einsum("qhgk,qhgd->khd", prob_mat.astype(jnp.bfloat16), do_rows, preferred_element_type=jnp.float32)
    dk_part = jnp.einsum("qhgk,qhgd->khd", d_scores, q_rows, preferred_element_type=jnp.float32) * attn_scale
    dq_part = jnp.einsum("qhgk,khd->qhgd", d_scores, k_blk, preferred_element_type=jnp.float32) * attn_scale
    return dq_part, dk_part, dv_part


def forward_branches(q_cur, half_rows, k_blk, v_blk):
    def from_earlier(state_old):
        return attend_update(state_old, q_cur, k_blk[:half_rows], v_blk[:half_rows], None)

    def from_later(state_old):
        tail_old = tuple(arr_part[half_rows:] for arr_part in state_old)
        tail_new = attend_update(tail_old, q_cur[half_rows:], k_blk, v_blk, None)
        return tuple(jnp.concatenate([old_part[:half_rows], new_part]) for old_part, new_part in zip(state_old, tail_new))

    return from_earlier, from_later


def backward_branches(q_cur, do_cur, log_norm, row_dots, half_rows, k_blk, v_blk):
    def from_earlier(grads_old):
        dq_old, dk_old, dv_old = grads_old
        dq_part, dk_part, dv_part = grad_update(q_cur, do_cur, log_norm, row_dots, k_blk[:half_rows], v_blk[:half_rows], None)
        return (dq_old + dq_part,
                jnp.concatenate([dk_old[:half_rows] + dk_part, dk_old[half_rows:]]),
                jnp.concatenate([dv_old[:half_rows] + dv_part, dv_old[half_rows:]]))

    def from_later(grads_old):
        dq_old, dk_old, dv_old = grads_old
        dq_part, dk_part, dv_part = grad_update(q_cur[half_rows:], do_cur[half_rows:], log_norm[half_rows:], row_dots[half_rows:], k_blk, v_blk, None)
        return (jnp.concatenate([dq_old[:half_rows], dq_old[half_rows:] + dq_part]), dk_old + dk_part, dv_old + dv_part)

    return from_earlier, from_later


def solution(mesh):
    seq_shards = mesh.shape["cp"]
    send_perm = [(src_idx, (src_idx + 1) % seq_shards) for src_idx in range(seq_shards)]

    def device_fn(x_blk, w_query, w_key, w_value, w_out, dy_blk):
        my_rank = lax.axis_index("cp")
        model_dim, q_heads, head_dim = w_query.shape
        kv_heads = w_key.shape[1]
        groups = q_heads // kv_heads
        wq_flat = w_query.reshape(model_dim, q_heads * head_dim)
        wk_flat = w_key.reshape(model_dim, kv_heads * head_dim)
        wv_flat = w_value.reshape(model_dim, kv_heads * head_dim)
        wo_flat = w_out.reshape(q_heads * head_dim, model_dim)

        x_rows = lax.all_gather(x_blk, "tp", axis=0, tiled=True)
        n_rows = x_rows.shape[0]
        half_rows = n_rows // 2
        q_cur = jnp.dot(x_rows, wq_flat, preferred_element_type=jnp.float32).astype(jnp.bfloat16).reshape(n_rows, kv_heads, groups, head_dim)
        k_own = jnp.dot(x_rows, wk_flat, preferred_element_type=jnp.float32).astype(jnp.bfloat16).reshape(n_rows, kv_heads, head_dim)
        v_own = jnp.dot(x_rows, wv_flat, preferred_element_type=jnp.float32).astype(jnp.bfloat16).reshape(n_rows, kv_heads, head_dim)
        offsets = jnp.arange(half_rows, dtype=jnp.int32)
        positions = jnp.concatenate([my_rank * half_rows + offsets, (2 * seq_shards - 1 - my_rank) * half_rows + offsets])
        own_pair = (positions, positions)

        stat_shape = (n_rows, kv_heads, groups)
        softmax_state = (jnp.full(stat_shape, -jnp.inf, jnp.float32), jnp.zeros(stat_shape, jnp.float32), jnp.zeros(q_cur.shape, jnp.float32))
        softmax_state = attend_update(softmax_state, q_cur, k_own, v_own, own_pair)

        def forward_step(step_idx, loop_carry):
            k_blk, v_blk, state_in = loop_carry
            k_blk = lax.ppermute(k_blk, "cp", send_perm)
            v_blk = lax.ppermute(v_blk, "cp", send_perm)
            source = (my_rank - step_idx) % seq_shards
            from_earlier, from_later = forward_branches(q_cur, half_rows, k_blk, v_blk)
            return k_blk, v_blk, lax.cond(source < my_rank, from_earlier, from_later, state_in)

        softmax_state = lax.fori_loop(1, seq_shards, forward_step, (k_own, v_own, softmax_state))[2]
        row_max, row_sum, out_acc = softmax_state
        log_norm = row_max + jnp.log(row_sum)
        o_cur = (out_acc / row_sum[..., None]).astype(jnp.bfloat16)
        o_flat = o_cur.reshape(n_rows, q_heads * head_dim)
        y_part = jnp.dot(o_flat, wo_flat, preferred_element_type=jnp.float32)
        y_blk = lax.psum_scatter(y_part, "tp", scatter_dimension=0, tiled=True).astype(jnp.bfloat16)

        dy_rows = lax.all_gather(dy_blk, "tp", axis=0, tiled=True)
        do_cur = lax.dot_general(dy_rows, wo_flat, COLS_CONTRACT, preferred_element_type=jnp.float32).astype(jnp.bfloat16).reshape(q_cur.shape)
        row_dots = jnp.sum(do_cur.astype(jnp.float32) * o_cur.astype(jnp.float32), axis=-1)
        dq_acc, dk_own, dv_own = grad_update(q_cur, do_cur, log_norm, row_dots, k_own, v_own, own_pair)

        def backward_step(step_idx, loop_carry):
            k_blk, v_blk, dk_blk, dv_blk, dq_in = loop_carry
            k_blk = lax.ppermute(k_blk, "cp", send_perm)
            v_blk = lax.ppermute(v_blk, "cp", send_perm)
            dk_blk = lax.ppermute(dk_blk, "cp", send_perm)
            dv_blk = lax.ppermute(dv_blk, "cp", send_perm)
            source = (my_rank - step_idx) % seq_shards
            from_earlier, from_later = backward_branches(q_cur, do_cur, log_norm, row_dots, half_rows, k_blk, v_blk)
            dq_out, dk_out, dv_out = lax.cond(source < my_rank, from_earlier, from_later, (dq_in, dk_blk, dv_blk))
            return k_blk, v_blk, dk_out, dv_out, dq_out

        loop_out = lax.fori_loop(1, seq_shards, backward_step, (k_own, v_own, dk_own, dv_own, dq_acc))
        dk_home = lax.ppermute(loop_out[2], "cp", send_perm)
        dv_home = lax.ppermute(loop_out[3], "cp", send_perm)
        dq_flat = loop_out[4].astype(jnp.bfloat16).reshape(n_rows, q_heads * head_dim)
        dk_flat = dk_home.astype(jnp.bfloat16).reshape(n_rows, kv_heads * head_dim)
        dv_flat = dv_home.astype(jnp.bfloat16).reshape(n_rows, kv_heads * head_dim)
        dx_part = (lax.dot_general(dq_flat, wq_flat, COLS_CONTRACT, preferred_element_type=jnp.float32)
                   + lax.dot_general(dk_flat, wk_flat, COLS_CONTRACT, preferred_element_type=jnp.float32)
                   + lax.dot_general(dv_flat, wv_flat, COLS_CONTRACT, preferred_element_type=jnp.float32))
        dx_blk = lax.psum_scatter(dx_part, "tp", scatter_dimension=0, tiled=True).astype(jnp.bfloat16)
        grad_wq = lax.dot_general(x_rows, dq_flat, ROWS_CONTRACT, preferred_element_type=jnp.float32).astype(jnp.bfloat16).reshape(model_dim, q_heads, head_dim)
        grad_wk = lax.dot_general(x_rows, dk_flat, ROWS_CONTRACT, preferred_element_type=jnp.float32).astype(jnp.bfloat16).reshape(model_dim, kv_heads, head_dim)
        grad_wv = lax.dot_general(x_rows, dv_flat, ROWS_CONTRACT, preferred_element_type=jnp.float32).astype(jnp.bfloat16).reshape(model_dim, kv_heads, head_dim)
        grad_wo = lax.dot_general(o_flat, dy_rows, ROWS_CONTRACT, preferred_element_type=jnp.float32).astype(jnp.bfloat16).reshape(q_heads, head_dim, model_dim)
        return y_blk, dx_blk, grad_wq[None], grad_wk[None], grad_wv[None], grad_wo[None]

    return jax.shard_map(device_fn, mesh=mesh,
                         in_specs=(ROW_SPEC, HEAD_SPEC, HEAD_SPEC, HEAD_SPEC, OUT_W_SPEC, ROW_SPEC),
                         out_specs=(ROW_SPEC, ROW_SPEC, GRAD_SPEC, GRAD_SPEC, GRAD_SPEC, GRAD_OUT_SPEC),
                         check_vma=False)
```

profile of v0, /device:TPU:0, one launch (start us, length us, event | category | flops | bytes accessed | tf_op | source)
XLA Modules:
  0.0 920.8 jit_solution(14988171878244500248)
XLA Ops:
  9.4 57.1 %all-gather.3.cloned.1.call-done = bf16[1024,2048]{1,0:T(8,128)(2,1)} async-done(((bf16[512,2048]{1,0:T(8,128)(2,1)}), bf16[1024,2048]{1,0:T(8,128)(2,1)}) %all-gather.3.cloned.1.call-update) | async-done | bytes 4194320 | tf_op jit(solution)/shard_map/all_gather | solution.py:90
  78.9 25.2 %fusion.78 = (f32[1024,4,4]{0,2,1:T(4,128)S(1)}, f32[4,1024,1024,4]{2,1,3,0:T(8,128)}) fusion(pred[1024,1024]{0,1:T(8,128)(4,1)S(1)} %broadcast_compare_fusion, bf16[1024,4,64,1]{0,2,3,1:T(8,128)(2,1)} %bitcast.43, bf16[1024,4,4,64]{0,3,2,1:T(8,128)(2,1)} %bitcast.45), kind=kOutput, calls=%fused_computation.91 | convolution fusion | flops 2197798912 | bytes 70844416 | tf_op jit(solution)/shard_map/qhgd,khd->qhgk/dot_general | solution.py:23
  104.1 21.6 %fusion.80 = f32[1024,4,4]{0,2,1:T(4,128)S(1)} fusion(f32[4,1024,1024,4]{2,1,3,0:T(8,128)} %get-tuple-element.663, f32[1024,4,4]{0,2,1:T(4,128)S(1)} %get-tuple-element.812, pred[1024,1024]{0,1:T(8,128)(4,1)S(1)} %broadcast_compare_fusion), kind=kLoop, calls=%fused_computation.93 | loop fusion | flops 67092480 | bytes 68288512 | tf_op jit(solution)/shard_map/reduce_sum | solution.py:29
  134.0 26.1 %bitcast_add_fusion.6 = f32[1024,4,4,64]{0,3,2,1:T(8,128)} fusion(bf16[1024,4,64,1]{0,2,3,1:T(8,128)(2,1)} %bitcast.48, f32[4,1024,1024,4]{2,1,3,0:T(8,128)} %get-tuple-element.663, f32[1024,4,4]{0,2,1:T(4,128)S(1)} %get-tuple-element.812, pred[1024,1024]{0,1:T(8,128)(4,1)S(1)} %broadcast_compare_fusion, f32[1024,4,4]{0,2,1:T(4,128)S(1)} %get-tuple-element.660), kind=kOutput, calls=%fused_computation.101 | convolution fusion | flops 2215641088 | bytes 73007104 | tf_op jit(solution)/shard_map/qhgk,khd->qhgd/dot_general | solution.py:30
  160.1 189.4 %while.46 = (s32[]{:T(128)}, bf16[1024,4,64]{0,2,1:T(8,128)(2,1)}, bf16[1024,4,64]{0,2,1:T(8,128)(2,1)}, f32[1024,4,4]{0,2,1:T(4,128)S(1)}, f32[1024,4,4]{0,2,1:...) while((s32[]{:T(128)}, bf16[1024,4,64]{0,2,1:T(8,128)(2,1)}, ...), condition=%wide.region_9.10_spmd, body=%wide.region_2.9_spmd.sunk | while | flops 2216738816 | bytes 143589872 | solution.py:112
  174.8 45.2 %conditional.4 = (f32[1024,4,4]{0,2,1:T(4,128)}, f32[1024,4,4]{0,2,1:T(4,128)S(1)}, f32[1024,4,4,64]{0,3,2,1:T(8,128)}) conditional(s32[]{:T(128)} %convert_element_type.171, (f32[1024,4,4]{0,2,1:T(4,128)S(1)}, bf16[1024,4,4,64]{0,3,2,1:T(8,128)(2,1)}, bf16[1024,4,64]{0,2,1:T(8,128)(2,1)S(1)}, f32[1024,4,4]{0,2,1:T(4,128)S(1)}, ...), branch_computations={%region_3.5_spmd, %region_6.8_spmd} | conditional | flops 2216738816 | bytes 137166912 | solution.py:110
  237.8 45.2 %conditional.4 = (f32[1024,4,4]{0,2,1:T(4,128)}, f32[1024,4,4]{0,2,1:T(4,128)S(1)}, f32[1024,4,4,64]{0,3,2,1:T(8,128)}) conditional(s32[]{:T(128)} %convert_element_type.171, (f32[1024,4,4]{0,2,1:T(4,128)S(1)}, bf16[1024,4,4,64]{0,3,2,1:T(8,128)(2,1)}, bf16[1024,4,64]{0,2,1:T(8,128)(2,1)S(1)}, f32[1024,4,4]{0,2,1:T(4,128)S(1)}, ...), branch_computations={%region_3.5_spmd, %region_6.8_spmd} | conditional | flops 2216738816 | bytes 137166912 | solution.py:110
  300.7 45.2 %conditional.4 = (f32[1024,4,4]{0,2,1:T(4,128)}, f32[1024,4,4]{0,2,1:T(4,128)S(1)}, f32[1024,4,4,64]{0,3,2,1:T(8,128)}) conditional(s32[]{:T(128)} %convert_element_type.171, (f32[1024,4,4]{0,2,1:T(4,128)S(1)}, bf16[1024,4,4,64]{0,3,2,1:T(8,128)(2,1)}, bf16[1024,4,64]{0,2,1:T(8,128)(2,1)S(1)}, f32[1024,4,4]{0,2,1:T(4,128)S(1)}, ...), branch_computations={%region_3.5_spmd, %region_6.8_spmd} | conditional | flops 2216738816 | bytes 137166912 | solution.py:110
  370.4 38.9 %fusion.75 = bf16[1024,4,4,1024]{0,3,2,1:T(8,128)(2,1)} fusion(f32[4,1024,1024,4]{2,1,3,0:T(8,128)} %get-tuple-element.663, bf16[1024,4,64,1]{0,2,3,1:T(8,128)(2,1)} %bitcast.48, bf16[1024,4,4,64]{0,3,2,1:T(8,128)(2,1)} %bitcast.54, f32[1024,4,4]{0,2,1:T(4,128)} %get-tuple-element.855, f32[1024,4,4]{0,2,1:T(4,128)} %bitcast.295, ...), kind=kOutput, calls=%fused_computation.85 | convolution fusion | flops 2248146944 | bytes 104464384 | tf_op jit(solution)/shard_map/qhgd,khd->qhgk/dot_general | solution.py:40
  409.3 18.7 %multiply_bitcast_fusion = f32[1024,4,4,64]{0,3,2,1:T(8,128)} fusion(bf16[1024,4,64,1]{0,2,3,1:T(8,128)(2,1)} %bitcast.43, bf16[1024,4,4,1024]{0,3,2,1:T(8,128)(2,1)} %fusion.75), kind=kOutput, calls=%fused_computation.102 | convolution fusion | flops 2148532224 | bytes 38273024 | tf_op jit(solution)/shard_map/qhgk,khd->qhgd/dot_general | solution.py:44
  428.0 17.5 %fusion.91 = f32[1024,4,64]{0,2,1:T(8,128)} fusion(bf16[1024,4,4,64]{0,3,2,1:T(8,128)(2,1)} %bitcast.45, bf16[1024,4,4,1024]{0,3,2,1:T(8,128)(2,1)} %fusion.75), kind=kOutput, calls=%fused_computation.114 | convolution fusion | flops 2147745792 | bytes 36700160 | tf_op jit(solution)/shard_map/qhgk,qhgd->khd/dot_general | solution.py:43
  445.5 25.1 %fusion.92 = f32[1024,4,64]{0,2,1:T(8,128)} fusion(bf16[1024,4,4,64]{0,3,2,1:T(8,128)(2,1)} %bitcast.54, f32[4,1024,1024,4]{2,1,3,0:T(8,128)} %get-tuple-element.663, f32[1024,4,4]{0,2,1:T(4,128)} %bitcast.295, pred[1024,1024]{0,1:T(8,128)(4,1)S(1)} %copy-done.14), kind=kOutput, calls=%fused_computation.115 | convolution fusion | flops 2214592512 | bytes 71368704 | tf_op jit(solution)/shard_map/qhgk,qhgd->khd/dot_general | solution.py:42
  470.7 314.1 %while.47 = (s32[]{:T(128)}, bf16[1024,4,64]{0,2,1:T(8,128)(2,1)}, bf16[1024,4,64]{0,2,1:T(8,128)(2,1)}, f32[1024,4,64]{0,2,1:T(8,128)}, f32[1024,4,64]{0,2,1:T(...) while((s32[]{:T(128)}, bf16[1024,4,64]{0,2,1:T(8,128)(2,1)}, ...), condition=%wide.region_15.16_spmd, body=%wide.region_12.15_spmd.sunk | while | flops 5438832640 | bytes 220037936 | solution.py:136
  492.3 25.9 %collective-permute-done.2 = bf16[1024,4,64]{0,2,1:T(8,128)(2,1)S(1)} collective-permute-done((bf16[1024,4,64]{0,2,1:T(8,128)(2,1)}, bf16[1024,4,64]{0,2,1:T(8,128)(2,1)S(1)}, u32[]{:S(2)}, u32[]{:S(2)}) %collective-permute-start.2) | collective-permute-done | bytes 524320 | tf_op jit(solution)/shard_map/while/body/eval_jaxpr/ppermute | solution.py:127
  524.6 61.6 %conditional.5 = (f32[1024,4,4,64]{0,3,2,1:T(8,128)}, f32[1024,4,64]{0,2,1:T(8,128)}, f32[1024,4,64]{0,2,1:T(8,128)}) conditional(s32[]{:T(128)} %convert_element_type.172, (f32[1024,4,4,64]{0,3,2,1:T(8,128)}, bf16[1024,4,4,64]{0,3,2,1:T(8,128)(2,1)}, bf16[1024,4,64]{0,2,1:T(8,128)(2,1)S(1)}, f32[1024,4,4]{0,2,1:T(4,128)}, ...), branch_computations={%region_13.13_spmd, %region_14.14_spmd} | conditional | flops 5438832640 | bytes 205357280 | solution.py:133
  524.6 15.2 %fusion.45 = f32[4,1024,512,4]{2,1,3,0:T(8,128)} fusion(bf16[1024,4,4,64]{0,3,2,1:T(8,128)(2,1)} %get-tuple-element.557, bf16[1024,4,64]{0,2,1:T(8,128)(2,1)S(1)} %get-tuple-element.556), kind=kOutput, calls=%fused_computation.53 | convolution fusion | flops 1073741824 | bytes 35127296 | tf_op jit(solution)/shard_map/while/body/eval_jaxpr/cond/branch_0_fun/qhgd,khd->qhgk/dot_general | solution.py:36
  571.2 15.0 %fusion.39 = f32[1024,4,64]{0,2,1:T(8,128)} fusion(f32[1024,4,64]{0,2,1:T(8,128)} %get-tuple-element.563, f32[4,1024,512,4]{2,1,3,0:T(8,128)} %fusion.45, f32[512,4,4]{0,2,1:T(4,128)} %copy-done.12, bf16[1024,4,4,64]{0,3,2,1:T(8,128)(2,1)} %get-tuple-element.560), kind=kOutput, calls=%fused_computation.49 | convolution fusion | flops 1099169792 | bytes 36732928 | tf_op jit(solution)/shard_map/while/body/eval_jaxpr/cond/branch_0_fun/qhgk,qhgd->khd/dot_general | solution.py:42
  592.2 25.1 %collective-permute-done.2 = bf16[1024,4,64]{0,2,1:T(8,128)(2,1)S(1)} collective-permute-done((bf16[1024,4,64]{0,2,1:T(8,128)(2,1)}, bf16[1024,4,64]{0,2,1:T(8,128)(2,1)S(1)}, u32[]{:S(2)}, u32[]{:S(2)}) %collective-permute-start.2) | collective-permute-done | bytes 524320 | tf_op jit(solution)/shard_map/while/body/eval_jaxpr/ppermute | solution.py:127
  623.7 61.6 %conditional.5 = (f32[1024,4,4,64]{0,3,2,1:T(8,128)}, f32[1024,4,64]{0,2,1:T(8,128)}, f32[1024,4,64]{0,2,1:T(8,128)}) conditional(s32[]{:T(128)} %convert_element_type.172, (f32[1024,4,4,64]{0,3,2,1:T(8,128)}, bf16[1024,4,4,64]{0,3,2,1:T(8,128)(2,1)}, bf16[1024,4,64]{0,2,1:T(8,128)(2,1)S(1)}, f32[1024,4,4]{0,2,1:T(4,128)}, ...), branch_computations={%region_13.13_spmd, %region_14.14_spmd} | conditional | flops 5438832640 | bytes 205357280 | solution.py:133
  623.7 15.2 %fusion.45 = f32[4,1024,512,4]{2,1,3,0:T(8,128)} fusion(bf16[1024,4,4,64]{0,3,2,1:T(8,128)(2,1)} %get-tuple-element.557, bf16[1024,4,64]{0,2,1:T(8,128)(2,1)S(1)} %get-tuple-element.556), kind=kOutput, calls=%fused_computation.53 | convolution fusion | flops 1073741824 | bytes 35127296 | tf_op jit(solution)/shard_map/while/body/eval_jaxpr/cond/branch_0_fun/qhgd,khd->qhgk/dot_general | solution.py:36
  692.1 24.2 %collective-permute-done.2 = bf16[1024,4,64]{0,2,1:T(8,128)(2,1)S(1)} collective-permute-done((bf16[1024,4,64]{0,2,1:T(8,128)(2,1)}, bf16[1024,4,64]{0,2,1:T(8,128)(2,1)S(1)}, u32[]{:S(2)}, u32[]{:S(2)}) %collective-permute-start.2) | collective-permute-done | bytes 524320 | tf_op jit(solution)/shard_map/while/body/eval_jaxpr/ppermute | solution.py:127
  722.8 61.6 %conditional.5 = (f32[1024,4,4,64]{0,3,2,1:T(8,128)}, f32[1024,4,64]{0,2,1:T(8,128)}, f32[1024,4,64]{0,2,1:T(8,128)}) conditional(s32[]{:T(128)} %convert_element_type.172, (f32[1024,4,4,64]{0,3,2,1:T(8,128)}, bf16[1024,4,4,64]{0,3,2,1:T(8,128)(2,1)}, bf16[1024,4,64]{0,2,1:T(8,128)(2,1)S(1)}, f32[1024,4,4]{0,2,1:T(4,128)}, ...), branch_computations={%region_13.13_spmd, %region_14.14_spmd} | conditional | flops 5438832640 | bytes 205357280 | solution.py:133
  722.8 15.2 %fusion.45 = f32[4,1024,512,4]{2,1,3,0:T(8,128)} fusion(bf16[1024,4,4,64]{0,3,2,1:T(8,128)(2,1)} %get-tuple-element.557, bf16[1024,4,64]{0,2,1:T(8,128)(2,1)S(1)} %get-tuple-element.556), kind=kOutput, calls=%fused_computation.53 | convolution fusion | flops 1073741824 | bytes 35127296 | tf_op jit(solution)/shard_map/while/body/eval_jaxpr/cond/branch_0_fun/qhgd,khd->qhgk/dot_general | solution.py:36
  831.4 78.8 %reduce-scatter.5.cloned.1.call-done = f32[512,2048]{1,0:T(8,128)} async-done(((f32[1024,2048]{1,0:T(8,128)}), f32[512,2048]{1,0:T(8,128)}) %reduce-scatter.5.cloned.1.call-update) | async-done | bytes 4194320 | tf_op jit(solution)/shard_map/reduce_scatter | solution.py:145
  (205 shorter events, 444.2 us)
Async XLA Ops:
  7.2 59.4 %all-gather.3.cloned.1.call-start = ((), (), s32[]{:S(2)}) async-start(), calls=%async_computation.2 | async-start | bytes 6291456 | tf_op jit(solution)/shard_map/all_gather | solution.py:90
  7.9 341.6 %all-gather.5.cloned.1.call-start = ((), (), s32[]{:S(2)}) async-start(), calls=%async_computation.4 | async-start | bytes 6291456 | tf_op jit(solution)/shard_map/all_gather | solution.py:120
  8.7 818.9 %reduce-scatter.3.cloned.1.call-start = ((), (), s32[]{:S(2)}) async-start(), calls=%async_computation.3 | async-start | bytes 12582912 | tf_op jit(solution)/shard_map/reduce_scatter | solution.py:118
  160.5 8.6 collective-permute-start
  160.6 14.2 %collective-permute-start.1 = (bf16[1024,4,64]{0,2,1:T(8,128)(2,1)}, bf16[1024,4,64]{0,2,1:T(8,128)(2,1)}, u32[]{:S(2)}, u32[]{:S(2)}) collective-permute-start(bf16[1024,4,64]{0,2,1:T(8,128)(2,1)} %get-tuple-element.823), channel_id=1, source_target_pairs={{0,1},{1,2},{2,3},{3,0},{4,5},{5,6},{6,7},{7,4}} | collective-permute-start | bytes 1572872 | tf_op jit(solution)/shard_map/while/body/eval_jaxpr/ppermute | solution.py:107
  223.5 8.6 collective-permute-start
  224.4 13.4 %collective-permute-start.1 = (bf16[1024,4,64]{0,2,1:T(8,128)(2,1)}, bf16[1024,4,64]{0,2,1:T(8,128)(2,1)}, u32[]{:S(2)}, u32[]{:S(2)}) collective-permute-start(bf16[1024,4,64]{0,2,1:T(8,128)(2,1)} %get-tuple-element.823), channel_id=1, source_target_pairs={{0,1},{1,2},{2,3},{3,0},{4,5},{5,6},{6,7},{7,4}} | collective-permute-start | bytes 1572872 | tf_op jit(solution)/shard_map/while/body/eval_jaxpr/ppermute | solution.py:107
  286.5 8.6 collective-permute-start
  287.4 13.4 %collective-permute-start.1 = (bf16[1024,4,64]{0,2,1:T(8,128)(2,1)}, bf16[1024,4,64]{0,2,1:T(8,128)(2,1)}, u32[]{:S(2)}, u32[]{:S(2)}) collective-permute-start(bf16[1024,4,64]{0,2,1:T(8,128)(2,1)} %get-tuple-element.823), channel_id=1, source_target_pairs={{0,1},{1,2},{2,3},{3,0},{4,5},{5,6},{6,7},{7,4}} | collective-permute-start | bytes 1572872 | tf_op jit(solution)/shard_map/while/body/eval_jaxpr/ppermute | solution.py:107
  369.2 541.0 %reduce-scatter.5.cloned.1.call-start = ((), (), s32[]{:S(2)}) async-start(), calls=%async_computation.5 | async-start | bytes 12582912 | tf_op jit(solution)/shard_map/reduce_scatter | solution.py:145
  487.1 37.5 %collective-permute-start.4 = (f32[1024,4,64]{0,2,1:T(8,128)}, f32[1024,4,64]{0,2,1:T(8,128)S(1)}, u32[]{:S(2)}, u32[]{:S(2)}) collective-permute-start(f32[1024,4,64]{0,2,1:T(8,128)} %get-tuple-element.863), channel_id=1, source_target_pairs={{0,1},{1,2},{2,3},{3,0},{4,5},{5,6},{6,7},{7,4}} | collective-permute-start | bytes 3145736 | tf_op jit(solution)/shard_map/while/body/eval_jaxpr/ppermute | solution.py:129
  489.8 34.8 %collective-permute-start.5 = (f32[1024,4,64]{0,2,1:T(8,128)}, f32[1024,4,64]{0,2,1:T(8,128)}, u32[]{:S(2)}, u32[]{:S(2)}) collective-permute-start(f32[1024,4,64]{0,2,1:T(8,128)} %get-tuple-element.864), channel_id=1, source_target_pairs={{0,1},{1,2},{2,3},{3,0},{4,5},{5,6},{6,7},{7,4}} | collective-permute-start | bytes 3145736 | tf_op jit(solution)/shard_map/while/body/eval_jaxpr/ppermute | solution.py:130
  492.2 25.9 %collective-permute-start.2 = (bf16[1024,4,64]{0,2,1:T(8,128)(2,1)}, bf16[1024,4,64]{0,2,1:T(8,128)(2,1)S(1)}, u32[]{:S(2)}, u32[]{:S(2)}) collective-permute-start(bf16[1024,4,64]{0,2,1:T(8,128)(2,1)} %get-tuple-element.861), channel_id=1, source_target_pairs={{0,1},{1,2},{2,3},{3,0},{4,5},{5,6},{6,7},{7,4}} | collective-permute-start | bytes 1572872 | tf_op jit(solution)/shard_map/while/body/eval_jaxpr/ppermute | solution.py:127
  492.3 31.5 %collective-permute-start.3 = (bf16[1024,4,64]{0,2,1:T(8,128)(2,1)}, bf16[1024,4,64]{0,2,1:T(8,128)(2,1)S(1)}, u32[]{:S(2)}, u32[]{:S(2)}) collective-permute-start(bf16[1024,4,64]{0,2,1:T(8,128)(2,1)} %get-tuple-element.862), channel_id=1, source_target_pairs={{0,1},{1,2},{2,3},{3,0},{4,5},{5,6},{6,7},{7,4}} | collective-permute-start | bytes 1572872 | tf_op jit(solution)/shard_map/while/body/eval_jaxpr/ppermute | solution.py:128
  586.2 37.5 %collective-permute-start.4 = (f32[1024,4,64]{0,2,1:T(8,128)}, f32[1024,4,64]{0,2,1:T(8,128)S(1)}, u32[]{:S(2)}, u32[]{:S(2)}) collective-permute-start(f32[1024,4,64]{0,2,1:T(8,128)} %get-tuple-element.863), channel_id=1, source_target_pairs={{0,1},{1,2},{2,3},{3,0},{4,5},{5,6},{6,7},{7,4}} | collective-permute-start | bytes 3145736 | tf_op jit(solution)/shard_map/while/body/eval_jaxpr/ppermute | solution.py:129
  589.7 34.0 %collective-permute-start.5 = (f32[1024,4,64]{0,2,1:T(8,128)}, f32[1024,4,64]{0,2,1:T(8,128)}, u32[]{:S(2)}, u32[]{:S(2)}) collective-permute-start(f32[1024,4,64]{0,2,1:T(8,128)} %get-tuple-element.864), channel_id=1, source_target_pairs={{0,1},{1,2},{2,3},{3,0},{4,5},{5,6},{6,7},{7,4}} | collective-permute-start | bytes 3145736 | tf_op jit(solution)/shard_map/while/body/eval_jaxpr/ppermute | solution.py:130
  592.2 25.1 %collective-permute-start.2 = (bf16[1024,4,64]{0,2,1:T(8,128)(2,1)}, bf16[1024,4,64]{0,2,1:T(8,128)(2,1)S(1)}, u32[]{:S(2)}, u32[]{:S(2)}) collective-permute-start(bf16[1024,4,64]{0,2,1:T(8,128)(2,1)} %get-tuple-element.861), channel_id=1, source_target_pairs={{0,1},{1,2},{2,3},{3,0},{4,5},{5,6},{6,7},{7,4}} | collective-permute-start | bytes 1572872 | tf_op jit(solution)/shard_map/while/body/eval_jaxpr/ppermute | solution.py:127
  592.2 30.7 %collective-permute-start.3 = (bf16[1024,4,64]{0,2,1:T(8,128)(2,1)}, bf16[1024,4,64]{0,2,1:T(8,128)(2,1)S(1)}, u32[]{:S(2)}, u32[]{:S(2)}) collective-permute-start(bf16[1024,4,64]{0,2,1:T(8,128)(2,1)} %get-tuple-element.862), channel_id=1, source_target_pairs={{0,1},{1,2},{2,3},{3,0},{4,5},{5,6},{6,7},{7,4}} | collective-permute-start | bytes 1572872 | tf_op jit(solution)/shard_map/while/body/eval_jaxpr/ppermute | solution.py:128
  685.3 37.5 %collective-permute-start.4 = (f32[1024,4,64]{0,2,1:T(8,128)}, f32[1024,4,64]{0,2,1:T(8,128)S(1)}, u32[]{:S(2)}, u32[]{:S(2)}) collective-permute-start(f32[1024,4,64]{0,2,1:T(8,128)} %get-tuple-element.863), channel_id=1, source_target_pairs={{0,1},{1,2},{2,3},{3,0},{4,5},{5,6},{6,7},{7,4}} | collective-permute-start | bytes 3145736 | tf_op jit(solution)/shard_map/while/body/eval_jaxpr/ppermute | solution.py:129
  688.7 34.0 %collective-permute-start.5 = (f32[1024,4,64]{0,2,1:T(8,128)}, f32[1024,4,64]{0,2,1:T(8,128)}, u32[]{:S(2)}, u32[]{:S(2)}) collective-permute-start(f32[1024,4,64]{0,2,1:T(8,128)} %get-tuple-element.864), channel_id=1, source_target_pairs={{0,1},{1,2},{2,3},{3,0},{4,5},{5,6},{6,7},{7,4}} | collective-permute-start | bytes 3145736 | tf_op jit(solution)/shard_map/while/body/eval_jaxpr/ppermute | solution.py:130
  692.1 24.3 %collective-permute-start.2 = (bf16[1024,4,64]{0,2,1:T(8,128)(2,1)}, bf16[1024,4,64]{0,2,1:T(8,128)(2,1)S(1)}, u32[]{:S(2)}, u32[]{:S(2)}) collective-permute-start(bf16[1024,4,64]{0,2,1:T(8,128)(2,1)} %get-tuple-element.861), channel_id=1, source_target_pairs={{0,1},{1,2},{2,3},{3,0},{4,5},{5,6},{6,7},{7,4}} | collective-permute-start | bytes 1572872 | tf_op jit(solution)/shard_map/while/body/eval_jaxpr/ppermute | solution.py:127
  692.1 29.9 %collective-permute-start.3 = (bf16[1024,4,64]{0,2,1:T(8,128)(2,1)}, bf16[1024,4,64]{0,2,1:T(8,128)(2,1)S(1)}, u32[]{:S(2)}, u32[]{:S(2)}) collective-permute-start(bf16[1024,4,64]{0,2,1:T(8,128)(2,1)} %get-tuple-element.862), channel_id=1, source_target_pairs={{0,1},{1,2},{2,3},{3,0},{4,5},{5,6},{6,7},{7,4}} | collective-permute-start | bytes 1572872 | tf_op jit(solution)/shard_map/while/body/eval_jaxpr/ppermute | solution.py:128
  788.7 12.8 %collective-permute-start.6 = (bf16[1024,4,64]{0,2,1:T(8,128)(2,1)S(1)}, bf16[1024,4,64]{0,2,1:T(8,128)(2,1)S(1)}, u32[]{:S(2)}, u32[]{:S(2)}) collective-permute-start(bf16[1024,4,64]{0,2,1:T(8,128)(2,1)S(1)} %convert.8), channel_id=1, source_target_pairs={{0,1},{1,2},{2,3},{3,0},{4,5},{5,6},{6,7},{7,4}} | collective-permute-start | bytes 1572872 | tf_op jit(solution)/shard_map/ppermute | solution.py:137
  794.3 8.6 collective-permute-start.7
  (36 other events, 534.7 us)
Sparse Core Ops, SparseCore 0:
  9.5 57.0 all-gather.2
  68.1 54.2 all-gather.4
  369.3 99.9 reduce-scatter.2
  808.5 101.6 reduce-scatter.4
where the time goes:
time: 932 us; the launch traced here: 921 us
  matrix products  473 us (51%)
  waiting for transfers between devices  260 us (28%)
  other arithmetic  93.5 us (10%)
  starting transfers between devices  35.1 us (4%)
  local copies, waits for them, and re-layouts  27.5 us (3%)
  loops' own time  17.7 us (2%)
  between operations  14.2 us (2%)
    dot_general x4, matrix products, grad_update(): jnp.einsum('qhgd,khd->qhgk', do_rows, v_blk, preferred_element_type=jnp.f...  83 us
    reduce_scatter x1, waiting for transfers between devices, device_fn(): lax.psum_scatter(dx_part, 'tp', scatter_dimension=0, tiled=True)  78.8 us
    ppermute x3, waiting for transfers between devices, backward_step(): k_blk = lax.ppermute(k_blk, 'cp', send_perm)  75.2 us
    dot_general x4, matrix products, grad_update(): jnp.einsum('qhgk,qhgd->khd', prob_mat.astype(jnp.bfloat16), do_rows, pref...  70.1 us
    dot_general x4, matrix products, attend_update(): jnp.einsum('qhgd,khd->qhgk', q_rows, k_blk, preferred_element_type=jnp.fl...  68.6 us
    dot_general x4, matrix products, attend_update(): jnp.einsum('qhgk,khd->qhgd', prob_mat.astype(jnp.bfloat16), v_blk, prefer...  67.1 us
    reduce_sum x4, other arithmetic, attend_update(): new_sum = row_sum * factor + jnp.sum(prob_mat, axis=-1)  62.7 us
    all_gather x1, waiting for transfers between devices, device_fn(): x_rows = lax.all_gather(x_blk, 'tp', axis=0, tiled=True)  57.1 us
  transfers between devices with their start and end apart: 24, of which 15 were waited for; matrix products, arithmetic and copies ran while one was open for 62% of the time, Pallas kernels for 0%

commit v1 on v0

v1 whole, which is shorter than its diff:
```python
import jax
import jax.numpy as jnp
from jax import lax
from jax.experimental import pallas as pl
from jax.experimental.pallas import tpu as pltpu
from jax.sharding import PartitionSpec as P

ROW_SPEC = P(("dp", "cp", "tp"), None)
HEAD_SPEC = P(None, "tp", None)
OUT_W_SPEC = P("tp", None, None)
GRAD_SPEC = P(("dp", "cp"), None, "tp", None)
GRAD_OUT_SPEC = P(("dp", "cp"), "tp", None, None)
NT = (((1,), (1,)), ((), ()))
TN = (((0,), (0,)), ((), ()))
F32 = jnp.float32
BF16 = jnp.bfloat16
VMEM_LIMIT = 60 * 1024 * 1024


def stored_block(pos_blk, n_blk):
    half = n_blk // 2
    return jnp.where(pos_blk < half, 2 * pos_blk, 2 * n_blk - 1 - 2 * pos_blk)


def fwd_kernel(n_blk, blk, groups, dim, q_ref, kv_ref, o_ref, lse_ref, kvt_s, rq_s, acc_s, m_s, l_s):
    step = pl.program_id(0)

    @pl.when(step == 0)
    def _():
        for b in range(n_blk):
            kvt_s[:, b * blk:(b + 1) * blk] = kv_ref[b * blk:(b + 1) * blk, :].T
        rq_s[...] = jnp.zeros_like(rq_s)

    q_t = q_ref[...].T
    for h in range(groups):
        rq_s[h, :dim, :] = q_t[h * dim:(h + 1) * dim, :]

    def tile(j, diag):
        off = pl.multiple_of(stored_block(j, n_blk) * blk, blk)
        kv_j = kv_ref[pl.ds(off, blk), :]
        v_t = kvt_s[dim:, pl.ds(off, blk)]
        for h in range(groups):
            s = jnp.dot(kv_j, rq_s[h], preferred_element_type=F32)
            if diag:
                keep = lax.broadcasted_iota(jnp.int32, s.shape, 0) <= lax.broadcasted_iota(jnp.int32, s.shape, 1)
                s = jnp.where(keep, s, -jnp.inf)
                m_new = jnp.max(s, axis=0, keepdims=True)
                p = jnp.exp(s - m_new)
                l_s[h] = jnp.sum(p, axis=0, keepdims=True)
                acc_s[h] = jnp.dot(v_t, p.astype(BF16), preferred_element_type=F32)
            else:
                m_old = m_s[h]
                m_new = jnp.maximum(m_old, jnp.max(s, axis=0, keepdims=True))
                p = jnp.exp(s - m_new)
                alpha = jnp.exp(m_old - m_new)
                l_s[h] = l_s[h] * alpha + jnp.sum(p, axis=0, keepdims=True)
                acc_s[h] = acc_s[h] * alpha + jnp.dot(v_t, p.astype(BF16), preferred_element_type=F32)
            m_s[h] = m_new

    tile(step, True)

    @pl.loop(0, step)
    def _(j):
        tile(j, False)

    outs = []
    for h in range(groups):
        outs.append((acc_s[h] / l_s[h]).astype(BF16))
        lse_ref[0, h:h + 1, :] = m_s[h] + jnp.log(l_s[h])
    o_ref[...] = jnp.concatenate(outs, axis=0).T


def bwd_kernel(n_blk, blk, groups, dim, q_ref, do_ref, o_ref, lse_ref, kv_ref, dq_ref, dkv_ref,
               kt_s, rq_s, rd_s, rqk_s, rdo_s, dot_s, dqt_s, dkv_s):
    step = pl.program_id(0)

    @pl.when(step == 0)
    def _():
        for b in range(n_blk):
            kt_s[:, b * blk:(b + 1) * blk] = kv_ref[b * blk:(b + 1) * blk, :].T
        rq_s[...] = jnp.zeros_like(rq_s)
        rd_s[...] = jnp.zeros_like(rd_s)
        dkv_s[...] = jnp.zeros_like(dkv_s)

    q = q_ref[...]
    do = do_ref[...]
    q_t = q.T
    do_t = do.T
    o_t = o_ref[...].T
    zero = jnp.zeros((blk, dim), BF16)
    for h in range(groups):
        rows = slice(h * dim, (h + 1) * dim)
        rq_s[h, :dim, :] = q_t[rows, :]
        rd_s[h, dim:, :] = do_t[rows, :]
        rqk_s[h] = jnp.concatenate([q[:, rows], zero], axis=1)
        rdo_s[h] = jnp.concatenate([zero, do[:, rows]], axis=1)
        dot_s[h] = jnp.sum(do_t[rows, :].astype(F32) * o_t[rows, :].astype(F32), axis=0, keepdims=True)
    dqt_s[...] = jnp.zeros_like(dqt_s)

    def tile(j, diag):
        off = pl.multiple_of(stored_block(j, n_blk) * blk, blk)
        kv_j = kv_ref[pl.ds(off, blk), :]
        k_t = kt_s[:dim, pl.ds(off, blk)]
        total = dkv_s[pl.ds(off, blk), :]
        for h in range(groups):
            s = jnp.dot(kv_j, rq_s[h], preferred_element_type=F32)
            p = jnp.exp(s - lse_ref[0, h:h + 1, :])
            if diag:
                keep = lax.broadcasted_iota(jnp.int32, s.shape, 0) <= lax.broadcasted_iota(jnp.int32, s.shape, 1)
                p = jnp.where(keep, p, 0.0)
            dp = jnp.dot(kv_j, rd_s[h], preferred_element_type=F32)
            ds = (p * (dp - dot_s[h])).astype(BF16)
            dqt_s[h] += jnp.dot(k_t, ds, preferred_element_type=F32)
            total += jnp.dot(ds, rqk_s[h], preferred_element_type=F32)
            total += jnp.dot(p.astype(BF16), rdo_s[h], preferred_element_type=F32)
        dkv_s[pl.ds(off, blk), :] = total

    tile(step, True)

    @pl.loop(0, step)
    def _(j):
        tile(j, False)

    scale = dim ** -0.5
    dq_ref[...] = jnp.concatenate([(dqt_s[h] * scale).astype(BF16) for h in range(groups)], axis=0).T

    @pl.when(step == n_blk - 1)
    def _():
        dkv_ref[...] = dkv_s[...].astype(BF16)


def row_block_spec(n_blk, blk, cols):
    return pl.BlockSpec((blk, cols), lambda i: (stored_block(i, n_blk), 0))


def attend(q, kv, n_blk, groups, dim):
    rows = q.shape[0]
    blk = rows // n_blk
    cols = groups * dim
    full = pl.BlockSpec((rows, 2 * dim), lambda i: (0, 0))
    elems = rows * rows * groups // 2
    return pl.pallas_call(
        lambda *refs: fwd_kernel(n_blk, blk, groups, dim, *refs),
        grid=(n_blk,),
        in_specs=[row_block_spec(n_blk, blk, cols), full],
        out_specs=[row_block_spec(n_blk, blk, cols), pl.BlockSpec((1, groups, blk), lambda i: (i, 0, 0))],
        out_shape=[jax.ShapeDtypeStruct((rows, cols), BF16), jax.ShapeDtypeStruct((n_blk, groups, blk), F32)],
        scratch_shapes=[
            pltpu.VMEM((2 * dim, rows), BF16),
            pltpu.VMEM((groups, 2 * dim, blk), BF16),
            pltpu.VMEM((groups, dim, blk), F32),
            pltpu.VMEM((groups, 1, blk), F32),
            pltpu.VMEM((groups, 1, blk), F32),
        ],
        compiler_params=pltpu.CompilerParams(dimension_semantics=("arbitrary",), vmem_limit_bytes=VMEM_LIMIT),
        cost_estimate=pl.CostEstimate(flops=elems * 4 * dim * 4, bytes_accessed=rows * cols * 6, transcendentals=elems),
        name="attend_fwd",
    )(q, kv)


def attend_grad(q, do, o, lse, kv, n_blk, groups, dim):
    rows = q.shape[0]
    blk = rows // n_blk
    cols = groups * dim
    full = pl.BlockSpec((rows, 2 * dim), lambda i: (0, 0))
    elems = rows * rows * groups // 2
    row_spec = row_block_spec(n_blk, blk, cols)
    return pl.pallas_call(
        lambda *refs: bwd_kernel(n_blk, blk, groups, dim, *refs),
        grid=(n_blk,),
        in_specs=[row_spec, row_spec, row_spec, pl.BlockSpec((1, groups, blk), lambda i: (i, 0, 0)), full],
        out_specs=[row_spec, full],
        out_shape=[jax.ShapeDtypeStruct((rows, cols), BF16), jax.ShapeDtypeStruct((rows, 2 * dim), BF16)],
        scratch_shapes=[
            pltpu.VMEM((2 * dim, rows), BF16),
            pltpu.VMEM((groups, 2 * dim, blk), BF16),
            pltpu.VMEM((groups, 2 * dim, blk), BF16),
            pltpu.VMEM((groups, blk, 2 * dim), BF16),
            pltpu.VMEM((groups, blk, 2 * dim), BF16),
            pltpu.VMEM((groups, 1, blk), F32),
            pltpu.VMEM((groups, dim, blk), F32),
            pltpu.VMEM((rows, 2 * dim), F32),
        ],
        compiler_params=pltpu.CompilerParams(dimension_semantics=("arbitrary",), vmem_limit_bytes=VMEM_LIMIT),
        cost_estimate=pl.CostEstimate(flops=elems * 10 * dim * 4, bytes_accessed=rows * cols * 8, transcendentals=elems),
        name="attend_bwd",
    )(q, do, o, lse, kv)


def solution(mesh):
    seq_shards = mesh.shape["cp"]

    def device_fn(x_blk, w_query, w_key, w_value, w_out, dy_blk):
        model_dim, q_heads, dim = w_query.shape
        kv_heads = w_key.shape[1]
        groups = q_heads // kv_heads
        q_cols = q_heads * dim
        n_blk = 2 * seq_shards
        scale = dim ** -0.5
        wq_t = w_query.transpose(1, 2, 0).reshape(q_cols, model_dim)
        wk_t = w_key.transpose(1, 2, 0)
        wv_t = w_value.transpose(1, 2, 0)
        wkv_t = jnp.stack([wk_t, wv_t], axis=1).reshape(2 * kv_heads * dim, model_dim)
        wo = w_out.reshape(q_cols, model_dim)

        def mm(a, b, dims):
            return lax.dot_general(a, b, dims, preferred_element_type=F32)

        def to_heads(a):
            return lax.all_to_all(a, "cp", split_axis=1, concat_axis=0, tiled=True)

        def to_rows(a):
            return lax.all_to_all(a, "cp", split_axis=0, concat_axis=1, tiled=True)

        x_rows = lax.all_gather(x_blk, "tp", axis=0, tiled=True)
        q_own = (mm(x_rows, wq_t, NT).astype(BF16) * scale).astype(BF16)
        kv_own = mm(x_rows, wkv_t, NT).astype(BF16)
        q_all = to_heads(q_own)
        kv_all = to_heads(kv_own)
        dy_rows = lax.all_gather(dy_blk, "tp", axis=0, tiled=True)
        o_all, lse = attend(q_all, kv_all, n_blk, groups, dim)
        do_own = mm(dy_rows, wo, NT).astype(BF16)
        do_all = to_heads(do_own)
        o_own = to_rows(o_all)
        y_part = mm(o_own, wo, (((1,), (0,)), ((), ())))
        y_blk = lax.psum_scatter(y_part, "tp", scatter_dimension=0, tiled=True).astype(BF16)

        dq_all, dkv_all = attend_grad(q_all, do_all, o_all, lse, kv_all, n_blk, groups, dim)
        grad_wo = mm(o_own, dy_rows, TN).astype(BF16).reshape(q_heads, dim, model_dim)
        dq_own = to_rows(dq_all)
        dkv_own = to_rows(dkv_all)
        dx_part = mm(dq_own, wq_t, (((1,), (0,)), ((), ()))) + mm(dkv_own, wkv_t, (((1,), (0,)), ((), ())))
        dx_blk = lax.psum_scatter(dx_part, "tp", scatter_dimension=0, tiled=True).astype(BF16)
        gq_t = mm(dq_own, x_rows, TN).astype(BF16).reshape(q_heads, dim, model_dim)
        gkv_t = mm(dkv_own, x_rows, TN).astype(BF16).reshape(kv_heads, 2, dim, model_dim)
        grad_wq = gq_t.transpose(2, 0, 1)
        grad_wk = gkv_t[:, 0].transpose(2, 0, 1)
        grad_wv = gkv_t[:, 1].transpose(2, 0, 1)
        return y_blk, dx_blk, grad_wq[None], grad_wk[None], grad_wv[None], grad_wo[None]

    return jax.shard_map(device_fn, mesh=mesh,
                         in_specs=(ROW_SPEC, HEAD_SPEC, HEAD_SPEC, HEAD_SPEC, OUT_W_SPEC, ROW_SPEC),
                         out_specs=(ROW_SPEC, ROW_SPEC, GRAD_SPEC, GRAD_SPEC, GRAD_SPEC, GRAD_OUT_SPEC),
                         check_vma=False)
```

time: 932 us -> 618 us (0.66)
  matrix products: 473 us -> 65.2 us
  Pallas kernels: 0 us -> 205 us
  other arithmetic: 93.5 us -> 9.07 us
  blocking collectives: 0 us -> 28.6 us
  loops' own time: 17.7 us -> 0 us
  starting transfers between devices: 35.1 us -> 19.3 us
  waiting for transfers between devices: 260 us -> 248 us
    dot_general x39 -> x9, matrix products: 473 us -> 65.2 us  [mm(): return lax.dot_general(a, b, dims, preferred_element_type=F32)]
    pallas_call x0 -> x2, Pallas kernels: none -> 205 us  [the longest x1 128 us: attend_grad(): pl.pallas_call(lambda *refs: bwd_kernel(n_blk, blk, groups, dim, *refs),...]
    ppermute x20 -> x0, waiting for transfers between devices: 122 us -> none  [the longest x3 75.2 us: backward_step(): k_blk = lax.ppermute(k_blk, 'cp', send_perm)]
    reduce_scatter x1, waiting for transfers between devices: 0.01 us -> 94.8 us  [device_fn(): lax.psum_scatter(y_part, 'tp', scatter_dimension=0, tiled=True).astype(BF16)]
    reduce_sum x4 -> x0, other arithmetic: 62.7 us -> none  [attend_update(): new_sum = row_sum * factor + jnp.sum(prob_mat, axis=-1)]
    reduce_scatter x1, waiting for transfers between devices: 78.8 us -> 36.5 us  [device_fn(): lax.psum_scatter(dx_part, 'tp', scatter_dimension=0, tiled=True)]
    ppermute x20 -> x0, starting transfers between devices: 35 us -> none  [the longest x3 9.6 us: backward_step(): dk_blk = lax.ppermute(dk_blk, 'cp', send_perm)]
    all_to_all x0 -> x5, waiting for transfers between devices: none -> 30.9 us  [the longest x2 27.2 us: to_rows(): return lax.all_to_all(a, 'cp', split_axis=0, concat_axis=1, tiled=True)]
  transfers between devices with their start and end apart: 24 -> 9, of which waited for: 15 -> 7; matrix products, arithmetic and copies ran while one was open for 62% -> 12% of each run, Pallas kernels for 0% -> 13%
where the time goes in v1:
time: 618 us; the launch traced here: 610 us
  waiting for transfers between devices  248 us (40%)
  Pallas kernels  205 us (33%)
  matrix products  65.2 us (11%)
  blocking collectives  28.6 us (5%)
  local copies, waits for them, and re-layouts  19.9 us (3%)
  starting transfers between devices  19.3 us (3%)
  between operations  14.4 us (2%)
  other arithmetic  9.07 us (1%)
    pallas_call x1, Pallas kernels, attend_grad(): pl.pallas_call(lambda *refs: bwd_kernel(n_blk, blk, groups, dim, *refs),...  128 us
    reduce_scatter x1, waiting for transfers between devices, device_fn(): lax.psum_scatter(y_part, 'tp', scatter_dimension=0, tiled=True).astype(BF16)  94.8 us
    pallas_call x1, Pallas kernels, attend(): pl.pallas_call(lambda *refs: fwd_kernel(n_blk, blk, groups, dim, *refs),...  76.7 us
    dot_general x9, matrix products, mm(): return lax.dot_general(a, b, dims, preferred_element_type=F32)  65.2 us
    all_gather x1, waiting for transfers between devices, device_fn(): x_rows = lax.all_gather(x_blk, 'tp', axis=0, tiled=True)  56.4 us
    reduce_scatter x1, waiting for transfers between devices, device_fn(): lax.psum_scatter(dx_part, 'tp', scatter_dimension=0, tiled=True)  36.5 us
    all_to_all x1, blocking collectives, to_rows(): return lax.all_to_all(a, 'cp', split_axis=0, concat_axis=1, tiled=True)  28.6 us
    all_gather x1, waiting for transfers between devices, device_fn(): dy_rows = lax.all_gather(dy_blk, 'tp', axis=0, tiled=True)  28.5 us
  transfers between devices with their start and end apart: 9, of which 7 were waited for; matrix products, arithmetic and copies ran while one was open for 12% of the time, Pallas kernels for 13%

profile of v1, /device:TPU:0, one launch (start us, length us, event | category | flops | bytes accessed | tf_op | source)
XLA Modules:
  0.0 609.7 jit_solution(15691395902720790355)
XLA Ops:
  10.1 56.4 %all-gather.3.cloned.1.call-done = bf16[1024,2048]{1,0:T(8,128)(2,1)} async-done(((bf16[512,2048]{1,0:T(8,128)(2,1)}), bf16[1024,2048]{1,0:T(8,128)(2,1)}) %all-gather.3.cloned.1.call-update) | async-done | bytes 4194320 | tf_op jit(solution)/shard_map/all_gather | solution.py:215
  66.5 4.5 convolution_convert_fusion.4
  75.9 8.0 %convert_multiply_fusion = bf16[1024,1024]{0,1:T(8,128)(2,1)S(1)} fusion(bf16[1024,2048]{1,0:T(8,128)(2,1)} %all-gather.3.cloned.1.call-done, bf16[1024,2048]{1,0:T(8,128)(2,1)} %bitcast.99), kind=kOutput, calls=%fused_computation.5 | convolution fusion | flops 4297064448 | bytes 10485760 | tf_op jit(solution)/shard_map/dot_general | solution.py:207
  86.5 3.6 all-to-all-done.1
  90.1 3.6 all-to-all-start
  93.8 28.5 %all-gather.5.cloned.1.call-done = bf16[1024,2048]{1,0:T(8,128)(2,1)} async-done(((bf16[512,2048]{1,0:T(8,128)(2,1)}), bf16[1024,2048]{1,0:T(8,128)(2,1)}) %all-gather.5.cloned.1.call-update) | async-done | bytes 4194320 | tf_op jit(solution)/shard_map/all_gather | solution.py:220
  122.3 9.3 %convolution_convert_fusion.3 = bf16[1024,1024]{0,1:T(8,128)(2,1)} fusion(bf16[1024,2048]{1,0:T(8,128)(2,1)} %all-gather.5.cloned.1.call-done, bf16[1024,2048]{1,0:T(8,128)(2,1)} %bitcast.101), kind=kOutput, calls=%fused_computation.6 | convolution fusion | flops 4296015872 | bytes 10485760 | tf_op jit(solution)/shard_map/dot_general | solution.py:207
  131.6 3.9 copy.20
  135.5 4.6 all-to-all-start.3
  140.2 76.7 %attend_fwd.1 = (bf16[4096,256]{1,0:T(8,128)(2,1)}, f32[8,4,512]{2,1,0:T(4,128)}) custom-call(bf16[4096,256]{1,0:T(8,128)(2,1)} %bitcast.85, bf16[4096,128]{1,0:T(8,128)(2,1)} %bitcast.93), custom_call_target="tpu_custom_call" | custom-call | flops 34359738368 | bytes 6291456 | tf_op jit(solution)/shard_map/attend_fwd/pallas_call | solution.py:142
  216.8 128.2 %attend_bwd.1 = (bf16[4096,256]{1,0:T(8,128)(2,1)}, bf16[4096,128]{1,0:T(8,128)(2,1)}) custom-call(bf16[4096,256]{1,0:T(8,128)(2,1)} %bitcast.86, bf16[4096,256]{1,0:T(8,128)(2,1)} %bitcast.21.refs_1_, bf16[4096,256]{1,0:T(8,128)(2,1)} %get-tuple-element.10.refs_2_, f32[8,4,512]{2,1,0:T(4,128)} %get-tuple-element.11.refs_3_, bf16[4096,128]{1,0:T(8,128)(2,1)} %bitcast.94), custom_call_target="tpu_custom_call" | custom-call | flops 85899345920 | bytes 8388608 | tf_op jit(solution)/shard_map/attend_bwd/pallas_call | solution.py:168
  345.0 4.0 copy.21
  354.0 24.1 %all-to-all-done.4 = bf16[4,1024,256]{1,2,0:T(8,128)(2,1)S(1)} async-done(((bf16[4,1024,256]{1,2,0:T(8,128)(2,1)}), bf16[4,1024,256]{1,2,0:T(8,128)(2,1)S(1)}, u32[]{:S(2)}, u32[]{:S(2)}) %all-to-all-start.4) | async-done | bytes 2097184 | tf_op jit(solution)/shard_map/all_to_all | solution.py:213
  381.9 10.8 %fusion.1 = f32[1024,2048]{1,0:T(8,128)} fusion(bf16[1024,1024]{0,1:T(8,128)(2,1)} %bitcast.82, bf16[1024,2048]{1,0:T(8,128)(2,1)} %bitcast.100), kind=kOutput, calls=%fused_computation.11 | convolution fusion | flops 4294967296 | bytes 14680064 | tf_op jit(solution)/shard_map/dot_general | solution.py:207
  395.8 9.0 %convolution_add_fusion = f32[1024,2048]{1,0:T(8,128)} fusion(f32[1024,2048]{1,0:T(8,128)} %fusion.1, bf16[1024,512]{0,1:T(8,128)(2,1)S(1)} %bitcast.80, bf16[512,2048]{1,0:T(8,128)(2,1)S(1)} %bitcast.79), kind=kOutput, calls=%fused_computation | convolution fusion | flops 2149580800 | bytes 19922944 | tf_op jit(solution)/shard_map/dot_general | solution.py:207
  407.9 28.6 %all_to_all.114 = bf16[4,1024,256]{1,2,0:T(8,128)(2,1)S(1)} all-to-all(bf16[4,1024,256]{1,2,0:T(8,128)(2,1)S(1)} %copy.19), channel_id=1, replica_groups=mesh['dp'=1,'tp'=2,'cp'=4] {'cp'}, dimensions={0} | all-to-all | bytes 4194304 | tf_op jit(solution)/shard_map/all_to_all | solution.py:213
  437.9 6.9 %fusion = f32[1024,2048]{1,0:T(8,128)} fusion(bf16[1024,1024]{0,1:T(8,128)(2,1)S(1)} %bitcast.87, bf16[1024,2048]{1,0:T(8,128)(2,1)S(1)} %bitcast.102), kind=kOutput, calls=%fused_computation.10 | convolution fusion | flops 4294967296 | bytes 14680064 | tf_op jit(solution)/shard_map/dot_general | solution.py:207
  444.7 4.7 convolution_convert_fusion.2
  451.8 6.0 convolution_convert_fusion
  457.8 6.0 convolution_convert_fusion.1
  463.8 36.5 %reduce-scatter.5.cloned.1.call-done = f32[512,2048]{1,0:T(8,128)} async-done(((f32[1024,2048]{1,0:T(8,128)}), f32[512,2048]{1,0:T(8,128)}) %reduce-scatter.5.cloned.1.call-update) | async-done | bytes 4194320 | tf_op jit(solution)/shard_map/reduce_scatter | solution.py:233
  500.3 3.8 convert_element_type.32
  504.2 94.8 %reduce-scatter.3.cloned.1.call-done = f32[512,2048]{1,0:T(8,128)} async-done(((f32[1024,2048]{1,0:T(8,128)}), f32[512,2048]{1,0:T(8,128)}) %reduce-scatter.3.cloned.1.call-update) | async-done | bytes 4194320 | tf_op jit(solution)/shard_map/reduce_scatter | solution.py:226
  598.9 3.8 convert_element_type.30
  (46 shorter events, 28.9 us)
Async XLA Ops:
  7.2 1.5 copy-start.9
  7.2 59.4 %all-gather.3.cloned.1.call-start = ((), (), s32[]{:S(2)}) async-start(), calls=%async_computation.8 | async-start | bytes 6291456 | tf_op jit(solution)/shard_map/all_gather | solution.py:215
  7.9 114.4 %all-gather.5.cloned.1.call-start = ((), (), s32[]{:S(2)}) async-start(), calls=%async_computation.10 | async-start | bytes 6291456 | tf_op jit(solution)/shard_map/all_gather | solution.py:220
  10.1 61.0 %copy-start = (bf16[4,2,64,2048]{3,2,1,0:T(8,128)(2,1)}, bf16[4,2,64,2048]{3,2,1,0:T(8,128)(2,1)S(1)}, u32[]{:S(2)}) copy-start(bf16[4,2,64,2048]{3,2,1,0:T(8,128)(2,1)S(1)} %pad_maximum_fusion) | copy-start | bytes 6291460
  72.4 17.7 %all-to-all-start.1 = ((bf16[1024,4,128]{2,0,1:T(8,128)(2,1)}), bf16[1024,4,128]{2,0,1:T(8,128)(2,1)S(1)}, u32[]{:S(2)}, u32[]{:S(2)}) async-start(bf16[1024,4,128]{2,0,1:T(8,128)(2,1)} %copy.18), calls=%async_computation.1 | async-start | bytes 2097152 | tf_op jit(solution)/shard_map/all_to_all | solution.py:210
  90.1 41.4 %copy-start.7 = (bf16[1024,4,128]{2,0,1:T(8,128)(2,1)}, bf16[1024,4,128]{2,0,1:T(8,128)(2,1)S(1)}, u32[]{:S(2)}) copy-start(bf16[1024,4,128]{2,0,1:T(8,128)(2,1)S(1)} %all-to-all-done.1) | copy-start | bytes 3145732
  90.1 45.4 %all-to-all-start = ((bf16[1024,4,256]{2,0,1:T(8,128)(2,1)}), bf16[1024,4,256]{2,0,1:T(8,128)(2,1)S(1)}, u32[]{:S(2)}, u32[]{:S(2)}) async-start(bf16[1024,4,256]{2,0,1:T(8,128)(2,1)} %copy.17), calls=%async_computation | async-start | bytes 4194304 | tf_op jit(solution)/shard_map/all_to_all | solution.py:210
  135.5 4.6 copy-start.4
  135.5 81.3 %all-to-all-start.3 = ((bf16[1024,4,256]{2,0,1:T(8,128)(2,1)}), bf16[1024,4,256]{2,0,1:T(8,128)(2,1)}, u32[]{:S(2)}, u32[]{:S(2)}) async-start(bf16[1024,4,256]{2,0,1:T(8,128)(2,1)} %copy.20), calls=%async_computation.4 | async-start | bytes 4194304 | tf_op jit(solution)/shard_map/all_to_all | solution.py:210
  345.0 7.7 %copy-start.8 = (bf16[4096,128]{1,0:T(8,128)(2,1)S(1)}, bf16[4096,128]{1,0:T(8,128)(2,1)}, u32[]{:S(2)}) copy-start(bf16[4096,128]{1,0:T(8,128)(2,1)} %get-tuple-element.13) | copy-start | bytes 3145732
  349.0 29.0 %all-to-all-start.4 = ((bf16[4,1024,256]{1,2,0:T(8,128)(2,1)}), bf16[4,1024,256]{1,2,0:T(8,128)(2,1)S(1)}, u32[]{:S(2)}, u32[]{:S(2)}) async-start(bf16[4,1024,256]{1,2,0:T(8,128)(2,1)} %copy.21), calls=%async_computation.5 | async-start | bytes 4194304 | tf_op jit(solution)/shard_map/all_to_all | solution.py:213
  378.1 3.8 copy-start.2
  378.1 17.7 %all-to-all-start.5 = ((bf16[4,1024,128]{1,2,0:T(8,128)(2,1)}), bf16[4,1024,128]{1,2,0:T(8,128)(2,1)S(1)}, u32[]{:S(2)}, u32[]{:S(2)}) async-start(bf16[4,1024,128]{1,2,0:T(8,128)(2,1)} %copy.22), calls=%async_computation.6 | async-start | bytes 2097152 | tf_op jit(solution)/shard_map/all_to_all | solution.py:213
  381.6 118.7 %reduce-scatter.5.cloned.1.call-start = ((), (), s32[]{:S(2)}) async-start(), calls=%async_computation.11 | async-start | bytes 12582912 | tf_op jit(solution)/shard_map/reduce_scatter | solution.py:233
  381.9 13.9 %copy-start.1 = (bf16[4,2,64,2048]{3,2,1,0:T(8,128)(2,1)S(1)}, bf16[4,2,64,2048]{3,2,1,0:T(8,128)(2,1)}, u32[]{:S(2)}) copy-start(bf16[4,2,64,2048]{3,2,1,0:T(8,128)(2,1)} %copy-done) | copy-start | bytes 6291460
  404.8 194.1 %reduce-scatter.3.cloned.1.call-start = ((), (), s32[]{:S(2)}) async-start(), calls=%async_computation.9 | async-start | bytes 12582912 | tf_op jit(solution)/shard_map/reduce_scatter | solution.py:226
  407.9 30.0 %copy-start.10 = (bf16[16,64,2048]{2,1,0:T(8,128)(2,1)S(1)}, bf16[16,64,2048]{2,1,0:T(8,128)(2,1)}, u32[]{:S(2)}) copy-start(bf16[16,64,2048]{2,1,0:T(8,128)(2,1)} %param.10) | copy-start | bytes 12582916
  436.5 1.3 copy-start.5
  444.7 6.2 %copy-start.12 = (bf16[1024,2048]{1,0:T(8,128)(2,1)S(1)}, bf16[1024,2048]{1,0:T(8,128)(2,1)}, u32[]{:S(2)}) copy-start(bf16[1024,2048]{1,0:T(8,128)(2,1)} %all-gather.5.cloned.1.call-done) | copy-start | bytes 12582916
  449.4 2.4 copy-start.6
  451.8 6.0 copy-start.3
  451.8 6.0 copy-start.11
Sparse Core Ops, SparseCore 0:
  9.5 57.0 all-gather.2
  68.0 54.1 all-gather.4
  404.9 95.3 reduce-scatter.4
  502.4 96.4 reduce-scatter.2

commit v2 on v1

v2 whole, which is shorter than its diff:
```python
import jax
import jax.numpy as jnp
from jax import lax
from jax.experimental import pallas as pl
from jax.experimental.pallas import tpu as pltpu
from jax.sharding import PartitionSpec as P

ROW_SPEC = P(("dp", "cp", "tp"), None)
HEAD_SPEC = P(None, "tp", None)
OUT_W_SPEC = P("tp", None, None)
GRAD_SPEC = P(("dp", "cp"), None, "tp", None)
GRAD_OUT_SPEC = P(("dp", "cp"), "tp", None, None)
NT = (((1,), (1,)), ((), ()))
TN = (((0,), (0,)), ((), ()))
NN = (((1,), (0,)), ((), ()))
F32 = jnp.float32
BF16 = jnp.bfloat16
VMEM_LIMIT = 60 * 1024 * 1024


def half_of(pos_blk, n_blk):
    return jnp.where(pos_blk < n_blk // 2, 0, 1)


def shard_of(pos_blk, n_blk):
    return jnp.where(pos_blk < n_blk // 2, pos_blk, n_blk - 1 - pos_blk)


def stored_block(pos_blk, n_blk):
    return 2 * shard_of(pos_blk, n_blk) + half_of(pos_blk, n_blk)


def keep_mask(shape):
    return lax.broadcasted_iota(jnp.int32, shape, 0) <= lax.broadcasted_iota(jnp.int32, shape, 1)


def load_keys(n_blk, own_ref, other_ref, kv_s, kvt_s):
    own_half = lax.axis_index("tp")
    for b in range(n_blk):
        half, shard = (0, b) if b < n_blk // 2 else (1, n_blk - 1 - b)
        block = jnp.where(own_half == half, own_ref[shard], other_ref[shard])
        kv_s[b] = block
        kvt_s[b] = block.T


def load_queries(n_blk, pos, own_ref, other_ref):
    return jnp.where(lax.axis_index("tp") == half_of(pos, n_blk), own_ref[...], other_ref[...])


def fwd_kernel(n_blk, groups, dim, first, *refs):
    q_own, q_other, kv_own, kv_other = refs[:4]
    o_ref, lse_ref, kv_s, kvt_s, rq_s, acc_s, m_s, l_s = refs[-8:]
    pos = first + pl.program_id(0)

    @pl.when(pl.program_id(0) == 0)
    def _():
        load_keys(n_blk, kv_own, kv_other, kv_s, kvt_s)
        rq_s[...] = jnp.zeros_like(rq_s)

    q_t = load_queries(n_blk, pos, q_own, q_other).T
    for h in range(groups):
        rq_s[h, :dim, :] = q_t[h * dim:(h + 1) * dim, :]

    def tile(j, diag):
        kv_j = kv_s[j]
        v_t = kvt_s[j, dim:, :]
        for h in range(groups):
            s = jnp.dot(kv_j, rq_s[h], preferred_element_type=F32)
            if diag:
                s = jnp.where(keep_mask(s.shape), s, -jnp.inf)
                m_new = jnp.max(s, axis=0, keepdims=True)
                p = jnp.exp(s - m_new)
                l_s[h] = jnp.sum(p, axis=0, keepdims=True)
                acc_s[h] = jnp.dot(v_t, p.astype(BF16), preferred_element_type=F32)
            else:
                m_old = m_s[h]
                m_new = jnp.maximum(m_old, jnp.max(s, axis=0, keepdims=True))
                p = jnp.exp(s - m_new)
                alpha = jnp.exp(m_old - m_new)
                l_s[h] = l_s[h] * alpha + jnp.sum(p, axis=0, keepdims=True)
                acc_s[h] = acc_s[h] * alpha + jnp.dot(v_t, p.astype(BF16), preferred_element_type=F32)
            m_s[h] = m_new

    tile(pos, True)

    @pl.loop(0, pos)
    def _(j):
        tile(j, False)

    for h in range(groups):
        o_ref[h * dim:(h + 1) * dim, :] = (acc_s[h] / l_s[h]).astype(BF16)
        lse_ref[h:h + 1, :] = m_s[h] + jnp.log(l_s[h])


def bwd_kernel(n_blk, groups, dim, first, count, *refs):
    q_own, q_other, kv_own, kv_other, do_ref, o_ref, lse_ref = refs[:7]
    upper = first > 0
    g_ref = refs[7 if upper else 8]
    kv_s, kvt_s, rq_s, rd_s, rqk_s, rdo_s, dot_s, dqt_s, dkv_s = refs[-9:]
    step = pl.program_id(0)
    pos = first + step
    blk = do_ref.shape[0]
    cols = groups * dim

    @pl.when(step == 0)
    def _():
        load_keys(n_blk, kv_own, kv_other, kv_s, kvt_s)
        rq_s[...] = jnp.zeros_like(rq_s)
        rd_s[...] = jnp.zeros_like(rd_s)
        dkv_s[...] = jnp.zeros_like(dkv_s) if upper else refs[7][...]

    q = load_queries(n_blk, pos, q_own, q_other)
    do = do_ref[...]
    q_t = q.T
    do_t = do.T
    zero = jnp.zeros((blk, dim), BF16)
    for h in range(groups):
        rows = slice(h * dim, (h + 1) * dim)
        rq_s[h, :dim, :] = q_t[rows, :]
        rd_s[h, dim:, :] = do_t[rows, :]
        rqk_s[h] = jnp.concatenate([q[:, rows], zero], axis=1)
        rdo_s[h] = jnp.concatenate([zero, do[:, rows]], axis=1)
        dot_s[h] = jnp.sum(do_t[rows, :].astype(F32) * o_ref[rows, :].astype(F32), axis=0, keepdims=True)
    dqt_s[...] = jnp.zeros_like(dqt_s)

    def tile(j, diag):
        kv_j = kv_s[j]
        k_t = kvt_s[j, :dim, :]
        total = dkv_s[j]
        for h in range(groups):
            s = jnp.dot(kv_j, rq_s[h], preferred_element_type=F32)
            p = jnp.exp(s - lse_ref[h:h + 1, :])
            if diag:
                p = jnp.where(keep_mask(s.shape), p, 0.0)
            dp = jnp.dot(kv_j, rd_s[h], preferred_element_type=F32)
            ds = (p * (dp - dot_s[h])).astype(BF16)
            dqt_s[h] += jnp.dot(k_t, ds, preferred_element_type=F32)
            total += jnp.dot(ds, rqk_s[h], preferred_element_type=F32)
            total += jnp.dot(p.astype(BF16), rdo_s[h], preferred_element_type=F32)
        dkv_s[j] = total

    tile(pos, True)

    @pl.loop(0, pos)
    def _(j):
        tile(j, False)

    shard = shard_of(pos, n_blk)
    for h in range(groups):
        g_ref[shard, h * dim:(h + 1) * dim, :] = dqt_s[h].astype(BF16)

    @pl.when(step == count - 1)
    def _():
        for b in range(first, first + count):
            s = b if b < n_blk // 2 else n_blk - 1 - b
            g_ref[s, cols:, :] = dkv_s[b].astype(BF16).T
        if upper:
            refs[8][...] = dkv_s[:first]


def key_specs(n_half, blk, groups, dim, first):
    cols = groups * dim
    query = pl.BlockSpec((None, blk, cols), lambda i: (shard_of(first + i, 2 * n_half), 0, 0))
    keys = pl.BlockSpec((n_half, blk, 2 * dim), lambda i: (0, 0, cols // (2 * dim)))
    return [query, query, keys, keys]


def feature_spec(n_blk, cols, blk, first):
    return pl.BlockSpec((None, cols, blk), lambda i: (shard_of(first + i, n_blk), 0, half_of(first + i, n_blk)))


def attend(own, other, prev, first, count, groups, dim):
    n_half, blk = own.shape[:2]
    n_blk = 2 * n_half
    cols = groups * dim
    elems = blk * blk * groups * sum(range(first + 1, first + count + 1))
    out_shape = [jax.ShapeDtypeStruct((n_half, cols, 2 * blk), BF16), jax.ShapeDtypeStruct((n_blk, groups, blk), F32)]
    return pl.pallas_call(
        lambda *refs: fwd_kernel(n_blk, groups, dim, first, *refs),
        grid=(count,),
        in_specs=key_specs(n_half, blk, groups, dim, first) + [pl.BlockSpec(memory_space=pl.ANY)] * len(prev),
        out_specs=[feature_spec(n_blk, cols, blk, first), pl.BlockSpec((None, groups, blk), lambda i: (first + i, 0, 0))],
        out_shape=out_shape,
        input_output_aliases={4 + i: i for i in range(len(prev))},
        scratch_shapes=[
            pltpu.VMEM((n_blk, blk, 2 * dim), BF16),
            pltpu.VMEM((n_blk, 2 * dim, blk), BF16),
            pltpu.VMEM((groups, 2 * dim, blk), BF16),
            pltpu.VMEM((groups, dim, blk), F32),
            pltpu.VMEM((groups, 1, blk), F32),
            pltpu.VMEM((groups, 1, blk), F32),
        ],
        compiler_params=pltpu.CompilerParams(dimension_semantics=("arbitrary",), vmem_limit_bytes=VMEM_LIMIT),
        cost_estimate=pl.CostEstimate(flops=elems * 4 * 4 * dim, bytes_accessed=count * blk * cols * 4, transcendentals=elems),
        name="attend_fwd",
    )(own, other, own, other, *prev)


def attend_grad(own, other, do, o, lse, carried, first, count, groups, dim):
    n_half, blk = own.shape[:2]
    n_blk = 2 * n_half
    cols = groups * dim
    elems = blk * blk * groups * sum(range(first + 1, first + count + 1))
    feats = cols + 2 * dim
    keys_shape = (n_blk, blk, 2 * dim) if first else (n_half, blk, 2 * dim)
    whole = pl.BlockSpec((n_half, blk, 2 * dim), lambda i: (0, 0, 0))
    out_specs = [pl.BlockSpec((n_half, feats, blk), lambda i: (0, 0, 0))] + [whole] * (first > 0)
    out_shape = [jax.ShapeDtypeStruct((n_half, feats, blk), BF16)] + [jax.ShapeDtypeStruct((n_half, blk, 2 * dim), F32)] * (first > 0)
    return pl.pallas_call(
        lambda *refs: bwd_kernel(n_blk, groups, dim, first, count, *refs),
        grid=(count,),
        in_specs=key_specs(n_half, blk, groups, dim, first) + [
            pl.BlockSpec((None, blk, cols), lambda i: (stored_block(first + i, n_blk), 0, 0)),
            feature_spec(n_blk, cols, blk, first),
            pl.BlockSpec((None, groups, blk), lambda i: (first + i, 0, 0))] + [whole] * len(carried),
        out_specs=out_specs,
        out_shape=out_shape,
        scratch_shapes=[
            pltpu.VMEM((n_blk, blk, 2 * dim), BF16),
            pltpu.VMEM((n_blk, 2 * dim, blk), BF16),
            pltpu.VMEM((groups, 2 * dim, blk), BF16),
            pltpu.VMEM((groups, 2 * dim, blk), BF16),
            pltpu.VMEM((groups, blk, 2 * dim), BF16),
            pltpu.VMEM((groups, blk, 2 * dim), BF16),
            pltpu.VMEM((groups, 1, blk), F32),
            pltpu.VMEM((groups, dim, blk), F32),
            pltpu.VMEM(keys_shape, F32),
        ],
        compiler_params=pltpu.CompilerParams(dimension_semantics=("arbitrary",), vmem_limit_bytes=VMEM_LIMIT),
        cost_estimate=pl.CostEstimate(flops=elems * 10 * 4 * dim, bytes_accessed=count * blk * cols * 8, transcendentals=elems),
        name="attend_bwd",
    )(own, other, own, other, do, o, lse, *carried)


def solution(mesh):
    seq_shards = mesh.shape["cp"]
    swap = [(0, 1), (1, 0)]

    def device_fn(x_blk, w_query, w_key, w_value, w_out, dy_blk):
        model_dim, q_heads, dim = w_query.shape
        half_rows = x_blk.shape[0]
        kv_heads = w_key.shape[1]
        groups = q_heads // kv_heads
        cols = groups * dim
        feats = cols + 2 * dim
        q_cols = q_heads * dim
        n_half = seq_shards
        n_blk = 2 * seq_shards
        scale = dim ** -0.5
        mine = lax.axis_index("tp")
        quarter = lax.axis_index("cp")
        wo = w_out.reshape(q_cols, model_dim)
        w_all = jnp.concatenate([(w_query * scale).astype(BF16).transpose(1, 2, 0).reshape(kv_heads, cols, model_dim),
                                 w_key.transpose(1, 2, 0), w_value.transpose(1, 2, 0)], axis=1)
        w_flat = w_all.reshape(kv_heads * feats, model_dim)

        def mm(a, b, dims):
            return lax.dot_general(a, b, dims, preferred_element_type=F32)

        def exchange(a):
            return lax.ppermute(a, "tp", swap)

        def switch(a):
            return lax.all_to_all(a, "cp", split_axis=0, concat_axis=0, tiled=True)

        def project(rows):
            return mm(rows, w_flat, NT).astype(BF16).reshape(half_rows, kv_heads, feats).transpose(1, 0, 2)

        def after(value, other):
            return lax.optimization_barrier((value, other))

        def quarter_of(w):
            part = w.shape[0] // seq_shards
            return exchange(lax.dynamic_slice_in_dim(w, quarter * part, part, axis=0))

        def spread(w):
            return lax.all_gather(w, "cp", axis=0, tiled=True)

        x_peer = exchange(x_blk)
        own = switch(project(x_blk))
        x_peer, own = after(x_peer, own)
        dy_late, x_peer = after(dy_blk, x_peer)
        dy_rows = lax.all_gather(dy_late, "tp", axis=0, tiled=True)
        other = switch(project(x_peer))

        partial = attend(own, other, (), 0, n_half, groups, dim)
        dy_ready, partial = after(dy_rows, partial)
        do_own = mm(dy_ready, wo, NT).astype(BF16).reshape(2 * half_rows, kv_heads, cols).transpose(1, 0, 2)
        late, do_own = after((w_flat, wo), do_own)
        do_all = switch(do_own).reshape(n_blk, half_rows, cols)
        quarters = tuple(quarter_of(w) for w in late)
        o_all, lse = attend(own, other, partial, n_half, n_half, groups, dim)
        quarters, o_all = after(quarters, o_all)
        w_peer, wo_peer = (spread(w) for w in quarters)

        o_own = switch(o_all).reshape(q_cols, 2 * half_rows)
        g_upper, carried = attend_grad(own, other, do_all, o_all, lse, (), n_half, n_half, groups, dim)
        g_upper, o_own = after(g_upper, o_own)
        o_mine = lax.dynamic_slice_in_dim(o_own, mine * half_rows, half_rows, axis=1)
        o_peer = exchange(lax.dynamic_slice_in_dim(o_own, (1 - mine) * half_rows, half_rows, axis=1))
        g_upper = switch(g_upper)
        g_lower, = attend_grad(own, other, do_all, o_all, lse, (carried,), 0, n_half, groups, dim)
        g_lower = switch(g_lower)

        is_first = mine == 0
        g_mine = jnp.where(is_first, g_lower, g_upper)
        g_other = jnp.where(is_first, g_upper, g_lower)
        g_peer = exchange(g_other).reshape(kv_heads * feats, half_rows)

        def weight_grad(lo, hi, factor):
            def part(g, rows):
                return mm(g[:, lo:hi].reshape(kv_heads * (hi - lo), half_rows), rows, NN)

            total = part(g_mine, x_blk) + part(g_other, x_peer)
            return (total * factor).astype(BF16).reshape(1, -1, dim, model_dim).transpose(0, 3, 1, 2)

        grad_wo = mm(o_own, dy_rows, NN).astype(BF16).reshape(1, q_heads, dim, model_dim)
        y_blk = (mm(o_mine, wo, TN) + mm(o_peer, wo_peer, TN)).astype(BF16)
        grad_wq = weight_grad(0, cols, scale)
        grad_wk = weight_grad(cols, cols + dim, 1.0)
        grad_wv = weight_grad(cols + dim, feats, 1.0)
        dx_blk = (mm(g_mine.reshape(kv_heads * feats, half_rows), w_flat, TN) + mm(g_peer, w_peer, TN)).astype(BF16)
        return y_blk, dx_blk, grad_wq, grad_wk, grad_wv, grad_wo

    return jax.shard_map(device_fn, mesh=mesh,
                         in_specs=(ROW_SPEC, HEAD_SPEC, HEAD_SPEC, HEAD_SPEC, OUT_W_SPEC, ROW_SPEC),
                         out_specs=(ROW_SPEC, ROW_SPEC, GRAD_SPEC, GRAD_SPEC, GRAD_SPEC, GRAD_OUT_SPEC),
                         check_vma=False)
```

time: 618 us -> 496 us (0.80)
  waiting for transfers between devices: 248 us -> 116 us
  starting transfers between devices: 19.3 us -> 27.4 us
  Pallas kernels: 205 us -> 212 us
    reduce_scatter x2 -> x0, waiting for transfers between devices: 131 us -> none  [the longest x1 94.8 us: device_fn(): lax.psum_scatter(y_part, 'tp', scatter_dimension=0, tiled=True).astype(BF16)]
    all_gather x2 -> x3, waiting for transfers between devices: 84.9 us -> 0.01 us  [the longest x2 0.01 us: spread(): return lax.all_gather(w, 'cp', axis=0, tiled=True)]
    all_to_all x5, waiting for transfers between devices: 30.9 us -> 91.5 us  [switch(): return lax.all_to_all(a, 'cp', split_axis=0, concat_axis=0, tiled=True)]
    ppermute x0 -> x5, waiting for transfers between devices: none -> 24 us  [exchange(): return lax.ppermute(a, 'tp', swap)]
    all_to_all x6 -> x0, local copies, waits for them, and re-layouts: 16.1 us -> none  [the longest x3 8.35 us: to_rows(): return lax.all_to_all(a, 'cp', split_axis=0, concat_axis=1, tiled=True)]
    ppermute x0 -> x5, starting transfers between devices: none -> 8.4 us  [exchange(): return lax.ppermute(a, 'tp', swap)]
    convert_element_type x2 -> x0, other arithmetic: 7.65 us -> none  [the longest x1 3.83 us: device_fn(): lax.psum_scatter(dx_part, 'tp', scatter_dimension=0, tiled=True)]
    pallas_call x2 -> x4, Pallas kernels: 205 us -> 212 us  [the longest x2 133 us: attend_grad(): pl.pallas_call(lambda *refs: bwd_kernel(n_blk, groups, dim, first, count,...]
  transfers between devices with their start and end apart: 9 -> 13, of which waited for: 7 -> 6; matrix products, arithmetic and copies ran while one was open for 12% -> 14% of each run, Pallas kernels for 13% -> 43%
where the time goes in v2:
time: 496 us; the launch traced here: 488 us
  Pallas kernels  212 us (43%)
  waiting for transfers between devices  116 us (23%)
  matrix products  68.8 us (14%)
  starting transfers between devices  27.4 us (6%)
  blocking collectives  23.3 us (5%)
  local copies, waits for them, and re-layouts  18 us (4%)
  between operations  14.2 us (3%)
  other arithmetic  8.54 us (2%)
    pallas_call x2, Pallas kernels, attend_grad(): pl.pallas_call(lambda *refs: bwd_kernel(n_blk, groups, dim, first, count,...  133 us
    all_to_all x5, waiting for transfers between devices, switch(): return lax.all_to_all(a, 'cp', split_axis=0, concat_axis=0, tiled=True)  91.5 us
    pallas_call x2, Pallas kernels, attend(): pl.pallas_call(lambda *refs: fwd_kernel(n_blk, groups, dim, first, *refs)...  78.9 us
    dot_general x14, matrix products, mm(): return lax.dot_general(a, b, dims, preferred_element_type=F32)  68.8 us
    ppermute x5, waiting for transfers between devices, exchange(): return lax.ppermute(a, 'tp', swap)  24 us
    all_to_all x1, blocking collectives, switch(): return lax.all_to_all(a, 'cp', split_axis=0, concat_axis=0, tiled=True)  23.3 us
    all_to_all x5, starting transfers between devices, switch(): return lax.all_to_all(a, 'cp', split_axis=0, concat_axis=0, tiled=True)  18.7 us
  transfers between devices with their start and end apart: 13, of which 6 were waited for; matrix products, arithmetic and copies ran while one was open for 14% of the time, Pallas kernels for 43%

profile of v2, /device:TPU:0, one launch (start us, length us, event | category | flops | bytes accessed | tf_op | source)
XLA Modules:
  0.0 488.0 jit_solution(14042681385721173935)
XLA Ops:
  13.2 4.6 pad_maximum_fusion
  22.2 23.3 %all_to_all.30.refs_0_.refs_2_ = bf16[4,512,384]{2,1,0:T(8,128)(2,1)} all-to-all(bf16[4,512,384]{2,1,0:T(8,128)(2,1)S(1)} %bitcast.71), channel_id=1, replica_groups=mesh['dp'=1,'tp'=2,'cp'=4] {'cp'}, dimensions={0} | all-to-all | bytes 3145728 | tf_op jit(solution)/shard_map/all_to_all | solution.py:264
  45.5 11.1 %collective-permute-done = bf16[512,2048]{1,0:T(8,128)(2,1)} collective-permute-done((bf16[512,2048]{1,0:T(8,128)(2,1)}, bf16[512,2048]{1,0:T(8,128)(2,1)}, u32[]{:S(2)}, u32[]{:S(2)}) %collective-permute-start) | collective-permute-done | bytes 2097184 | tf_op jit(solution)/shard_map/ppermute | solution.py:261
  56.6 6.9 %convolution_convert_fusion.1 = bf16[512,1536]{1,0:T(8,128)(2,1)S(1)} fusion(bf16[512,2048]{1,0:T(8,128)(2,1)} %collective-permute-done, bf16[1536,2048]{1,0:T(8,128)(2,1)} %bitcast.66), kind=kOutput, calls=%fused_computation.6 | convolution fusion | flops 3222011904 | bytes 9961472 | tf_op jit(solution)/shard_map/dot_general | solution.py:258
  65.7 3.6 all-to-all-start.1
  69.6 19.8 %all-to-all-done.1.refs_1_.refs_3_ = bf16[4,512,384]{2,1,0:T(8,128)(2,1)S(1)} async-done(((bf16[4,512,384]{2,1,0:T(8,128)(2,1)}), bf16[4,512,384]{2,1,0:T(8,128)(2,1)S(1)}, u32[]{:S(2)}, u32[]{:S(2)}) %all-to-all-start.1) | async-done | bytes 1572896 | tf_op jit(solution)/shard_map/all_to_all | solution.py:264
  90.5 22.7 %attend_fwd.2 = (bf16[4,256,1024]{2,1,0:T(8,128)(2,1)}, f32[8,4,512]{2,1,0:T(4,128)}) custom-call(bf16[4,512,384]{2,1,0:T(8,128)(2,1)} %all_to_all.30.refs_0_.refs_2_, bf16[4,512,384]{2,1,0:T(8,128)(2,1)} %copy-done.7, bf16[4,512,384]{2,1,0:T(8,128)(2,1)} %all_to_all.30.refs_0_.refs_2_, bf16[4,512,384]{2,1,0:T(8,128)(2,1)} %copy-done.7), custom_call_target="tpu_custom_call" | custom-call | flops 10737418240 | bytes 2097152 | tf_op jit(solution)/shard_map/attend_fwd/pallas_call | solution.py:178
  113.2 8.0 %convolution_convert_fusion.3 = bf16[1024,1024]{0,1:T(8,128)(2,1)S(1)} fusion(bf16[1024,2048]{1,0:T(8,128)(2,1)} %all-gather.4.cloned.1.call-done, bf16[1024,2048]{1,0:T(8,128)(2,1)} %bitcast.91), kind=kOutput, calls=%fused_computation.13 | convolution fusion | flops 4296015872 | bytes 10485760 | tf_op jit(solution)/shard_map/dot_general | solution.py:258
  129.6 56.2 %attend_fwd.3 = (bf16[4,256,1024]{2,1,0:T(8,128)(2,1)}, f32[8,4,512]{2,1,0:T(4,128)}) custom-call(bf16[4,512,384]{2,1,0:T(8,128)(2,1)} %all_to_all.30.refs_0_.refs_2_, bf16[4,512,384]{2,1,0:T(8,128)(2,1)} %copy-done.7, bf16[4,512,384]{2,1,0:T(8,128)(2,1)} %all_to_all.30.refs_0_.refs_2_, ...), custom_call_target="tpu_custom_call", output_to_operand_aliasing={{0}: (4, {}), {1}: (5, {})} | custom-call | flops 27917287424 | bytes 2097152 | tf_op jit(solution)/shard_map/attend_fwd/pallas_call | solution.py:178
  187.0 3.7 all-to-all-start.2
  191.4 47.4 %all-to-all-done.2 = bf16[4,1024,256]{2,1,0:T(8,128)(2,1)S(1)} async-done(((bf16[4,1024,256]{2,1,0:T(8,128)(2,1)}), bf16[4,1024,256]{2,1,0:T(8,128)(2,1)S(1)}, u32[]{:S(2)}, u32[]{:S(2)}) %all-to-all-start.2) | async-done | bytes 2097184 | tf_op jit(solution)/shard_map/all_to_all | solution.py:264
  240.1 3.8 all-to-all-start.3
  243.9 93.7 %attend_bwd.2 = (bf16[4,384,512]{2,1,0:T(8,128)(2,1)}, f32[4,512,128]{2,1,0:T(8,128)}) custom-call(bf16[4,512,384]{2,1,0:T(8,128)(2,1)} %all_to_all.30.refs_0_.refs_2_, bf16[4,512,384]{2,1,0:T(8,128)(2,1)} %copy-done.7, bf16[4,512,384]{2,1,0:T(8,128)(2,1)} %all_to_all.30.refs_0_.refs_2_, bf16[4,512,384]{2,1,0:T(8,128)(2,1)} %copy-done.7, ...), custom_call_target="tpu_custom_call" | custom-call | flops 69793218560 | bytes 4194304 | tf_op jit(solution)/shard_map/attend_bwd/pallas_call | solution.py:209
  337.6 39.0 %attend_bwd.3 = bf16[4,384,512]{2,1,0:T(8,128)(2,1)} custom-call(bf16[4,512,384]{2,1,0:T(8,128)(2,1)} %all_to_all.30.refs_0_.refs_2_, bf16[4,512,384]{2,1,0:T(8,128)(2,1)} %copy-done.7, bf16[4,512,384]{2,1,0:T(8,128)(2,1)} %all_to_all.30.refs_0_.refs_2_, bf16[4,512,384]{2,1,0:T(8,128)(2,1)} %copy-done.7, bf16[8,512,256]{2,1,0:T(8,128)(2,1)} %bitcast.78, ...), custom_call_target="tpu_custom_call" | custom-call | flops 26843545600 | bytes 4194304 | tf_op jit(solution)/shard_map/attend_bwd/pallas_call | solution.py:209
  381.6 20.0 %all-to-all-done.4 = bf16[4,384,512]{2,1,0:T(8,128)(2,1)S(1)} async-done(((bf16[4,384,512]{2,1,0:T(8,128)(2,1)}), bf16[4,384,512]{2,1,0:T(8,128)(2,1)S(1)}, u32[]{:S(2)}, u32[]{:S(2)}) %all-to-all-start.4) | async-done | bytes 1572896 | tf_op jit(solution)/shard_map/all_to_all | solution.py:264
  401.6 4.0 all-to-all-start.5
  405.6 7.1 %fusion.3 = f32[512,2048]{1,0:T(8,128)} fusion(bf16[1024,2048]{1,0:T(8,128)(2,1)} %bitcast.93, bf16[1024,1024]{1,0:T(8,128)(2,1)} %bitcast.73, s32[]{:T(128)S(6)} %select_n.26), kind=kOutput, calls=%fused_computation.16 | convolution fusion | flops 2147483648 | bytes 9437188 | tf_op jit(solution)/shard_map/dot_general | solution.py:258
  415.3 6.0 %convolution_convert_fusion = bf16[1024,2048]{1,0:T(8,128)(2,1)} fusion(bf16[1024,1024]{1,0:T(8,128)(2,1)S(1)} %bitcast.75, bf16[1024,2048]{1,0:T(8,128)(2,1)S(1)} %copy-done.10), kind=kOutput, calls=%fused_computation.5 | convolution fusion | flops 4297064448 | bytes 10485760 | tf_op jit(solution)/shard_map/dot_general | solution.py:258
  421.3 4.3 all-to-all-done.5
  437.0 5.2 %fusion.8 = f32[512,2048,1]{1,0,2:T(8,128)} fusion(bf16[4,384,512]{2,1,0:T(8,128)(2,1)S(1)} %get-tuple-element.49, bf16[4,384,2048]{2,1,0:T(8,128)(2,1)S(1)} %bitcast.69), kind=kOutput, calls=%fused_computation.24 | convolution fusion | flops 3221225472 | bytes 12058624 | tf_op jit(solution)/shard_map/dot_general | solution.py:258
  446.8 6.0 %multiply_convert_fusion = bf16[1024,2048]{1,0:T(8,128)(2,1)} fusion(f32[1024,2048]{1,0:T(8,128)S(1)} %fusion.9, bf16[1024,512]{1,0:T(8,128)(2,1)S(1)} %bitcast.84, bf16[512,2048]{1,0:T(8,128)(2,1)} %collective-permute-done), kind=kOutput, calls=%fused_computation | convolution fusion | flops 2153775104 | bytes 15728640 | tf_op jit(solution)/shard_map/dot_general | solution.py:258
  452.8 7.5 %add_convert_fusion = bf16[512,2048]{1,0:T(8,128)(2,1)} fusion(f32[512,2048]{1,0:T(8,128)} %fusion.3, bf16[1024,512]{1,0:T(8,128)(2,1)} %collective-permute-done.3, bf16[1024,2048]{1,0:T(8,128)(2,1)} %all-gather.6.cloned.1.call-done), kind=kOutput, calls=%fused_computation.4 | convolution fusion | flops 2149580800 | bytes 11534336 | tf_op jit(solution)/shard_map/dot_general | solution.py:258
  460.3 12.9 %collective-permute-done.4 = bf16[4,384,512]{2,1,0:T(8,128)(2,1)S(1)} collective-permute-done((bf16[4,384,512]{2,1,0:T(8,128)(2,1)}, bf16[4,384,512]{2,1,0:T(8,128)(2,1)S(1)}, u32[]{:S(2)}, u32[]{:S(2)}) %collective-permute-start.4) | collective-permute-done | bytes 1572896 | tf_op jit(solution)/shard_map/ppermute | solution.py:261
  473.2 8.1 %fusion = bf16[512,2048]{1,0:T(8,128)(2,1)} fusion(f32[512,2048,1]{1,0,2:T(8,128)} %fusion.8, bf16[1536,512]{1,0:T(8,128)(2,1)S(1)} %bitcast.76, bf16[1536,2048]{1,0:T(8,128)(2,1)} %all-gather.8.cloned.1.call-done), kind=kOutput, calls=%fused_computation.3 | convolution fusion | flops 3223322624 | bytes 14155776 | tf_op jit(solution)/shard_map/dot_general | solution.py:258
  (64 shorter events, 49.0 us)
Async XLA Ops:
  7.2 6.0 %copy-start.8 = (bf16[2048,4,64]{0,2,1:T(8,128)(2,1)S(1)}, bf16[2048,4,64]{0,2,1:T(8,128)(2,1)}, u32[]{:S(2)}) copy-start(bf16[2048,4,64]{0,2,1:T(8,128)(2,1)} %param.9) | copy-start | bytes 3145732
  7.2 6.0 %copy-start.9 = (bf16[2048,4,64]{0,2,1:T(8,128)(2,1)S(1)}, bf16[2048,4,64]{0,2,1:T(8,128)(2,1)}, u32[]{:S(2)}) copy-start(bf16[2048,4,64]{0,2,1:T(8,128)(2,1)} %param.8) | copy-start | bytes 3145732
  7.2 106.0 %all-gather.4.cloned.1.call-start = ((), (), s32[]{:S(2)}) async-start(), calls=%async_computation.6 | async-start | bytes 6291456 | tf_op jit(solution)/shard_map/all_gather | solution.py:283
  7.2 49.3 %collective-permute-start = (bf16[512,2048]{1,0:T(8,128)(2,1)}, bf16[512,2048]{1,0:T(8,128)(2,1)}, u32[]{:S(2)}, u32[]{:S(2)}) collective-permute-start(bf16[512,2048]{1,0:T(8,128)(2,1)} %param.6), channel_id=1, source_target_pairs={{0,4},{4,0},{1,5},{5,1},{2,6},{6,2},{3,7},{7,3}} | collective-permute-start | bytes 6291464 | tf_op jit(solution)/shard_map/ppermute | solution.py:261
  13.2 4.7 copy-start.1
  17.8 3.5 copy-start
  65.7 23.6 %all-to-all-start.1 = ((bf16[4,512,384]{2,1,0:T(8,128)(2,1)}), bf16[4,512,384]{2,1,0:T(8,128)(2,1)S(1)}, u32[]{:S(2)}, u32[]{:S(2)}) async-start(bf16[4,512,384]{2,1,0:T(8,128)(2,1)} %bitcast.9), calls=%async_computation.1 | async-start | bytes 3145728 | tf_op jit(solution)/shard_map/all_to_all | solution.py:264
  69.3 383.5 %all-gather.6.cloned.1.call-start = ((), (), s32[]{:S(2)}) async-start(), calls=%async_computation.7 | async-start | bytes 5242880 | tf_op jit(solution)/shard_map/all_gather | solution.py:277
  125.2 60.6 %collective-permute-start.1 = (bf16[384,2048]{1,0:T(8,128)(2,1)S(1)}, bf16[384,2048]{1,0:T(8,128)(2,1)S(1)}, u32[]{:S(2)}, u32[]{:S(2)}) collective-permute-start(bf16[384,2048]{1,0:T(8,128)(2,1)S(1)} %constant_dynamic-slice_fusion.2), channel_id=1, source_target_pairs={{0,4},{4,0},{1,5},{5,1},{2,6},{6,2},{3,7},{7,3}} | collective-permute-start | bytes 4718600 | tf_op jit(solution)/shard_map/ppermute | solution.py:261
  129.3 56.5 %collective-permute-start.2 = (bf16[256,2048]{1,0:T(8,128)(2,1)}, bf16[256,2048]{1,0:T(8,128)(2,1)}, u32[]{:S(2)}, u32[]{:S(2)}) collective-permute-start(bf16[256,2048]{1,0:T(8,128)(2,1)} %constant_dynamic-slice_fusion.1), channel_id=1, source_target_pairs={{0,4},{4,0},{1,5},{5,1},{2,6},{6,2},{3,7},{7,3}} | collective-permute-start | bytes 3145736 | tf_op jit(solution)/shard_map/ppermute | solution.py:261
  187.0 51.8 %all-to-all-start.2 = ((bf16[4,1024,256]{2,1,0:T(8,128)(2,1)}), bf16[4,1024,256]{2,1,0:T(8,128)(2,1)S(1)}, u32[]{:S(2)}, u32[]{:S(2)}) async-start(bf16[4,1024,256]{2,1,0:T(8,128)(2,1)} %bitcast.12), calls=%async_computation.2 | async-start | bytes 4194304 | tf_op jit(solution)/shard_map/all_to_all | solution.py:264
  190.7 282.5 %all-gather.8.cloned.1.call-start = ((), (), s32[]{:S(2)}) async-start(), calls=%async_computation.8 | async-start | bytes 7864320 | tf_op jit(solution)/shard_map/all_gather | solution.py:277
  238.8 1.3 copy-start.5
  240.1 136.5 %all-to-all-start.3 = ((bf16[4,256,1024]{2,1,0:T(8,128)(2,1)}), bf16[4,256,1024]{2,1,0:T(8,128)(2,1)S(1)}, u32[]{:S(2)}, u32[]{:S(2)}) async-start(bf16[4,256,1024]{2,1,0:T(8,128)(2,1)} %get-tuple-element.40.refs_5_), calls=%async_computation.3 | async-start | bytes 4194304 | tf_op jit(solution)/shard_map/all_to_all | solution.py:264
  376.7 1.3 copy-start.3
  378.0 23.6 %all-to-all-start.4 = ((bf16[4,384,512]{2,1,0:T(8,128)(2,1)}), bf16[4,384,512]{2,1,0:T(8,128)(2,1)S(1)}, u32[]{:S(2)}, u32[]{:S(2)}) async-start(bf16[4,384,512]{2,1,0:T(8,128)(2,1)} %attend_bwd.3), calls=%async_computation.4 | async-start | bytes 3145728 | tf_op jit(solution)/shard_map/all_to_all | solution.py:264
  401.6 24.0 %all-to-all-start.5 = ((bf16[4,384,512]{2,1,0:T(8,128)(2,1)}), bf16[4,384,512]{2,1,0:T(8,128)(2,1)S(1)}, u32[]{:S(2)}, u32[]{:S(2)}) async-start(bf16[4,384,512]{2,1,0:T(8,128)(2,1)} %get-tuple-element.46), calls=%async_computation.5 | async-start | bytes 3145728 | tf_op jit(solution)/shard_map/all_to_all | solution.py:264
  405.6 7.1 %copy-start.4 = (bf16[4,256,1024]{2,1,0:T(8,128)(2,1)S(1)}, bf16[4,256,1024]{2,1,0:T(8,128)(2,1)}, u32[]{:S(2)}) copy-start(bf16[4,256,1024]{2,1,0:T(8,128)(2,1)} %copy-done.3) | copy-start | bytes 6291460
  405.6 9.6 %copy-start.10 = (bf16[1024,2048]{1,0:T(8,128)(2,1)S(1)}, bf16[1024,2048]{1,0:T(8,128)(2,1)}, u32[]{:S(2)}) copy-start(bf16[1024,2048]{1,0:T(8,128)(2,1)} %all-gather.4.cloned.1.call-done) | copy-start | bytes 12582916
  413.8 39.1 %collective-permute-start.3 = (bf16[1024,512]{1,0:T(8,128)(2,1)}, bf16[1024,512]{1,0:T(8,128)(2,1)}, u32[]{:S(2)}, u32[]{:S(2)}) collective-permute-start(bf16[1024,512]{1,0:T(8,128)(2,1)} %constant_dynamic-slice_fusion), channel_id=1, source_target_pairs={{0,4},{4,0},{1,5},{5,1},{2,6},{6,2},{3,7},{7,3}} | collective-permute-start | bytes 3145736 | tf_op jit(solution)/shard_map/ppermute | solution.py:261
  427.0 2.7 copy-start.2
  427.0 46.2 %collective-permute-start.4 = (bf16[4,384,512]{2,1,0:T(8,128)(2,1)}, bf16[4,384,512]{2,1,0:T(8,128)(2,1)S(1)}, u32[]{:S(2)}, u32[]{:S(2)}) collective-permute-start(bf16[4,384,512]{2,1,0:T(8,128)(2,1)} %get-tuple-element.48), channel_id=1, source_target_pairs={{0,4},{4,0},{1,5},{5,1},{2,6},{6,2},{3,7},{7,3}} | collective-permute-start | bytes 4718600 | tf_op jit(solution)/shard_map/ppermute | solution.py:261
  431.1 5.8 %slice-start = ((s8[6291456]{0:T(1024)(128)(4,1)}), s8[4194304]{0:T(1024)(128)(4,1)S(1)}, s32[]{:S(2)}) async-start(s8[6291456]{0:T(1024)(128)(4,1)} %bitcast.68), calls=%async_computation.9 | async-start | bytes 8388608
  434.6 2.4 slice-start.1
  (2 other events, 2.3 us)
Sparse Core Ops, SparseCore 0:
  56.7 55.1 all-gather.3
  186.0 54.3 all-gather.5
  241.9 62.9 all-gather.7

commit v3 on v2

--- a/solution.py
+++ b/solution.py
@@ -16,6 +16,8 @@
 F32 = jnp.float32
 BF16 = jnp.bfloat16
 VMEM_LIMIT = 60 * 1024 * 1024
+FWD_SPLIT, FWD_AHEAD, FWD_BEHIND = 256, 2, 1
+BWD_SPLIT, BWD_AHEAD, BWD_BEHIND = 512, 1, 0
 
 
 def half_of(pos_blk, n_blk):
@@ -30,8 +32,8 @@
     return 2 * shard_of(pos_blk, n_blk) + half_of(pos_blk, n_blk)
 
 
-def keep_mask(shape):
-    return lax.broadcasted_iota(jnp.int32, shape, 0) <= lax.broadcasted_iota(jnp.int32, shape, 1)
+def keep_mask(shape, col=0):
+    return lax.broadcasted_iota(jnp.int32, shape, 0) <= lax.broadcasted_iota(jnp.int32, shape, 1) + col
 
 
 def load_keys(n_blk, own_ref, other_ref, kv_s, kvt_s):
@@ -51,6 +53,7 @@
     q_own, q_other, kv_own, kv_other = refs[:4]
     o_ref, lse_ref, kv_s, kvt_s, rq_s, acc_s, m_s, l_s = refs[-8:]
     pos = first + pl.program_id(0)
+    blk = q_own.shape[0]
 
     @pl.when(pl.program_id(0) == 0)
     def _():
@@ -64,22 +67,39 @@
     def tile(j, diag):
         kv_j = kv_s[j]
         v_t = kvt_s[j, dim:, :]
-        for h in range(groups):
-            s = jnp.dot(kv_j, rq_s[h], preferred_element_type=F32)
+        chains = [(h, slice(c, c + FWD_SPLIT)) for h in range(groups) for c in range(0, blk, FWD_SPLIT)]
+
+        def scores(h, cs):
+            return jnp.dot(kv_j, rq_s[h, :, cs], preferred_element_type=F32)
+
+        def output(h, cs, p, alpha):
+            o = jnp.dot(v_t, p, preferred_element_type=F32)
+            acc_s[h, :, cs] = o if alpha is None else acc_s[h, :, cs] * alpha + o
+
+        ahead = [scores(*chain) for chain in chains[:FWD_AHEAD]]
+        behind = []
+        for i, (h, cs) in enumerate(chains):
+            if i + FWD_AHEAD < len(chains):
+                ahead.append(scores(*chains[i + FWD_AHEAD]))
+            s = ahead[i]
             if diag:
-                s = jnp.where(keep_mask(s.shape), s, -jnp.inf)
+                s = jnp.where(keep_mask(s.shape, cs.start), s, -jnp.inf)
                 m_new = jnp.max(s, axis=0, keepdims=True)
                 p = jnp.exp(s - m_new)
-                l_s[h] = jnp.sum(p, axis=0, keepdims=True)
-                acc_s[h] = jnp.dot(v_t, p.astype(BF16), preferred_element_type=F32)
+                alpha = None
+                l_s[h, :, cs] = jnp.sum(p, axis=0, keepdims=True)
             else:
-                m_old = m_s[h]
+                m_old = m_s[h, :, cs]
                 m_new = jnp.maximum(m_old, jnp.max(s, axis=0, keepdims=True))
                 p = jnp.exp(s - m_new)
                 alpha = jnp.exp(m_old - m_new)
-                l_s[h] = l_s[h] * alpha + jnp.sum(p, axis=0, keepdims=True)
-                acc_s[h] = acc_s[h] * alpha + jnp.dot(v_t, p.astype(BF16), preferred_element_type=F32)
-            m_s[h] = m_new
+                l_s[h, :, cs] = l_s[h, :, cs] * alpha + jnp.sum(p, axis=0, keepdims=True)
+            m_s[h, :, cs] = m_new
+            behind.append((h, cs, p.astype(BF16), alpha))
+            if len(behind) > FWD_BEHIND:
+                output(*behind.pop(0))
+        for item in behind:
+            output(*item)
 
     tile(pos, True)
 
@@ -96,7 +116,7 @@
     q_own, q_other, kv_own, kv_other, do_ref, o_ref, lse_ref = refs[:7]
     upper = first > 0
     g_ref = refs[7 if upper else 8]
-    kv_s, kvt_s, rq_s, rd_s, rqk_s, rdo_s, dot_s, dqt_s, dkv_s = refs[-9:]
+    kv_s, kvt_s, rq_s, rd_s, dot_s, dqt_s, dkv_s = refs[-7:]
     step = pl.program_id(0)
     pos = first + step
     blk = do_ref.shape[0]
@@ -113,31 +133,47 @@
     do = do_ref[...]
     q_t = q.T
     do_t = do.T
-    zero = jnp.zeros((blk, dim), BF16)
     for h in range(groups):
         rows = slice(h * dim, (h + 1) * dim)
         rq_s[h, :dim, :] = q_t[rows, :]
         rd_s[h, dim:, :] = do_t[rows, :]
-        rqk_s[h] = jnp.concatenate([q[:, rows], zero], axis=1)
-        rdo_s[h] = jnp.concatenate([zero, do[:, rows]], axis=1)
         dot_s[h] = jnp.sum(do_t[rows, :].astype(F32) * o_ref[rows, :].astype(F32), axis=0, keepdims=True)
     dqt_s[...] = jnp.zeros_like(dqt_s)
 
     def tile(j, diag):
         kv_j = kv_s[j]
         k_t = kvt_s[j, :dim, :]
-        total = dkv_s[j]
-        for h in range(groups):
-            s = jnp.dot(kv_j, rq_s[h], preferred_element_type=F32)
-            p = jnp.exp(s - lse_ref[h:h + 1, :])
+        dk = dkv_s[j, :dim, :]
+        dv = dkv_s[j, dim:, :]
+        chains = [(h, slice(c, c + BWD_SPLIT)) for h in range(groups) for c in range(0, blk, BWD_SPLIT)]
+
+        def scores(h, cs):
+            return (jnp.dot(kv_j, rq_s[h, :, cs], preferred_element_type=F32),
+                    jnp.dot(kv_j, rd_s[h, :, cs], preferred_element_type=F32))
+
+        def outputs(dk, dv, h, cs, p, ds):
+            dqt_s[h, :, cs] += jnp.dot(k_t, ds, preferred_element_type=F32)
+            dk += lax.dot_general(rq_s[h, :dim, cs], ds, NT, preferred_element_type=F32)
+            dv += lax.dot_general(rd_s[h, dim:, cs], p, NT, preferred_element_type=F32)
+            return dk, dv
+
+        ahead = [scores(*chain) for chain in chains[:BWD_AHEAD]]
+        behind = []
+        for i, (h, cs) in enumerate(chains):
+            if i + BWD_AHEAD < len(chains):
+                ahead.append(scores(*chains[i + BWD_AHEAD]))
+            s, dp = ahead[i]
+            p = jnp.exp(s - lse_ref[h:h + 1, cs])
             if diag:
-                p = jnp.where(keep_mask(s.shape), p, 0.0)
-            dp = jnp.dot(kv_j, rd_s[h], preferred_element_type=F32)
-            ds = (p * (dp - dot_s[h])).astype(BF16)
-            dqt_s[h] += jnp.dot(k_t, ds, preferred_element_type=F32)
-            total += jnp.dot(ds, rqk_s[h], preferred_element_type=F32)
-            total += jnp.dot(p.astype(BF16), rdo_s[h], preferred_element_type=F32)
-        dkv_s[j] = total
+                p = jnp.where(keep_mask(s.shape, cs.start), p, 0.0)
+            ds = (p * (dp - dot_s[h, :, cs])).astype(BF16)
+            behind.append((h, cs, p.astype(BF16), ds))
+            if len(behind) > BWD_BEHIND:
+                dk, dv = outputs(dk, dv, *behind.pop(0))
+        for item in behind:
+            dk, dv = outputs(dk, dv, *item)
+        dkv_s[j, :dim, :] = dk
+        dkv_s[j, dim:, :] = dv
 
     tile(pos, True)
 
@@ -153,7 +189,7 @@
     def _():
         for b in range(first, first + count):
             s = b if b < n_blk // 2 else n_blk - 1 - b
-            g_ref[s, cols:, :] = dkv_s[b].astype(BF16).T
+            g_ref[s, cols:, :] = dkv_s[b].astype(BF16)
         if upper:
             refs[8][...] = dkv_s[:first]
 
@@ -202,10 +238,10 @@
     cols = groups * dim
     elems = blk * blk * groups * sum(range(first + 1, first + count + 1))
     feats = cols + 2 * dim
-    keys_shape = (n_blk, blk, 2 * dim) if first else (n_half, blk, 2 * dim)
-    whole = pl.BlockSpec((n_half, blk, 2 * dim), lambda i: (0, 0, 0))
+    keys_shape = (n_blk if first else n_half, 2 * dim, blk)
+    whole = pl.BlockSpec((n_half, 2 * dim, blk), lambda i: (0, 0, 0))
     out_specs = [pl.BlockSpec((n_half, feats, blk), lambda i: (0, 0, 0))] + [whole] * (first > 0)
-    out_shape = [jax.ShapeDtypeStruct((n_half, feats, blk), BF16)] + [jax.ShapeDtypeStruct((n_half, blk, 2 * dim), F32)] * (first > 0)
+    out_shape = [jax.ShapeDtypeStruct((n_half, feats, blk), BF16)] + [jax.ShapeDtypeStruct((n_half, 2 * dim, blk), F32)] * (first > 0)
     return pl.pallas_call(
         lambda *refs: bwd_kernel(n_blk, groups, dim, first, count, *refs),
         grid=(count,),
@@ -220,8 +256,6 @@
             pltpu.VMEM((n_blk, 2 * dim, blk), BF16),
             pltpu.VMEM((groups, 2 * dim, blk), BF16),
             pltpu.VMEM((groups, 2 * dim, blk), BF16),
-            pltpu.VMEM((groups, blk, 2 * dim), BF16),
-            pltpu.VMEM((groups, blk, 2 * dim), BF16),
             pltpu.VMEM((groups, 1, blk), F32),
             pltpu.VMEM((groups, dim, blk), F32),
             pltpu.VMEM(keys_shape, F32),

time: 496 us -> 471 us (0.950)
  Pallas kernels: 212 us -> 174 us
  waiting for transfers between devices: 116 us -> 131 us
    pallas_call x2, Pallas kernels: 133 us -> 112 us  [attend_grad(): pl.pallas_call(lambda *refs: bwd_kernel(n_blk, groups, dim, first, count,...]
    pallas_call x2, Pallas kernels: 78.9 us -> 61.9 us  [attend(): pl.pallas_call(lambda *refs: fwd_kernel(n_blk, groups, dim, first, *refs)...]
    ppermute x5, waiting for transfers between devices: 24 us -> 35.1 us  [exchange(): return lax.ppermute(a, 'tp', swap)]
  transfers between devices with their start and end apart: 13 -> 13, of which waited for: 6 -> 8; matrix products, arithmetic and copies ran while one was open for 14% -> 15% of each run, Pallas kernels for 43% -> 38%
where the time goes in v3:
time: 471 us; the launch traced here: 464 us
  Pallas kernels  174 us (37%)
  waiting for transfers between devices  131 us (28%)
  matrix products  68.8 us (15%)
  starting transfers between devices  25.6 us (5%)
  blocking collectives  23.3 us (5%)
  local copies, waits for them, and re-layouts  18 us (4%)
  between operations  14.3 us (3%)
  other arithmetic  8.54 us (2%)
    pallas_call x2, Pallas kernels, attend_grad(): pl.pallas_call(lambda *refs: bwd_kernel(n_blk, groups, dim, first, count,...  112 us
    all_to_all x5, waiting for transfers between devices, switch(): return lax.all_to_all(a, 'cp', split_axis=0, concat_axis=0, tiled=True)  91.8 us
    dot_general x14, matrix products, mm(): return lax.dot_general(a, b, dims, preferred_element_type=F32)  68.8 us
    pallas_call x2, Pallas kernels, attend(): pl.pallas_call(lambda *refs: fwd_kernel(n_blk, groups, dim, first, *refs)...  61.9 us
    ppermute x5, waiting for transfers between devices, exchange(): return lax.ppermute(a, 'tp', swap)  35.1 us
    all_to_all x1, blocking collectives, switch(): return lax.all_to_all(a, 'cp', split_axis=0, concat_axis=0, tiled=True)  23.3 us
    all_to_all x5, starting transfers between devices, switch(): return lax.all_to_all(a, 'cp', split_axis=0, concat_axis=0, tiled=True)  18.4 us
  transfers between devices with their start and end apart: 13, of which 8 were waited for; matrix products, arithmetic and copies ran while one was open for 15% of the time, Pallas kernels for 38%

profile of v3, /device:TPU:0, one launch (start us, length us, event | category | flops | bytes accessed | tf_op | source)
XLA Modules:
  0.0 463.6 jit_solution(11466703747797744525)
XLA Ops:
  13.2 4.6 %pad_maximum_fusion = bf16[4,384,2048]{2,1,0:T(8,128)(2,1)S(1)} fusion(bf16[4,64,2048]{2,1,0:T(8,128)(2,1)S(1)} %bitcast.81, bf16[4,64,2048]{2,1,0:T(8,128)(2,1)S(1)} %bitcast.82, bf16[4,256,2048]{2,1,0:T(8,128)(2,1)S(1)} %bitcast.70), kind=kLoop, calls=%fused_computation.1 | loop fusion | flops 18874368 | bytes 12582912 | tf_op jit(solution)/shard_map/concatenate | solution.py:287
  22.2 23.3 %all_to_all.30.refs_0_.refs_2_ = bf16[4,512,384]{2,1,0:T(8,128)(2,1)} all-to-all(bf16[4,512,384]{2,1,0:T(8,128)(2,1)S(1)} %bitcast.71), channel_id=1, replica_groups=mesh['dp'=1,'tp'=2,'cp'=4] {'cp'}, dimensions={0} | all-to-all | bytes 3145728 | tf_op jit(solution)/shard_map/all_to_all | solution.py:298
  45.5 11.1 %collective-permute-done = bf16[512,2048]{1,0:T(8,128)(2,1)} collective-permute-done((bf16[512,2048]{1,0:T(8,128)(2,1)}, bf16[512,2048]{1,0:T(8,128)(2,1)}, u32[]{:S(2)}, u32[]{:S(2)}) %collective-permute-start) | collective-permute-done | bytes 2097184 | tf_op jit(solution)/shard_map/ppermute | solution.py:295
  56.6 6.9 %convolution_convert_fusion.1 = bf16[512,1536]{1,0:T(8,128)(2,1)S(1)} fusion(bf16[512,2048]{1,0:T(8,128)(2,1)} %collective-permute-done, bf16[1536,2048]{1,0:T(8,128)(2,1)} %bitcast.66), kind=kOutput, calls=%fused_computation.6 | convolution fusion | flops 3222011904 | bytes 9961472 | tf_op jit(solution)/shard_map/dot_general | solution.py:292
  69.9 19.4 %all-to-all-done.1.refs_1_.refs_3_ = bf16[4,512,384]{2,1,0:T(8,128)(2,1)S(1)} async-done(((bf16[4,512,384]{2,1,0:T(8,128)(2,1)}), bf16[4,512,384]{2,1,0:T(8,128)(2,1)S(1)}, u32[]{:S(2)}, u32[]{:S(2)}) %all-to-all-start.1) | async-done | bytes 1572896 | tf_op jit(solution)/shard_map/all_to_all | solution.py:298
  90.5 17.9 %attend_fwd.2 = (bf16[4,256,1024]{2,1,0:T(8,128)(2,1)}, f32[8,4,512]{2,1,0:T(4,128)}) custom-call(bf16[4,512,384]{2,1,0:T(8,128)(2,1)} %all_to_all.30.refs_0_.refs_2_, bf16[4,512,384]{2,1,0:T(8,128)(2,1)} %copy-done.7, bf16[4,512,384]{2,1,0:T(8,128)(2,1)} %all_to_all.30.refs_0_.refs_2_, bf16[4,512,384]{2,1,0:T(8,128)(2,1)} %copy-done.7), custom_call_target="tpu_custom_call" | custom-call | flops 10737418240 | bytes 2097152 | tf_op jit(solution)/shard_map/attend_fwd/pallas_call | solution.py:214
  111.9 8.0 %convolution_convert_fusion.3 = bf16[1024,1024]{0,1:T(8,128)(2,1)S(1)} fusion(bf16[1024,2048]{1,0:T(8,128)(2,1)} %all-gather.4.cloned.1.call-done, bf16[1024,2048]{1,0:T(8,128)(2,1)} %bitcast.91), kind=kOutput, calls=%fused_computation.13 | convolution fusion | flops 4296015872 | bytes 10485760 | tf_op jit(solution)/shard_map/dot_general | solution.py:292
  128.3 43.9 %attend_fwd.3 = (bf16[4,256,1024]{2,1,0:T(8,128)(2,1)}, f32[8,4,512]{2,1,0:T(4,128)}) custom-call(bf16[4,512,384]{2,1,0:T(8,128)(2,1)} %all_to_all.30.refs_0_.refs_2_, bf16[4,512,384]{2,1,0:T(8,128)(2,1)} %copy-done.7, bf16[4,512,384]{2,1,0:T(8,128)(2,1)} %all_to_all.30.refs_0_.refs_2_, ...), custom_call_target="tpu_custom_call", output_to_operand_aliasing={{0}: (4, {}), {1}: (5, {})} | custom-call | flops 27917287424 | bytes 2097152 | tf_op jit(solution)/shard_map/attend_fwd/pallas_call | solution.py:214
  172.2 10.3 %collective-permute-done.2 = bf16[256,2048]{1,0:T(8,128)(2,1)} collective-permute-done((bf16[256,2048]{1,0:T(8,128)(2,1)}, bf16[256,2048]{1,0:T(8,128)(2,1)}, u32[]{:S(2)}, u32[]{:S(2)}) %collective-permute-start.2) | collective-permute-done | bytes 1048608 | tf_op jit(solution)/shard_map/ppermute | solution.py:295
  183.7 3.7 all-to-all-start.2
  188.1 47.1 %all-to-all-done.2 = bf16[4,1024,256]{2,1,0:T(8,128)(2,1)S(1)} async-done(((bf16[4,1024,256]{2,1,0:T(8,128)(2,1)}), bf16[4,1024,256]{2,1,0:T(8,128)(2,1)S(1)}, u32[]{:S(2)}, u32[]{:S(2)}) %all-to-all-start.2) | async-done | bytes 2097184 | tf_op jit(solution)/shard_map/all_to_all | solution.py:298
  236.5 3.8 all-to-all-start.3
  240.3 79.7 %attend_bwd.2 = (bf16[4,384,512]{2,1,0:T(8,128)(2,1)}, f32[4,128,512]{2,1,0:T(8,128)}) custom-call(bf16[4,512,384]{2,1,0:T(8,128)(2,1)} %all_to_all.30.refs_0_.refs_2_, bf16[4,512,384]{2,1,0:T(8,128)(2,1)} %copy-done.7, bf16[4,512,384]{2,1,0:T(8,128)(2,1)} %all_to_all.30.refs_0_.refs_2_, bf16[4,512,384]{2,1,0:T(8,128)(2,1)} %copy-done.7, ...), custom_call_target="tpu_custom_call" | custom-call | flops 69793218560 | bytes 4194304 | tf_op jit(solution)/shard_map/attend_bwd/pallas_call | solution.py:245
  320.1 32.4 %attend_bwd.3 = bf16[4,384,512]{2,1,0:T(8,128)(2,1)} custom-call(bf16[4,512,384]{2,1,0:T(8,128)(2,1)} %all_to_all.30.refs_0_.refs_2_, bf16[4,512,384]{2,1,0:T(8,128)(2,1)} %copy-done.7, bf16[4,512,384]{2,1,0:T(8,128)(2,1)} %all_to_all.30.refs_0_.refs_2_, bf16[4,512,384]{2,1,0:T(8,128)(2,1)} %copy-done.7, bf16[8,512,256]{2,1,0:T(8,128)(2,1)} %bitcast.78, ...), custom_call_target="tpu_custom_call" | custom-call | flops 26843545600 | bytes 4194304 | tf_op jit(solution)/shard_map/attend_bwd/pallas_call | solution.py:245
  357.4 20.0 %all-to-all-done.4 = bf16[4,384,512]{2,1,0:T(8,128)(2,1)S(1)} async-done(((bf16[4,384,512]{2,1,0:T(8,128)(2,1)}), bf16[4,384,512]{2,1,0:T(8,128)(2,1)S(1)}, u32[]{:S(2)}, u32[]{:S(2)}) %all-to-all-start.4) | async-done | bytes 1572896 | tf_op jit(solution)/shard_map/all_to_all | solution.py:298
  377.4 3.8 all-to-all-start.5
  381.2 7.1 %fusion.3 = f32[512,2048]{1,0:T(8,128)} fusion(bf16[1024,2048]{1,0:T(8,128)(2,1)} %bitcast.93, bf16[1024,1024]{1,0:T(8,128)(2,1)} %bitcast.73, s32[]{:T(128)S(6)} %select_n.26), kind=kOutput, calls=%fused_computation.16 | convolution fusion | flops 2147483648 | bytes 9437188 | tf_op jit(solution)/shard_map/dot_general | solution.py:292
  389.9 6.0 %convolution_convert_fusion = bf16[1024,2048]{1,0:T(8,128)(2,1)} fusion(bf16[1024,1024]{1,0:T(8,128)(2,1)S(1)} %bitcast.75, bf16[1024,2048]{1,0:T(8,128)(2,1)S(1)} %copy-done.10), kind=kOutput, calls=%fused_computation.5 | convolution fusion | flops 4297064448 | bytes 10485760 | tf_op jit(solution)/shard_map/dot_general | solution.py:292
  396.0 5.2 %all-to-all-done.5 = bf16[4,384,512]{2,1,0:T(8,128)(2,1)S(1)} async-done(((bf16[4,384,512]{2,1,0:T(8,128)(2,1)}), bf16[4,384,512]{2,1,0:T(8,128)(2,1)S(1)}, u32[]{:S(2)}, u32[]{:S(2)}) %all-to-all-start.5) | async-done | bytes 1572896 | tf_op jit(solution)/shard_map/all_to_all | solution.py:298
  411.7 5.3 %fusion.8 = f32[512,2048,1]{1,0,2:T(8,128)} fusion(bf16[4,384,512]{2,1,0:T(8,128)(2,1)S(1)} %get-tuple-element.49, bf16[4,384,2048]{2,1,0:T(8,128)(2,1)S(1)} %bitcast.69), kind=kOutput, calls=%fused_computation.24 | convolution fusion | flops 3221225472 | bytes 12058624 | tf_op jit(solution)/shard_map/dot_general | solution.py:292
  421.6 6.0 %multiply_convert_fusion = bf16[1024,2048]{1,0:T(8,128)(2,1)} fusion(f32[1024,2048]{1,0:T(8,128)S(1)} %fusion.9, bf16[1024,512]{1,0:T(8,128)(2,1)S(1)} %bitcast.84, bf16[512,2048]{1,0:T(8,128)(2,1)} %collective-permute-done), kind=kOutput, calls=%fused_computation | convolution fusion | flops 2153775104 | bytes 15728640 | tf_op jit(solution)/shard_map/dot_general | solution.py:292
  427.6 7.5 %add_convert_fusion = bf16[512,2048]{1,0:T(8,128)(2,1)} fusion(f32[512,2048]{1,0:T(8,128)} %fusion.3, bf16[1024,512]{1,0:T(8,128)(2,1)} %collective-permute-done.3, bf16[1024,2048]{1,0:T(8,128)(2,1)} %all-gather.6.cloned.1.call-done), kind=kOutput, calls=%fused_computation.4 | convolution fusion | flops 2149580800 | bytes 11534336 | tf_op jit(solution)/shard_map/dot_general | solution.py:292
  435.1 13.7 %collective-permute-done.4 = bf16[4,384,512]{2,1,0:T(8,128)(2,1)S(1)} collective-permute-done((bf16[4,384,512]{2,1,0:T(8,128)(2,1)}, bf16[4,384,512]{2,1,0:T(8,128)(2,1)S(1)}, u32[]{:S(2)}, u32[]{:S(2)}) %collective-permute-start.4) | collective-permute-done | bytes 1572896 | tf_op jit(solution)/shard_map/ppermute | solution.py:295
  448.8 8.1 %fusion = bf16[512,2048]{1,0:T(8,128)(2,1)} fusion(f32[512,2048,1]{1,0,2:T(8,128)} %fusion.8, bf16[1536,512]{1,0:T(8,128)(2,1)S(1)} %bitcast.76, bf16[1536,2048]{1,0:T(8,128)(2,1)} %all-gather.8.cloned.1.call-done), kind=kOutput, calls=%fused_computation.3 | convolution fusion | flops 3223322624 | bytes 14155776 | tf_op jit(solution)/shard_map/dot_general | solution.py:292
  (64 shorter events, 54.6 us)
Async XLA Ops:
  7.2 6.0 %copy-start.8 = (bf16[2048,4,64]{0,2,1:T(8,128)(2,1)S(1)}, bf16[2048,4,64]{0,2,1:T(8,128)(2,1)}, u32[]{:S(2)}) copy-start(bf16[2048,4,64]{0,2,1:T(8,128)(2,1)} %param.9) | copy-start | bytes 3145732
  7.2 6.0 %copy-start.9 = (bf16[2048,4,64]{0,2,1:T(8,128)(2,1)S(1)}, bf16[2048,4,64]{0,2,1:T(8,128)(2,1)}, u32[]{:S(2)}) copy-start(bf16[2048,4,64]{0,2,1:T(8,128)(2,1)} %param.8) | copy-start | bytes 3145732
  7.2 104.7 %all-gather.4.cloned.1.call-start = ((), (), s32[]{:S(2)}) async-start(), calls=%async_computation.6 | async-start | bytes 6291456 | tf_op jit(solution)/shard_map/all_gather | solution.py:317
  7.2 49.3 %collective-permute-start = (bf16[512,2048]{1,0:T(8,128)(2,1)}, bf16[512,2048]{1,0:T(8,128)(2,1)}, u32[]{:S(2)}, u32[]{:S(2)}) collective-permute-start(bf16[512,2048]{1,0:T(8,128)(2,1)} %param.6), channel_id=1, source_target_pairs={{0,4},{4,0},{1,5},{5,1},{2,6},{6,2},{3,7},{7,3}} | collective-permute-start | bytes 6291464 | tf_op jit(solution)/shard_map/ppermute | solution.py:295
  13.2 4.7 %copy-start.1 = (bf16[512,2048]{1,0:T(8,128)(2,1)S(1)}, bf16[512,2048]{1,0:T(8,128)(2,1)}, u32[]{:S(2)}) copy-start(bf16[512,2048]{1,0:T(8,128)(2,1)} %param.6) | copy-start | bytes 6291460
  17.8 3.5 copy-start
  65.7 23.6 %all-to-all-start.1 = ((bf16[4,512,384]{2,1,0:T(8,128)(2,1)}), bf16[4,512,384]{2,1,0:T(8,128)(2,1)S(1)}, u32[]{:S(2)}, u32[]{:S(2)}) async-start(bf16[4,512,384]{2,1,0:T(8,128)(2,1)} %bitcast.9), calls=%async_computation.1 | async-start | bytes 3145728 | tf_op jit(solution)/shard_map/all_to_all | solution.py:298
  69.3 358.3 %all-gather.6.cloned.1.call-start = ((), (), s32[]{:S(2)}) async-start(), calls=%async_computation.7 | async-start | bytes 5242880 | tf_op jit(solution)/shard_map/all_gather | solution.py:311
  123.9 58.6 %collective-permute-start.1 = (bf16[384,2048]{1,0:T(8,128)(2,1)S(1)}, bf16[384,2048]{1,0:T(8,128)(2,1)S(1)}, u32[]{:S(2)}, u32[]{:S(2)}) collective-permute-start(bf16[384,2048]{1,0:T(8,128)(2,1)S(1)} %constant_dynamic-slice_fusion.2), channel_id=1, source_target_pairs={{0,4},{4,0},{1,5},{5,1},{2,6},{6,2},{3,7},{7,3}} | collective-permute-start | bytes 4718600 | tf_op jit(solution)/shard_map/ppermute | solution.py:295
  126.6 55.9 %collective-permute-start.2 = (bf16[256,2048]{1,0:T(8,128)(2,1)}, bf16[256,2048]{1,0:T(8,128)(2,1)}, u32[]{:S(2)}, u32[]{:S(2)}) collective-permute-start(bf16[256,2048]{1,0:T(8,128)(2,1)} %constant_dynamic-slice_fusion.1), channel_id=1, source_target_pairs={{0,4},{4,0},{1,5},{5,1},{2,6},{6,2},{3,7},{7,3}} | collective-permute-start | bytes 3145736 | tf_op jit(solution)/shard_map/ppermute | solution.py:295
  183.7 51.5 %all-to-all-start.2 = ((bf16[4,1024,256]{2,1,0:T(8,128)(2,1)}), bf16[4,1024,256]{2,1,0:T(8,128)(2,1)S(1)}, u32[]{:S(2)}, u32[]{:S(2)}) async-start(bf16[4,1024,256]{2,1,0:T(8,128)(2,1)} %bitcast.12), calls=%async_computation.2 | async-start | bytes 4194304 | tf_op jit(solution)/shard_map/all_to_all | solution.py:298
  187.3 261.5 %all-gather.8.cloned.1.call-start = ((), (), s32[]{:S(2)}) async-start(), calls=%async_computation.8 | async-start | bytes 7864320 | tf_op jit(solution)/shard_map/all_gather | solution.py:311
  235.2 1.3 copy-start.5
  236.5 115.9 %all-to-all-start.3 = ((bf16[4,256,1024]{2,1,0:T(8,128)(2,1)}), bf16[4,256,1024]{2,1,0:T(8,128)(2,1)S(1)}, u32[]{:S(2)}, u32[]{:S(2)}) async-start(bf16[4,256,1024]{2,1,0:T(8,128)(2,1)} %get-tuple-element.40.refs_5_), calls=%async_computation.3 | async-start | bytes 4194304 | tf_op jit(solution)/shard_map/all_to_all | solution.py:298
  352.5 1.3 copy-start.3
  353.8 23.6 %all-to-all-start.4 = ((bf16[4,384,512]{2,1,0:T(8,128)(2,1)}), bf16[4,384,512]{2,1,0:T(8,128)(2,1)S(1)}, u32[]{:S(2)}, u32[]{:S(2)}) async-start(bf16[4,384,512]{2,1,0:T(8,128)(2,1)} %attend_bwd.3), calls=%async_computation.4 | async-start | bytes 3145728 | tf_op jit(solution)/shard_map/all_to_all | solution.py:298
  377.4 23.8 %all-to-all-start.5 = ((bf16[4,384,512]{2,1,0:T(8,128)(2,1)}), bf16[4,384,512]{2,1,0:T(8,128)(2,1)S(1)}, u32[]{:S(2)}, u32[]{:S(2)}) async-start(bf16[4,384,512]{2,1,0:T(8,128)(2,1)} %get-tuple-element.46), calls=%async_computation.5 | async-start | bytes 3145728 | tf_op jit(solution)/shard_map/all_to_all | solution.py:298
  381.2 7.1 %copy-start.4 = (bf16[4,256,1024]{2,1,0:T(8,128)(2,1)S(1)}, bf16[4,256,1024]{2,1,0:T(8,128)(2,1)}, u32[]{:S(2)}) copy-start(bf16[4,256,1024]{2,1,0:T(8,128)(2,1)} %copy-done.3) | copy-start | bytes 6291460
  381.2 8.8 %copy-start.10 = (bf16[1024,2048]{1,0:T(8,128)(2,1)S(1)}, bf16[1024,2048]{1,0:T(8,128)(2,1)}, u32[]{:S(2)}) copy-start(bf16[1024,2048]{1,0:T(8,128)(2,1)} %all-gather.4.cloned.1.call-done) | copy-start | bytes 12582916
  389.3 38.3 %collective-permute-start.3 = (bf16[1024,512]{1,0:T(8,128)(2,1)}, bf16[1024,512]{1,0:T(8,128)(2,1)}, u32[]{:S(2)}, u32[]{:S(2)}) collective-permute-start(bf16[1024,512]{1,0:T(8,128)(2,1)} %constant_dynamic-slice_fusion), channel_id=1, source_target_pairs={{0,4},{4,0},{1,5},{5,1},{2,6},{6,2},{3,7},{7,3}} | collective-permute-start | bytes 3145736 | tf_op jit(solution)/shard_map/ppermute | solution.py:295
  402.5 1.8 copy-start.2
  402.6 46.2 %collective-permute-start.4 = (bf16[4,384,512]{2,1,0:T(8,128)(2,1)}, bf16[4,384,512]{2,1,0:T(8,128)(2,1)S(1)}, u32[]{:S(2)}, u32[]{:S(2)}) collective-permute-start(bf16[4,384,512]{2,1,0:T(8,128)(2,1)} %get-tuple-element.48), channel_id=1, source_target_pairs={{0,4},{4,0},{1,5},{5,1},{2,6},{6,2},{3,7},{7,3}} | collective-permute-start | bytes 4718600 | tf_op jit(solution)/shard_map/ppermute | solution.py:295
  405.8 5.8 %slice-start = ((s8[6291456]{0:T(1024)(128)(4,1)}), s8[4194304]{0:T(1024)(128)(4,1)S(1)}, s32[]{:S(2)}) async-start(s8[6291456]{0:T(1024)(128)(4,1)} %bitcast.68), calls=%async_computation.9 | async-start | bytes 8388608
  409.3 2.4 slice-start.1
  (2 other events, 2.3 us)
Sparse Core Ops, SparseCore 0:
  56.7 55.1 all-gather.3
  182.6 54.0 all-gather.5
  238.3 63.0 all-gather.7

commit v4 on v3

--- a/solution.py
+++ b/solution.py
@@ -11,13 +11,14 @@
 GRAD_SPEC = P(("dp", "cp"), None, "tp", None)
 GRAD_OUT_SPEC = P(("dp", "cp"), "tp", None, None)
 NT = (((1,), (1,)), ((), ()))
-TN = (((0,), (0,)), ((), ()))
 NN = (((1,), (0,)), ((), ()))
 F32 = jnp.float32
 BF16 = jnp.bfloat16
 VMEM_LIMIT = 60 * 1024 * 1024
+DENSE_LIMIT = 40 * 1024 * 1024
+DENSE_TILES = 4
 FWD_SPLIT, FWD_AHEAD, FWD_BEHIND = 256, 2, 1
-BWD_SPLIT, BWD_AHEAD, BWD_BEHIND = 512, 1, 0
+BWD_SPLIT, BWD_AHEAD, BWD_BEHIND = 256, 1, 0
 
 
 def half_of(pos_blk, n_blk):
@@ -115,8 +116,8 @@
 def bwd_kernel(n_blk, groups, dim, first, count, *refs):
     q_own, q_other, kv_own, kv_other, do_ref, o_ref, lse_ref = refs[:7]
     upper = first > 0
-    g_ref = refs[7 if upper else 8]
-    kv_s, kvt_s, rq_s, rd_s, dot_s, dqt_s, dkv_s = refs[-7:]
+    g_ref = refs[7 if upper else 9]
+    kv_s, kvt_s, rq_s, rd_s, rdo_s, dot_s, dqt_s, dk_s, dv_s = refs[-9:]
     step = pl.program_id(0)
     pos = first + step
     blk = do_ref.shape[0]
@@ -127,7 +128,8 @@
         load_keys(n_blk, kv_own, kv_other, kv_s, kvt_s)
         rq_s[...] = jnp.zeros_like(rq_s)
         rd_s[...] = jnp.zeros_like(rd_s)
-        dkv_s[...] = jnp.zeros_like(dkv_s) if upper else refs[7][...]
+        dk_s[...] = jnp.zeros_like(dk_s) if upper else refs[7][...]
+        dv_s[...] = jnp.zeros_like(dv_s) if upper else refs[8][...]
 
     q = load_queries(n_blk, pos, q_own, q_other)
     do = do_ref[...]
@@ -137,14 +139,15 @@
         rows = slice(h * dim, (h + 1) * dim)
         rq_s[h, :dim, :] = q_t[rows, :]
         rd_s[h, dim:, :] = do_t[rows, :]
+        rdo_s[h] = do[:, rows]
         dot_s[h] = jnp.sum(do_t[rows, :].astype(F32) * o_ref[rows, :].astype(F32), axis=0, keepdims=True)
     dqt_s[...] = jnp.zeros_like(dqt_s)
 
     def tile(j, diag):
         kv_j = kv_s[j]
         k_t = kvt_s[j, :dim, :]
-        dk = dkv_s[j, :dim, :]
-        dv = dkv_s[j, dim:, :]
+        dk = dk_s[j]
+        dv = dv_s[j]
         chains = [(h, slice(c, c + BWD_SPLIT)) for h in range(groups) for c in range(0, blk, BWD_SPLIT)]
 
         def scores(h, cs):
@@ -154,7 +157,7 @@
         def outputs(dk, dv, h, cs, p, ds):
             dqt_s[h, :, cs] += jnp.dot(k_t, ds, preferred_element_type=F32)
             dk += lax.dot_general(rq_s[h, :dim, cs], ds, NT, preferred_element_type=F32)
-            dv += lax.dot_general(rd_s[h, dim:, cs], p, NT, preferred_element_type=F32)
+            dv += jnp.dot(p, rdo_s[h, cs, :], preferred_element_type=F32)
             return dk, dv
 
         ahead = [scores(*chain) for chain in chains[:BWD_AHEAD]]
@@ -172,8 +175,8 @@
                 dk, dv = outputs(dk, dv, *behind.pop(0))
         for item in behind:
             dk, dv = outputs(dk, dv, *item)
-        dkv_s[j, :dim, :] = dk
-        dkv_s[j, dim:, :] = dv
+        dk_s[j] = dk
+        dv_s[j] = dv
 
     tile(pos, True)
 
@@ -189,9 +192,11 @@
     def _():
         for b in range(first, first + count):
             s = b if b < n_blk // 2 else n_blk - 1 - b
-            g_ref[s, cols:, :] = dkv_s[b].astype(BF16)
+            g_ref[s, cols:cols + dim, :] = dk_s[b].astype(BF16)
+            g_ref[s, cols + dim:, :] = dv_s[b].T.astype(BF16)
         if upper:
-            refs[8][...] = dkv_s[:first]
+            refs[8][...] = dk_s[:first]
+            refs[9][...] = dv_s[:first]
 
 
 def key_specs(n_half, blk, groups, dim, first):
@@ -238,17 +243,19 @@
     cols = groups * dim
     elems = blk * blk * groups * sum(range(first + 1, first + count + 1))
     feats = cols + 2 * dim
-    keys_shape = (n_blk if first else n_half, 2 * dim, blk)
-    whole = pl.BlockSpec((n_half, 2 * dim, blk), lambda i: (0, 0, 0))
-    out_specs = [pl.BlockSpec((n_half, feats, blk), lambda i: (0, 0, 0))] + [whole] * (first > 0)
-    out_shape = [jax.ShapeDtypeStruct((n_half, feats, blk), BF16)] + [jax.ShapeDtypeStruct((n_half, 2 * dim, blk), F32)] * (first > 0)
+    held = n_blk if first else n_half
+    carry_shapes = [(n_half, dim, blk), (n_half, blk, dim)]
+    whole = [pl.BlockSpec(shape, lambda i: (0, 0, 0)) for shape in carry_shapes]
+    out_specs = [pl.BlockSpec((n_half, feats, blk), lambda i: (0, 0, 0))] + whole * (first > 0)
+    out_shape = [jax.ShapeDtypeStruct((n_half, feats, blk), BF16)] + [
+        jax.ShapeDtypeStruct(shape, F32) for shape in carry_shapes] * (first > 0)
     return pl.pallas_call(
         lambda *refs: bwd_kernel(n_blk, groups, dim, first, count, *refs),
         grid=(count,),
         in_specs=key_specs(n_half, blk, groups, dim, first) + [
             pl.BlockSpec((None, blk, cols), lambda i: (stored_block(first + i, n_blk), 0, 0)),
             feature_spec(n_blk, cols, blk, first),
-            pl.BlockSpec((None, groups, blk), lambda i: (first + i, 0, 0))] + [whole] * len(carried),
+            pl.BlockSpec((None, groups, blk), lambda i: (first + i, 0, 0))] + whole * (len(carried) > 0),
         out_specs=out_specs,
         out_shape=out_shape,
         scratch_shapes=[
@@ -256,14 +263,90 @@
             pltpu.VMEM((n_blk, 2 * dim, blk), BF16),
             pltpu.VMEM((groups, 2 * dim, blk), BF16),
             pltpu.VMEM((groups, 2 * dim, blk), BF16),
+            pltpu.VMEM((groups, blk, dim), BF16),
             pltpu.VMEM((groups, 1, blk), F32),
             pltpu.VMEM((groups, dim, blk), F32),
-            pltpu.VMEM(keys_shape, F32),
+            pltpu.VMEM((held, dim, blk), F32),
+            pltpu.VMEM((held, blk, dim), F32),
         ],
         compiler_params=pltpu.CompilerParams(dimension_semantics=("arbitrary",), vmem_limit_bytes=VMEM_LIMIT),
         cost_estimate=pl.CostEstimate(flops=elems * 10 * 4 * dim, bytes_accessed=count * blk * cols * 8, transcendentals=elems),
         name="attend_bwd",
     )(own, other, own, other, do, o, lse, *carried)
+
+
+def dense_call(kernel, grid, in_specs, out_specs, out_shape, scratch, flops, args):
+    return pl.pallas_call(
+        kernel, grid=(grid,), in_specs=in_specs, out_specs=out_specs, out_shape=out_shape, scratch_shapes=scratch,
+        compiler_params=pltpu.CompilerParams(dimension_semantics=("arbitrary",), vmem_limit_bytes=DENSE_LIMIT),
+        cost_estimate=pl.CostEstimate(flops=flops, bytes_accessed=sum(a.size * 2 for a in args), transcendentals=0),
+    )(*args)
+
+
+def project(rows, weight, parts):
+    count, depth = rows.shape
+    width = weight.shape[0] // parts
+
+    def kernel(a_ref, w_ref, o_ref):
+        o_ref[...] = lax.dot_general(a_ref[...], w_ref[...], NT, preferred_element_type=F32).astype(BF16)
+
+    return dense_call(kernel, parts,
+                      [pl.BlockSpec((count, depth), lambda i: (0, 0)), pl.BlockSpec((width, depth), lambda i: (i, 0))],
+                      pl.BlockSpec((None, count, width), lambda i: (i, 0, 0)),
+                      jax.ShapeDtypeStruct((parts, count, width), BF16), [], 2 * count * depth * width * parts, (rows, weight))
+
+
+def combine(own, w, peer, w_peer, tiles):
+    depth = w.shape[0]
+    count = own[0].shape[2]
+    cols = w.shape[1] // tiles
+    pieces = (*own, *peer)
+
+    def kernel(*refs):
+        w_ref, wp_ref, o_ref, at_s = refs[-4:]
+
+        @pl.when(pl.program_id(0) == 0)
+        def _():
+            for base, group in ((0, refs[:len(own)]), (depth, refs[len(own):len(pieces)])):
+                width = sum(ref.shape[1] for ref in group)
+                for ref in group:
+                    for c in range(ref.shape[0]):
+                        at_s[:, base + c * width:base + c * width + ref.shape[1]] = ref[c].T
+                    base += ref.shape[1]
+
+        total = jnp.dot(at_s[:, :depth], w_ref[...], preferred_element_type=F32)
+        total += jnp.dot(at_s[:, depth:], wp_ref[...], preferred_element_type=F32)
+        o_ref[...] = total.astype(BF16)
+
+    w_spec = pl.BlockSpec((depth, cols), lambda i: (0, i))
+    return dense_call(kernel, tiles,
+                      [pl.BlockSpec(p.shape, lambda i: (0, 0, 0)) for p in pieces] + [w_spec, w_spec],
+                      pl.BlockSpec((count, cols), lambda i: (0, i)),
+                      jax.ShapeDtypeStruct((count, w.shape[1]), BF16), [pltpu.VMEM((count, 2 * depth), BF16)],
+                      4 * count * depth * w.shape[1], (*pieces, w, w_peer))
+
+
+def weight_grads(g, x, g_peer, x_peer, cols, dim, scale):
+    heads, feats, count = g.shape
+    model = x.shape[1]
+
+    def kernel(g_ref, x_ref, gp_ref, xp_ref, q_ref, k_ref, v_ref):
+        def part(lo, hi):
+            total = jnp.dot(g_ref[lo:hi, :], x_ref[...], preferred_element_type=F32)
+            return total + jnp.dot(gp_ref[lo:hi, :], xp_ref[...], preferred_element_type=F32)
+
+        q_ref[...] = (part(0, cols) * scale).astype(BF16)
+        both = part(cols, feats).astype(BF16)
+        k_ref[...] = both[:dim]
+        v_ref[...] = both[dim:]
+
+    g_spec = pl.BlockSpec((None, feats, count), lambda i: (i, 0, 0))
+    x_spec = pl.BlockSpec((count, model), lambda i: (0, 0))
+    sizes = (cols, dim, dim)
+    return dense_call(kernel, heads, [g_spec, x_spec, g_spec, x_spec],
+                      [pl.BlockSpec((n, model), lambda i: (i, 0)) for n in sizes],
+                      [jax.ShapeDtypeStruct((heads * n, model), BF16) for n in sizes], [],
+                      4 * heads * feats * count * model, (g, x, g_peer, x_peer))
 
 
 def solution(mesh):
@@ -297,9 +380,6 @@
         def switch(a):
             return lax.all_to_all(a, "cp", split_axis=0, concat_axis=0, tiled=True)
 
-        def project(rows):
-            return mm(rows, w_flat, NT).astype(BF16).reshape(half_rows, kv_heads, feats).transpose(1, 0, 2)
-
         def after(value, other):
             return lax.optimization_barrier((value, other))
 
@@ -311,49 +391,48 @@
             return lax.all_gather(w, "cp", axis=0, tiled=True)
 
         x_peer = exchange(x_blk)
-        own = switch(project(x_blk))
+        own = switch(project(x_blk, w_flat, kv_heads))
         x_peer, own = after(x_peer, own)
         dy_late, x_peer = after(dy_blk, x_peer)
         dy_rows = lax.all_gather(dy_late, "tp", axis=0, tiled=True)
-        other = switch(project(x_peer))
+        other = switch(project(x_peer, w_flat, kv_heads))
 
         partial = attend(own, other, (), 0, n_half, groups, dim)
         dy_ready, partial = after(dy_rows, partial)
-        do_own = mm(dy_ready, wo, NT).astype(BF16).reshape(2 * half_rows, kv_heads, cols).transpose(1, 0, 2)
+        do_own = project(dy_ready, wo, kv_heads)
         late, do_own = after((w_flat, wo), do_own)
         do_all = switch(do_own).reshape(n_blk, half_rows, cols)
-        quarters = tuple(quarter_of(w) for w in late)
+        w_quarter, wo_quarter = (quarter_of(w) for w in late)
         o_all, lse = attend(own, other, partial, n_half, n_half, groups, dim)
-        quarters, o_all = after(quarters, o_all)
-        w_peer, wo_peer = (spread(w) for w in quarters)
+        wo_quarter, o_all = after(wo_quarter, o_all)
+        wo_peer = spread(wo_quarter)
 
         o_own = switch(o_all).reshape(q_cols, 2 * half_rows)
-        g_upper, carried = attend_grad(own, other, do_all, o_all, lse, (), n_half, n_half, groups, dim)
+        g_upper, *carried = attend_grad(own, other, do_all, o_all, lse, (), n_half, n_half, groups, dim)
         g_upper, o_own = after(g_upper, o_own)
+        w_quarter, g_upper = after(w_quarter, g_upper)
+        w_peer = spread(w_quarter)
         o_mine = lax.dynamic_slice_in_dim(o_own, mine * half_rows, half_rows, axis=1)
         o_peer = exchange(lax.dynamic_slice_in_dim(o_own, (1 - mine) * half_rows, half_rows, axis=1))
-        g_upper = switch(g_upper)
-        g_lower, = attend_grad(own, other, do_all, o_all, lse, (carried,), 0, n_half, groups, dim)
-        g_lower = switch(g_lower)
+        raw_upper = g_upper
+        g_upper = switch(raw_upper)
+        raw_lower, = attend_grad(own, other, do_all, o_all, lse, tuple(carried), 0, n_half, groups, dim)
 
         is_first = mine == 0
+        relay = exchange(jnp.where(is_first, raw_upper[:, :cols], raw_lower[:, :cols]))
+        g_lower = switch(raw_lower)
+        relay = switch(relay)
         g_mine = jnp.where(is_first, g_lower, g_upper)
         g_other = jnp.where(is_first, g_upper, g_lower)
-        g_peer = exchange(g_other).reshape(kv_heads * feats, half_rows)
-
-        def weight_grad(lo, hi, factor):
-            def part(g, rows):
-                return mm(g[:, lo:hi].reshape(kv_heads * (hi - lo), half_rows), rows, NN)
-
-            total = part(g_mine, x_blk) + part(g_other, x_peer)
-            return (total * factor).astype(BF16).reshape(1, -1, dim, model_dim).transpose(0, 3, 1, 2)
-
+        g_tail = exchange(g_other[:, cols:])
+
+        def heads_last(g):
+            return g.reshape(1, -1, dim, model_dim).transpose(0, 3, 1, 2)
+
+        y_blk = combine([o_mine[None]], wo, [o_peer[None]], wo_peer, DENSE_TILES)
         grad_wo = mm(o_own, dy_rows, NN).astype(BF16).reshape(1, q_heads, dim, model_dim)
-        y_blk = (mm(o_mine, wo, TN) + mm(o_peer, wo_peer, TN)).astype(BF16)
-        grad_wq = weight_grad(0, cols, scale)
-        grad_wk = weight_grad(cols, cols + dim, 1.0)
-        grad_wv = weight_grad(cols + dim, feats, 1.0)
-        dx_blk = (mm(g_mine.reshape(kv_heads * feats, half_rows), w_flat, TN) + mm(g_peer, w_peer, TN)).astype(BF16)
+        grad_wq, grad_wk, grad_wv = map(heads_last, weight_grads(g_mine, x_blk, g_other, x_peer, cols, dim, scale))
+        dx_blk = combine([g_mine], w_flat, [relay, g_tail], w_peer, DENSE_TILES)
         return y_blk, dx_blk, grad_wq, grad_wk, grad_wv, grad_wo
 
     return jax.shard_map(device_fn, mesh=mesh,

time: 471 us -> 401 us (0.85); the launches traced: 464 us -> 400 us
  matrix products: 68.8 us -> 6.02 us
  waiting for transfers between devices: 131 us -> 78.6 us
  Pallas kernels: 174 us -> 211 us
  starting transfers between devices: 25.6 us -> 31.6 us
  local copies, waits for them, and re-layouts: 18 us -> 23.7 us
    dot_general x14 -> x1, matrix products: 68.8 us -> 6.02 us  [mm(): return lax.dot_general(a, b, dims, preferred_element_type=F32)]
    all_to_all x5 -> x6, waiting for transfers between devices: 91.8 us -> 43.9 us  [switch(): return lax.all_to_all(a, 'cp', split_axis=0, concat_axis=0, tiled=True)]
    pallas_call x0 -> x6, Pallas kernels: none -> 44.4 us  [dense_call(): pl.pallas_call(kernel, grid=(grid,), in_specs=in_specs, out_specs=out_spe...]
    unnamed x26 -> x38, local copies, waits for them, and re-layouts: 4.96 us -> 18.8 us
    pallas_call x2, Pallas kernels: 112 us -> 105 us  [attend_grad(): pl.pallas_call(lambda *refs: bwd_kernel(n_blk, groups, dim, first, count,...]
    reshape x3 -> x0, local copies, waits for them, and re-layouts: 5 us -> none  [the longest x1 2.56 us: device_fn(): mm(dy_ready, wo, NT).astype(BF16).reshape(2 * half_rows, kv_heads, cols)]
    all_to_all x5 -> x6, starting transfers between devices: 18.4 us -> 22.6 us  [switch(): return lax.all_to_all(a, 'cp', split_axis=0, concat_axis=0, tiled=True)]
    ppermute x5 -> x6, waiting for transfers between devices: 35.1 us -> 31.5 us  [exchange(): return lax.ppermute(a, 'tp', swap)]
  transfers between devices with their start and end apart: 13 -> 15, of which waited for: 8 -> 6; matrix products, arithmetic and copies ran while one was open for 15% -> 6% of each run, Pallas kernels for 38% -> 49%
where the time goes in v4:
time: 401 us; the launch traced here: 400 us
  Pallas kernels  211 us (53%)
  waiting for transfers between devices  78.6 us (20%)
  starting transfers between devices  31.6 us (8%)
  local copies, waits for them, and re-layouts  23.7 us (6%)
  blocking collectives  23.3 us (6%)
  between operations  14 us (3%)
  other arithmetic  11.1 us (3%)
  matrix products  6.02 us (2%)
    pallas_call x2, Pallas kernels, attend_grad(): pl.pallas_call(lambda *refs: bwd_kernel(n_blk, groups, dim, first, count,...  105 us
    pallas_call x2, Pallas kernels, attend(): pl.pallas_call(lambda *refs: fwd_kernel(n_blk, groups, dim, first, *refs)...  61.9 us
    pallas_call x6, Pallas kernels, dense_call(): pl.pallas_call(kernel, grid=(grid,), in_specs=in_specs, out_specs=out_spe...  44.4 us
    all_to_all x6, waiting for transfers between devices, switch(): return lax.all_to_all(a, 'cp', split_axis=0, concat_axis=0, tiled=True)  43.9 us
    ppermute x6, waiting for transfers between devices, exchange(): return lax.ppermute(a, 'tp', swap)  31.5 us
    all_to_all x1, blocking collectives, switch(): return lax.all_to_all(a, 'cp', split_axis=0, concat_axis=0, tiled=True)  23.3 us
    all_to_all x6, starting transfers between devices, switch(): return lax.all_to_all(a, 'cp', split_axis=0, concat_axis=0, tiled=True)  22.6 us
    unnamed x38, local copies, waits for them, and re-layouts  18.8 us
  transfers between devices with their start and end apart: 15, of which 6 were waited for; matrix products, arithmetic and copies ran while one was open for 6% of the time, Pallas kernels for 49%

profile of v4, /device:TPU:0, one launch (start us, length us, event | category | flops | bytes accessed | tf_op | source)
XLA Modules:
  0.0 399.8 jit_solution(6829074855942797317)
XLA Ops:
  13.2 4.6 %pad_maximum_fusion = bf16[4,384,2048]{2,1,0:T(8,128)(2,1)S(1)} fusion(bf16[4,64,2048]{2,1,0:T(8,128)(2,1)S(1)} %bitcast.36, bf16[4,64,2048]{2,1,0:T(8,128)(2,1)} %bitcast.37, bf16[4,256,2048]{2,1,0:T(8,128)(2,1)S(1)} %bitcast.31), kind=kLoop, calls=%fused_computation | loop fusion | flops 18874368 | bytes 12582912 | tf_op jit(solution)/shard_map/concatenate | solution.py:370
  17.7 5.1 %shard_map.109 = bf16[4,512,384]{2,1,0:T(8,128)(2,1)S(1)} custom-call(bf16[512,2048]{1,0:T(8,128)(2,1)S(1)} %copy-done.8, bf16[1536,2048]{1,0:T(8,128)(2,1)S(1)} %bitcast.24), custom_call_target="tpu_custom_call" | custom-call | flops 3221225472 | bytes 8388608 | tf_op jit(solution)/shard_map/pallas_call | solution.py:279
  22.9 23.3 %all_to_all.35.refs_0_.refs_2_ = bf16[4,512,384]{2,1,0:T(8,128)(2,1)} all-to-all(bf16[4,512,384]{2,1,0:T(8,128)(2,1)S(1)} %shard_map.109), channel_id=1, replica_groups=mesh['dp'=1,'tp'=2,'cp'=4] {'cp'}, dimensions={0} | all-to-all | bytes 3145728 | tf_op jit(solution)/shard_map/all_to_all | solution.py:381
  46.1 10.3 %collective-permute-done.a_ref.xp_ref = bf16[512,2048]{1,0:T(8,128)(2,1)S(1)} collective-permute-done((bf16[512,2048]{1,0:T(8,128)(2,1)}, bf16[512,2048]{1,0:T(8,128)(2,1)S(1)}, u32[]{:S(2)}, u32[]{:S(2)}) %collective-permute-start) | collective-permute-done | bytes 2097184 | tf_op jit(solution)/shard_map/ppermute | solution.py:378
  60.0 5.9 %shard_map.110 = bf16[4,512,384]{2,1,0:T(8,128)(2,1)} custom-call(bf16[512,2048]{1,0:T(8,128)(2,1)S(1)} %collective-permute-done.a_ref.xp_ref, bf16[1536,2048]{1,0:T(8,128)(2,1)S(1)} %bitcast.26), custom_call_target="tpu_custom_call" | custom-call | flops 3221225472 | bytes 8388608 | tf_op jit(solution)/shard_map/pallas_call | solution.py:279
  65.8 3.6 all-to-all-start.1
  69.4 20.0 %all-to-all-done.1.refs_1_.refs_3_ = bf16[4,512,384]{2,1,0:T(8,128)(2,1)S(1)} async-done(((bf16[4,512,384]{2,1,0:T(8,128)(2,1)}), bf16[4,512,384]{2,1,0:T(8,128)(2,1)S(1)}, u32[]{:S(2)}, u32[]{:S(2)}) %all-to-all-start.1) | async-done | bytes 1572896 | tf_op jit(solution)/shard_map/all_to_all | solution.py:381
  90.7 17.9 %attend_fwd.2 = (bf16[4,256,1024]{2,1,0:T(8,128)(2,1)}, f32[8,4,512]{2,1,0:T(4,128)}) custom-call(bf16[4,512,384]{2,1,0:T(8,128)(2,1)} %all_to_all.35.refs_0_.refs_2_, bf16[4,512,384]{2,1,0:T(8,128)(2,1)} %copy-done.17, bf16[4,512,384]{2,1,0:T(8,128)(2,1)} %all_to_all.35.refs_0_.refs_2_, bf16[4,512,384]{2,1,0:T(8,128)(2,1)} %copy-done.17), custom_call_target="tpu_custom_call" | custom-call | flops 10737418240 | bytes 2097152 | tf_op jit(solution)/shard_map/attend_fwd/pallas_call | solution.py:219
  116.1 6.0 %shard_map.111 = bf16[4,1024,256]{2,1,0:T(8,128)(2,1)} custom-call(bf16[1024,2048]{1,0:T(8,128)(2,1)S(1)} %copy-done.5, bf16[1024,2048]{1,0:T(8,128)(2,1)S(1)} %bitcast.28), custom_call_target="tpu_custom_call" | custom-call | flops 4294967296 | bytes 8388608 | tf_op jit(solution)/shard_map/pallas_call | solution.py:279
  122.5 3.6 all-to-all-start.2
  130.7 43.9 %attend_fwd.3 = (bf16[4,256,1024]{2,1,0:T(8,128)(2,1)}, f32[8,4,512]{2,1,0:T(4,128)}) custom-call(bf16[4,512,384]{2,1,0:T(8,128)(2,1)} %all_to_all.35.refs_0_.refs_2_, bf16[4,512,384]{2,1,0:T(8,128)(2,1)} %copy-done.17, bf16[4,512,384]{2,1,0:T(8,128)(2,1)} %all_to_all.35.refs_0_.refs_2_, ...), custom_call_target="tpu_custom_call", output_to_operand_aliasing={{0}: (4, {}), {1}: (5, {})} | custom-call | flops 27917287424 | bytes 2097152 | tf_op jit(solution)/shard_map/attend_fwd/pallas_call | solution.py:219
  176.0 3.8 all-to-all-start.3
  179.9 73.3 %attend_bwd.2 = (bf16[4,384,512]{2,1,0:T(8,128)(2,1)}, f32[4,64,512]{2,1,0:T(8,128)}, f32[4,512,64]{2,1,0:T(8,128)}) custom-call(bf16[4,512,384]{2,1,0:T(8,128)(2,1)} %all_to_all.35.refs_0_.refs_2_, bf16[4,512,384]{2,1,0:T(8,128)(2,1)} %copy-done.17, bf16[4,512,384]{2,1,0:T(8,128)(2,1)} %all_to_all.35.refs_0_.refs_2_, bf16[4,512,384]{2,1,0:T(8,128)(2,1)} %copy-done.17, ...), custom_call_target="tpu_custom_call" | custom-call | flops 69793218560 | bytes 4194304 | tf_op jit(solution)/shard_map/attend_bwd/pallas_call | solution.py:252
  253.2 31.9 %attend_bwd.3 = bf16[4,384,512]{2,1,0:T(8,128)(2,1)} custom-call(bf16[4,512,384]{2,1,0:T(8,128)(2,1)} %all_to_all.35.refs_0_.refs_2_, bf16[4,512,384]{2,1,0:T(8,128)(2,1)} %copy-done.17, bf16[4,512,384]{2,1,0:T(8,128)(2,1)} %all_to_all.35.refs_0_.refs_2_, bf16[4,512,384]{2,1,0:T(8,128)(2,1)} %copy-done.17, bf16[8,512,256]{2,1,0:T(8,128)(2,1)} %bitcast.35, ...), custom_call_target="tpu_custom_call" | custom-call | flops 26843545600 | bytes 4194304 | tf_op jit(solution)/shard_map/attend_bwd/pallas_call | solution.py:252
  285.1 3.6 all-to-all-start.4
  288.7 23.9 %all-to-all-done.4 = bf16[4,384,512]{2,1,0:T(8,128)(2,1)S(1)} async-done(((bf16[4,384,512]{2,1,0:T(8,128)(2,1)}), bf16[4,384,512]{2,1,0:T(8,128)(2,1)S(1)}, u32[]{:S(2)}, u32[]{:S(2)}) %all-to-all-start.4) | async-done | bytes 1572896 | tf_op jit(solution)/shard_map/all_to_all | solution.py:381
  312.6 3.8 all-to-all-start.5
  321.5 6.0 %convolution_convert_fusion = bf16[1024,2048]{1,0:T(8,128)(2,1)} fusion(bf16[1024,1024]{1,0:T(8,128)(2,1)S(1)} %bitcast.33, bf16[1024,2048]{1,0:T(8,128)(2,1)S(1)} %copy-done.6), kind=kOutput, calls=%fused_computation.1 | convolution fusion | flops 4297064448 | bytes 10485760 | tf_op jit(solution)/shard_map/dot_general | solution.py:375
  327.5 16.9 %collective-permute-done.4 = bf16[4,256,512]{2,1,0:T(8,128)(2,1)} collective-permute-done((bf16[4,256,512]{2,1,0:T(8,128)(2,1)S(1)}, bf16[4,256,512]{2,1,0:T(8,128)(2,1)}, u32[]{:S(2)}, u32[]{:S(2)}) %collective-permute-start.4) | collective-permute-done | bytes 1048608 | tf_op jit(solution)/shard_map/ppermute | solution.py:378
  345.5 4.3 %all-to-all-start.6 = ((bf16[4,256,512]{2,1,0:T(8,128)(2,1)}), bf16[4,256,512]{2,1,0:T(8,128)(2,1)}, u32[]{:S(2)}, u32[]{:S(2)}) async-start(bf16[4,256,512]{2,1,0:T(8,128)(2,1)} %collective-permute-done.4), calls=%async_computation.6 | async-start | bytes 2097152 | tf_op jit(solution)/shard_map/all_to_all | solution.py:381
  354.3 8.2 %shard_map.114 = (bf16[1024,2048]{1,0:T(8,128)(2,1)}, bf16[256,2048]{1,0:T(8,128)(2,1)}, bf16[256,2048]{1,0:T(8,128)(2,1)}) custom-call(bf16[4,384,512]{2,1,0:T(8,128)(2,1)S(1)} %get-tuple-element.59.refs_0_.g_ref, bf16[512,2048]{1,0:T(8,128)(2,1)S(1)} %copy-done.9, bf16[4,384,512]{2,1,0:T(8,128)(2,1)S(1)} %get-tuple-element.58.gp_ref, ...), custom_call_target="tpu_custom_call" | custom-call | flops 6442450944 | bytes 7340032 | tf_op jit(solution)/shard_map/pallas_call | solution.py:279
  362.5 4.3 %collective-permute-done.2 = bf16[1024,512]{1,0:T(8,128)(2,1)} collective-permute-done((bf16[1024,512]{1,0:T(8,128)(2,1)}, bf16[1024,512]{1,0:T(8,128)(2,1)}, u32[]{:S(2)}, u32[]{:S(2)}) %collective-permute-start.2) | collective-permute-done | bytes 1048608 | tf_op jit(solution)/shard_map/ppermute | solution.py:378
  371.2 8.2 %shard_map.112 = bf16[512,2048]{1,0:T(8,128)(2,1)} custom-call(bf16[1,1024,512]{2,1,0:T(8,128)(2,1)S(1)} %get-tuple-element.61.refs_0_, bf16[1,1024,512]{2,1,0:T(8,128)(2,1)} %bitcast.9.refs_1_, bf16[1024,2048]{1,0:T(8,128)(2,1)S(1)} %bitcast.30, bf16[1024,2048]{1,0:T(8,128)(2,1)S(1)} %copy-done.7), custom_call_target="tpu_custom_call" | custom-call | flops 4294967296 | bytes 10485760 | tf_op jit(solution)/shard_map/pallas_call | solution.py:279
  382.2 11.0 %shard_map.113 = bf16[512,2048]{1,0:T(8,128)(2,1)} custom-call(bf16[4,384,512]{2,1,0:T(8,128)(2,1)S(1)} %get-tuple-element.59.refs_0_.g_ref, bf16[4,256,512]{2,1,0:T(8,128)(2,1)} %all-to-all-done.6.refs_1_, bf16[4,128,512]{2,1,0:T(8,128)(2,1)S(1)} %collective-permute-done.5.refs_2_, bf16[1536,2048]{1,0:T(8,128)(2,1)S(1)} %bitcast.27, ...), custom_call_target="tpu_custom_call" | custom-call | flops 6442450944 | bytes 15728640 | tf_op jit(solution)/shard_map/pallas_call | solution.py:279
  (67 shorter events, 42.6 us)
Async XLA Ops:
  7.2 6.0 %copy-start.18 = (bf16[2048,4,64]{0,2,1:T(8,128)(2,1)S(1)}, bf16[2048,4,64]{0,2,1:T(8,128)(2,1)}, u32[]{:S(2)}) copy-start(bf16[2048,4,64]{0,2,1:T(8,128)(2,1)} %param.9) | copy-start | bytes 3145732
  7.2 104.6 %all-gather.4.cloned.1.call-start = ((), (), s32[]{:S(2)}) async-start(), calls=%async_computation.7 | async-start | bytes 6291456 | tf_op jit(solution)/shard_map/all_gather | solution.py:397
  7.2 49.2 %collective-permute-start = (bf16[512,2048]{1,0:T(8,128)(2,1)}, bf16[512,2048]{1,0:T(8,128)(2,1)S(1)}, u32[]{:S(2)}, u32[]{:S(2)}) collective-permute-start(bf16[512,2048]{1,0:T(8,128)(2,1)} %x_ref.1), channel_id=1, source_target_pairs={{0,4},{4,0},{1,5},{5,1},{2,6},{6,2},{3,7},{7,3}} | collective-permute-start | bytes 6291464 | tf_op jit(solution)/shard_map/ppermute | solution.py:378
  13.1 4.6 %copy-start.8 = (bf16[512,2048]{1,0:T(8,128)(2,1)S(1)}, bf16[512,2048]{1,0:T(8,128)(2,1)}, u32[]{:S(2)}) copy-start(bf16[512,2048]{1,0:T(8,128)(2,1)} %x_ref.1) | copy-start | bytes 6291460
  17.7 5.2 %copy-start = (bf16[4,384,2048]{2,1,0:T(8,128)(2,1)}, bf16[4,384,2048]{2,1,0:T(8,128)(2,1)S(1)}, u32[]{:S(2)}) copy-start(bf16[4,384,2048]{2,1,0:T(8,128)(2,1)S(1)} %pad_maximum_fusion) | copy-start | bytes 18874372
  56.4 9.4 %copy-start.10 = (bf16[512,2048]{1,0:T(8,128)(2,1)}, bf16[512,2048]{1,0:T(8,128)(2,1)S(1)}, u32[]{:S(2)}) copy-start(bf16[512,2048]{1,0:T(8,128)(2,1)S(1)} %collective-permute-done.a_ref.xp_ref) | copy-start | bytes 6291460
  56.4 3.5 copy-start.1
  65.8 23.6 %all-to-all-start.1 = ((bf16[4,512,384]{2,1,0:T(8,128)(2,1)}), bf16[4,512,384]{2,1,0:T(8,128)(2,1)S(1)}, u32[]{:S(2)}, u32[]{:S(2)}) async-start(bf16[4,512,384]{2,1,0:T(8,128)(2,1)} %shard_map.110), calls=%async_computation.1 | async-start | bytes 3145728 | tf_op jit(solution)/shard_map/all_to_all | solution.py:381
  122.2 52.4 %collective-permute-start.1 = (bf16[256,2048]{1,0:T(8,128)(2,1)S(1)}, bf16[256,2048]{1,0:T(8,128)(2,1)}, u32[]{:S(2)}, u32[]{:S(2)}) collective-permute-start(bf16[256,2048]{1,0:T(8,128)(2,1)S(1)} %constant_dynamic-slice_fusion.2), channel_id=1, source_target_pairs={{0,4},{4,0},{1,5},{5,1},{2,6},{6,2},{3,7},{7,3}} | collective-permute-start | bytes 3145736 | tf_op jit(solution)/shard_map/ppermute | solution.py:378
  122.5 52.1 %all-to-all-start.2 = ((bf16[4,1024,256]{2,1,0:T(8,128)(2,1)}), bf16[4,1024,256]{2,1,0:T(8,128)(2,1)S(1)}, u32[]{:S(2)}, u32[]{:S(2)}) async-start(bf16[4,1024,256]{2,1,0:T(8,128)(2,1)} %shard_map.111), calls=%async_computation.2 | async-start | bytes 4194304 | tf_op jit(solution)/shard_map/all_to_all | solution.py:381
  126.2 240.7 %all-gather.6.cloned.1.call-start = ((), (), s32[]{:S(2)}) async-start(), calls=%async_computation.8 | async-start | bytes 5242880 | tf_op jit(solution)/shard_map/all_gather | solution.py:391
  129.0 124.2 %collective-permute-start.3 = (bf16[384,2048]{1,0:T(8,128)(2,1)}, bf16[384,2048]{1,0:T(8,128)(2,1)}, u32[]{:S(2)}, u32[]{:S(2)}) collective-permute-start(bf16[384,2048]{1,0:T(8,128)(2,1)} %constant_dynamic-slice_fusion), channel_id=1, source_target_pairs={{0,4},{4,0},{1,5},{5,1},{2,6},{6,2},{3,7},{7,3}} | collective-permute-start | bytes 4718600 | tf_op jit(solution)/shard_map/ppermute | solution.py:378
  176.0 77.2 %all-to-all-start.3 = ((bf16[4,256,1024]{2,1,0:T(8,128)(2,1)}), bf16[4,256,1024]{2,1,0:T(8,128)(2,1)S(1)}, u32[]{:S(2)}, u32[]{:S(2)}) async-start(bf16[4,256,1024]{2,1,0:T(8,128)(2,1)} %get-tuple-element.44.refs_5_), calls=%async_computation.3 | async-start | bytes 4194304 | tf_op jit(solution)/shard_map/all_to_all | solution.py:381
  179.8 199.6 %all-gather.8.cloned.1.call-start = ((), (), s32[]{:S(2)}) async-start(), calls=%async_computation.9 | async-start | bytes 7864320 | tf_op jit(solution)/shard_map/all_gather | solution.py:391
  253.2 31.9 %copy-start.12 = (bf16[4,256,1024]{2,1,0:T(8,128)(2,1)}, bf16[4,256,1024]{2,1,0:T(8,128)(2,1)S(1)}, u32[]{:S(2)}) copy-start(bf16[4,256,1024]{2,1,0:T(8,128)(2,1)S(1)} %all-to-all-done.3) | copy-start | bytes 6291460
  285.1 27.5 %all-to-all-start.4 = ((bf16[4,384,512]{2,1,0:T(8,128)(2,1)}), bf16[4,384,512]{2,1,0:T(8,128)(2,1)S(1)}, u32[]{:S(2)}, u32[]{:S(2)}) async-start(bf16[4,384,512]{2,1,0:T(8,128)(2,1)} %attend_bwd.3), calls=%async_computation.4 | async-start | bytes 3145728 | tf_op jit(solution)/shard_map/all_to_all | solution.py:381
  312.6 5.6 %copy-start.14 = (bf16[4,384,512]{2,1,0:T(8,128)(2,1)}, bf16[4,384,512]{2,1,0:T(8,128)(2,1)S(1)}, u32[]{:S(2)}) copy-start(bf16[4,384,512]{2,1,0:T(8,128)(2,1)S(1)} %all-to-all-done.4) | copy-start | bytes 4718596
  312.6 31.8 %all-to-all-start.5 = ((bf16[4,384,512]{2,1,0:T(8,128)(2,1)}), bf16[4,384,512]{2,1,0:T(8,128)(2,1)S(1)}, u32[]{:S(2)}, u32[]{:S(2)}) async-start(bf16[4,384,512]{2,1,0:T(8,128)(2,1)} %get-tuple-element.53), calls=%async_computation.5 | async-start | bytes 3145728 | tf_op jit(solution)/shard_map/all_to_all | solution.py:381
  318.2 26.2 %collective-permute-start.4 = (bf16[4,256,512]{2,1,0:T(8,128)(2,1)S(1)}, bf16[4,256,512]{2,1,0:T(8,128)(2,1)}, u32[]{:S(2)}, u32[]{:S(2)}) collective-permute-start(bf16[4,256,512]{2,1,0:T(8,128)(2,1)S(1)} %slice_select_fusion), channel_id=1, source_target_pairs={{0,4},{4,0},{1,5},{5,1},{2,6},{6,2},{3,7},{7,3}} | collective-permute-start | bytes 3145736 | tf_op jit(solution)/shard_map/ppermute | solution.py:378
  320.9 45.9 %collective-permute-start.2 = (bf16[1024,512]{1,0:T(8,128)(2,1)}, bf16[1024,512]{1,0:T(8,128)(2,1)}, u32[]{:S(2)}, u32[]{:S(2)}) collective-permute-start(bf16[1024,512]{1,0:T(8,128)(2,1)} %get-tuple-element.60), channel_id=1, source_target_pairs={{0,4},{4,0},{1,5},{5,1},{2,6},{6,2},{3,7},{7,3}} | collective-permute-start | bytes 3145736 | tf_op jit(solution)/shard_map/ppermute | solution.py:378
  345.5 33.9 %all-to-all-start.6 = ((bf16[4,256,512]{2,1,0:T(8,128)(2,1)}), bf16[4,256,512]{2,1,0:T(8,128)(2,1)}, u32[]{:S(2)}, u32[]{:S(2)}) async-start(bf16[4,256,512]{2,1,0:T(8,128)(2,1)} %collective-permute-done.4), calls=%async_computation.6 | async-start | bytes 2097152 | tf_op jit(solution)/shard_map/all_to_all | solution.py:381
  349.8 4.6 %copy-start.9 = (bf16[512,2048]{1,0:T(8,128)(2,1)S(1)}, bf16[512,2048]{1,0:T(8,128)(2,1)}, u32[]{:S(2)}) copy-start(bf16[512,2048]{1,0:T(8,128)(2,1)} %x_ref.1) | copy-start | bytes 6291460
  349.8 4.6 %copy-start.11 = (bf16[512,2048]{1,0:T(8,128)(2,1)S(1)}, bf16[512,2048]{1,0:T(8,128)(2,1)}, u32[]{:S(2)}) copy-start(bf16[512,2048]{1,0:T(8,128)(2,1)} %copy-done.10) | copy-start | bytes 6291460
  352.9 26.5 %collective-permute-start.5 = (bf16[4,128,512]{2,1,0:T(8,128)(2,1)}, bf16[4,128,512]{2,1,0:T(8,128)(2,1)S(1)}, u32[]{:S(2)}, u32[]{:S(2)}) collective-permute-start(bf16[4,128,512]{2,1,0:T(8,128)(2,1)} %slice.13), channel_id=1, source_target_pairs={{0,4},{4,0},{1,5},{5,1},{2,6},{6,2},{3,7},{7,3}} | collective-permute-start | bytes 1572872 | tf_op jit(solution)/shard_map/ppermute | solution.py:378
  (10 other events, 21.8 us)
Sparse Core Ops, SparseCore 0:
  56.6 55.1 all-gather.3
  174.8 54.5 all-gather.5
  253.4 47.9 all-gather.7

commit v5 on v4

--- a/solution.py
+++ b/solution.py
@@ -11,11 +11,10 @@
 GRAD_SPEC = P(("dp", "cp"), None, "tp", None)
 GRAD_OUT_SPEC = P(("dp", "cp"), "tp", None, None)
 NT = (((1,), (1,)), ((), ()))
-NN = (((1,), (0,)), ((), ()))
 F32 = jnp.float32
 BF16 = jnp.bfloat16
 VMEM_LIMIT = 60 * 1024 * 1024
-DENSE_LIMIT = 40 * 1024 * 1024
+DENSE_LIMIT = 62 * 1024 * 1024
 DENSE_TILES = 4
 FWD_SPLIT, FWD_AHEAD, FWD_BEHIND = 256, 2, 1
 BWD_SPLIT, BWD_AHEAD, BWD_BEHIND = 256, 1, 0
@@ -70,11 +69,14 @@
         v_t = kvt_s[j, dim:, :]
         chains = [(h, slice(c, c + FWD_SPLIT)) for h in range(groups) for c in range(0, blk, FWD_SPLIT)]
 
+        def seen(cs):
+            return cs.stop if diag else blk
+
         def scores(h, cs):
-            return jnp.dot(kv_j, rq_s[h, :, cs], preferred_element_type=F32)
+            return jnp.dot(kv_j[:seen(cs)], rq_s[h, :, cs], preferred_element_type=F32)
 
         def output(h, cs, p, alpha):
-            o = jnp.dot(v_t, p, preferred_element_type=F32)
+            o = jnp.dot(v_t[:, :seen(cs)], p, preferred_element_type=F32)
             acc_s[h, :, cs] = o if alpha is None else acc_s[h, :, cs] * alpha + o
 
         ahead = [scores(*chain) for chain in chains[:FWD_AHEAD]]
@@ -146,19 +148,25 @@
     def tile(j, diag):
         kv_j = kv_s[j]
         k_t = kvt_s[j, :dim, :]
-        dk = dk_s[j]
-        dv = dv_s[j]
+        dk, dv = (None, None) if diag else (dk_s[j], dv_s[j])
         chains = [(h, slice(c, c + BWD_SPLIT)) for h in range(groups) for c in range(0, blk, BWD_SPLIT)]
 
+        def seen(cs):
+            return cs.stop if diag else blk
+
         def scores(h, cs):
-            return (jnp.dot(kv_j, rq_s[h, :, cs], preferred_element_type=F32),
-                    jnp.dot(kv_j, rd_s[h, :, cs], preferred_element_type=F32))
+            return (jnp.dot(kv_j[:seen(cs)], rq_s[h, :, cs], preferred_element_type=F32),
+                    jnp.dot(kv_j[:seen(cs)], rd_s[h, :, cs], preferred_element_type=F32))
 
         def outputs(dk, dv, h, cs, p, ds):
-            dqt_s[h, :, cs] += jnp.dot(k_t, ds, preferred_element_type=F32)
-            dk += lax.dot_general(rq_s[h, :dim, cs], ds, NT, preferred_element_type=F32)
-            dv += jnp.dot(p, rdo_s[h, cs, :], preferred_element_type=F32)
-            return dk, dv
+            dqt_s[h, :, cs] += jnp.dot(k_t[:, :seen(cs)], ds, preferred_element_type=F32)
+            dk_part = lax.dot_general(rq_s[h, :dim, cs], ds, NT, preferred_element_type=F32)
+            dv_part = jnp.dot(p, rdo_s[h, cs, :], preferred_element_type=F32)
+            if diag:
+                dk_s[j, :, :seen(cs)] += dk_part
+                dv_s[j, :seen(cs), :] += dv_part
+                return dk, dv
+            return dk + dk_part, dv + dv_part
 
         ahead = [scores(*chain) for chain in chains[:BWD_AHEAD]]
         behind = []
@@ -175,8 +183,9 @@
                 dk, dv = outputs(dk, dv, *behind.pop(0))
         for item in behind:
             dk, dv = outputs(dk, dv, *item)
-        dk_s[j] = dk
-        dv_s[j] = dv
+        if not diag:
+            dk_s[j] = dk
+            dv_s[j] = dv
 
     tile(pos, True)
 
@@ -296,6 +305,18 @@
                       jax.ShapeDtypeStruct((parts, count, width), BF16), [], 2 * count * depth * width * parts, (rows, weight))
 
 
+def product(a, b, tiles):
+    count = a.shape[0] // tiles
+
+    def kernel(a_ref, b_ref, o_ref):
+        o_ref[...] = jnp.dot(a_ref[...], b_ref[...], preferred_element_type=F32).astype(BF16)
+
+    return dense_call(kernel, tiles,
+                      [pl.BlockSpec((count, a.shape[1]), lambda i: (i, 0)), pl.BlockSpec(b.shape, lambda i: (0, 0))],
+                      pl.BlockSpec((count, b.shape[1]), lambda i: (i, 0)),
+                      jax.ShapeDtypeStruct((a.shape[0], b.shape[1]), BF16), [], 2 * a.size * b.shape[1], (a, b))
+
+
 def combine(own, w, peer, w_peer, tiles):
     depth = w.shape[0]
     count = own[0].shape[2]
@@ -371,9 +392,6 @@
                                  w_key.transpose(1, 2, 0), w_value.transpose(1, 2, 0)], axis=1)
         w_flat = w_all.reshape(kv_heads * feats, model_dim)
 
-        def mm(a, b, dims):
-            return lax.dot_general(a, b, dims, preferred_element_type=F32)
-
         def exchange(a):
             return lax.ppermute(a, "tp", swap)
 
@@ -385,33 +403,32 @@
 
         def quarter_of(w):
             part = w.shape[0] // seq_shards
-            return exchange(lax.dynamic_slice_in_dim(w, quarter * part, part, axis=0))
+            return lax.dynamic_slice_in_dim(w, quarter * part, part, axis=0)
 
         def spread(w):
             return lax.all_gather(w, "cp", axis=0, tiled=True)
 
         x_peer = exchange(x_blk)
         own = switch(project(x_blk, w_flat, kv_heads))
-        x_peer, own = after(x_peer, own)
+        pieces = (quarter_of(w_flat), quarter_of(wo))
+        (x_peer, pieces), own = after((x_peer, pieces), own)
         dy_late, x_peer = after(dy_blk, x_peer)
         dy_rows = lax.all_gather(dy_late, "tp", axis=0, tiled=True)
         other = switch(project(x_peer, w_flat, kv_heads))
 
         partial = attend(own, other, (), 0, n_half, groups, dim)
+        dy_rows, pieces = after(dy_rows, pieces)
+        wo_quarter, w_quarter = exchange(pieces[1]), exchange(pieces[0])
         dy_ready, partial = after(dy_rows, partial)
         do_own = project(dy_ready, wo, kv_heads)
-        late, do_own = after((w_flat, wo), do_own)
         do_all = switch(do_own).reshape(n_blk, half_rows, cols)
-        w_quarter, wo_quarter = (quarter_of(w) for w in late)
         o_all, lse = attend(own, other, partial, n_half, n_half, groups, dim)
-        wo_quarter, o_all = after(wo_quarter, o_all)
-        wo_peer = spread(wo_quarter)
+        (wo_quarter, w_quarter), o_all = after((wo_quarter, w_quarter), o_all)
+        wo_peer, w_peer = spread(wo_quarter), spread(w_quarter)
 
         o_own = switch(o_all).reshape(q_cols, 2 * half_rows)
         g_upper, *carried = attend_grad(own, other, do_all, o_all, lse, (), n_half, n_half, groups, dim)
         g_upper, o_own = after(g_upper, o_own)
-        w_quarter, g_upper = after(w_quarter, g_upper)
-        w_peer = spread(w_quarter)
         o_mine = lax.dynamic_slice_in_dim(o_own, mine * half_rows, half_rows, axis=1)
         o_peer = exchange(lax.dynamic_slice_in_dim(o_own, (1 - mine) * half_rows, half_rows, axis=1))
         raw_upper = g_upper
@@ -430,7 +447,7 @@
             return g.reshape(1, -1, dim, model_dim).transpose(0, 3, 1, 2)
 
         y_blk = combine([o_mine[None]], wo, [o_peer[None]], wo_peer, DENSE_TILES)
-        grad_wo = mm(o_own, dy_rows, NN).astype(BF16).reshape(1, q_heads, dim, model_dim)
+        grad_wo = product(o_own, dy_rows, DENSE_TILES).reshape(1, q_heads, dim, model_dim)
         grad_wq, grad_wk, grad_wv = map(heads_last, weight_grads(g_mine, x_blk, g_other, x_peer, cols, dim, scale))
         dx_blk = combine([g_mine], w_flat, [relay, g_tail], w_peer, DENSE_TILES)
         return y_blk, dx_blk, grad_wq, grad_wk, grad_wv, grad_wo

time: 401 us -> 436 us (1.087)
  waiting for transfers between devices: 78.6 us -> 116 us
  local copies, waits for them, and re-layouts: 23.7 us -> 8.83 us
  Pallas kernels: 211 us -> 225 us
  matrix products: 6.02 us -> 0 us
    all_to_all x6, waiting for transfers between devices: 43.9 us -> 74.5 us  [switch(): return lax.all_to_all(a, 'cp', split_axis=0, concat_axis=0, tiled=True)]
    pallas_call x6 -> x7, Pallas kernels: 44.4 us -> 66.2 us  [dense_call(): pl.pallas_call(kernel, grid=(grid,), in_specs=in_specs, out_specs=out_spe...]
    unnamed x38 -> x16, local copies, waits for them, and re-layouts: 18.8 us -> 1.35 us
    pallas_call x2, Pallas kernels: 105 us -> 98.2 us  [attend_grad(): pl.pallas_call(lambda *refs: bwd_kernel(n_blk, groups, dim, first, count,...]
    dot_general x1 -> x0, matrix products: 6.02 us -> none  [mm(): return lax.dot_general(a, b, dims, preferred_element_type=F32)]
    ppermute x6, waiting for transfers between devices: 31.5 us -> 36.2 us  [exchange(): return lax.ppermute(a, 'tp', swap)]
  transfers between devices with their start and end apart: 15 -> 15, of which waited for: 6 -> 9; matrix products, arithmetic and copies ran while one was open for 6% -> 5% of each run, Pallas kernels for 49% -> 49%
where the time goes in v5:
time: 436 us; the launch traced here: 435 us
  Pallas kernels  225 us (52%)
  waiting for transfers between devices  116 us (27%)
  starting transfers between devices  33.3 us (8%)
  blocking collectives  24.5 us (6%)
  between operations  13.9 us (3%)
  other arithmetic  13.5 us (3%)
  local copies, waits for them, and re-layouts  8.83 us (2%)
    pallas_call x2, Pallas kernels, attend_grad(): pl.pallas_call(lambda *refs: bwd_kernel(n_blk, groups, dim, first, count,...  98.2 us
    all_to_all x6, waiting for transfers between devices, switch(): return lax.all_to_all(a, 'cp', split_axis=0, concat_axis=0, tiled=True)  74.5 us
    pallas_call x7, Pallas kernels, dense_call(): pl.pallas_call(kernel, grid=(grid,), in_specs=in_specs, out_specs=out_spe...  66.2 us
    pallas_call x2, Pallas kernels, attend(): pl.pallas_call(lambda *refs: fwd_kernel(n_blk, groups, dim, first, *refs)...  60.5 us
    ppermute x6, waiting for transfers between devices, exchange(): return lax.ppermute(a, 'tp', swap)  36.2 us
    all_to_all x1, blocking collectives, switch(): return lax.all_to_all(a, 'cp', split_axis=0, concat_axis=0, tiled=True)  24.5 us
    all_to_all x6, starting transfers between devices, switch(): return lax.all_to_all(a, 'cp', split_axis=0, concat_axis=0, tiled=True)  24.3 us
    ppermute x6, starting transfers between devices, exchange(): return lax.ppermute(a, 'tp', swap)  8.89 us
  transfers between devices with their start and end apart: 15, of which 9 were waited for; matrix products, arithmetic and copies ran while one was open for 5% of the time, Pallas kernels for 49%

profile of v5, /device:TPU:0, one launch (start us, length us, event | category | flops | bytes accessed | tf_op | source)
XLA Modules:
  0.0 435.1 jit_solution(6970712883074084575)
XLA Ops:
  13.1 6.0 %pad_maximum_fusion = bf16[4,384,2048]{2,1,0:T(8,128)(2,1)} fusion(bf16[4,64,2048]{2,1,0:T(8,128)(2,1)S(1)} %bitcast.31, bf16[4,64,2048]{2,1,0:T(8,128)(2,1)S(1)} %bitcast.32, bf16[4,256,2048]{2,1,0:T(8,128)(2,1)S(1)} %bitcast.22), kind=kLoop, calls=%fused_computation | loop fusion | flops 18874368 | bytes 12582912 | tf_op jit(solution)/shard_map/concatenate | solution.py:391
  19.1 8.3 %shard_map.109 = bf16[4,512,384]{2,1,0:T(8,128)(2,1)} custom-call(bf16[512,2048]{1,0:T(8,128)(2,1)} %x_ref.1, bf16[1536,2048]{1,0:T(8,128)(2,1)} %bitcast.23), custom_call_target="tpu_custom_call" | custom-call | flops 3221225472 | bytes 8388608 | tf_op jit(solution)/shard_map/pallas_call | solution.py:288
  36.0 14.9 %all-to-all-done.refs_0_.refs_2_ = bf16[4,512,384]{2,1,0:T(8,128)(2,1)S(1)} async-done(((bf16[4,512,384]{2,1,0:T(8,128)(2,1)}), bf16[4,512,384]{2,1,0:T(8,128)(2,1)S(1)}, u32[]{:S(2)}, u32[]{:S(2)}) %all-to-all-start) | async-done | bytes 1572896 | tf_op jit(solution)/shard_map/all_to_all | solution.py:399
  50.9 5.5 %collective-permute-done.a_ref.xp_ref = bf16[512,2048]{1,0:T(8,128)(2,1)} collective-permute-done((bf16[512,2048]{1,0:T(8,128)(2,1)}, bf16[512,2048]{1,0:T(8,128)(2,1)}, u32[]{:S(2)}, u32[]{:S(2)}) %collective-permute-start) | collective-permute-done | bytes 2097184 | tf_op jit(solution)/shard_map/ppermute | solution.py:396
  56.6 8.5 %shard_map.110 = bf16[4,512,384]{2,1,0:T(8,128)(2,1)} custom-call(bf16[512,2048]{1,0:T(8,128)(2,1)} %collective-permute-done.a_ref.xp_ref, bf16[1536,2048]{1,0:T(8,128)(2,1)} %bitcast.25), custom_call_target="tpu_custom_call" | custom-call | flops 3221225472 | bytes 8388608 | tf_op jit(solution)/shard_map/pallas_call | solution.py:288
  65.1 24.5 %all_to_all.35.refs_1_.refs_3_ = bf16[4,512,384]{2,1,0:T(8,128)(2,1)} all-to-all(bf16[4,512,384]{2,1,0:T(8,128)(2,1)} %shard_map.110), channel_id=1, replica_groups=mesh['dp'=1,'tp'=2,'cp'=4] {'cp'}, dimensions={0} | all-to-all | bytes 3145728 | tf_op jit(solution)/shard_map/all_to_all | solution.py:399
  89.6 17.4 %attend_fwd.2 = (bf16[4,256,1024]{2,1,0:T(8,128)(2,1)}, f32[8,4,512]{2,1,0:T(4,128)}) custom-call(bf16[4,512,384]{2,1,0:T(8,128)(2,1)} %copy-done.3, bf16[4,512,384]{2,1,0:T(8,128)(2,1)} %all_to_all.35.refs_1_.refs_3_, bf16[4,512,384]{2,1,0:T(8,128)(2,1)} %copy-done.3, bf16[4,512,384]{2,1,0:T(8,128)(2,1)} %all_to_all.35.refs_1_.refs_3_), custom_call_target="tpu_custom_call" | custom-call | flops 10737418240 | bytes 2097152 | tf_op jit(solution)/shard_map/attend_fwd/pallas_call | solution.py:228
  107.0 4.8 %all-gather.4.cloned.1.call-done.a_ref.b_ref = bf16[1024,2048]{1,0:T(8,128)(2,1)} async-done(((bf16[512,2048]{1,0:T(8,128)(2,1)}), bf16[1024,2048]{1,0:T(8,128)(2,1)}) %all-gather.4.cloned.1.call-update) | async-done | bytes 4194320 | tf_op jit(solution)/shard_map/all_gather | solution.py:416
  113.8 43.1 %attend_fwd.3 = (bf16[4,256,1024]{2,1,0:T(8,128)(2,1)}, f32[8,4,512]{2,1,0:T(4,128)}) custom-call(bf16[4,512,384]{2,1,0:T(8,128)(2,1)} %copy-done.3, bf16[4,512,384]{2,1,0:T(8,128)(2,1)} %all_to_all.35.refs_1_.refs_3_, bf16[4,512,384]{2,1,0:T(8,128)(2,1)} %copy-done.3, ...), custom_call_target="tpu_custom_call", output_to_operand_aliasing={{0}: (4, {}), {1}: (5, {})} | custom-call | flops 27917287424 | bytes 2097152 | tf_op jit(solution)/shard_map/attend_fwd/pallas_call | solution.py:228
  157.0 13.4 %collective-permute-done.1 = bf16[256,2048]{1,0:T(8,128)(2,1)} collective-permute-done((bf16[256,2048]{1,0:T(8,128)(2,1)S(1)}, bf16[256,2048]{1,0:T(8,128)(2,1)}, u32[]{:S(2)}, u32[]{:S(2)}) %collective-permute-start.1) | collective-permute-done | bytes 1048608 | tf_op jit(solution)/shard_map/ppermute | solution.py:396
  170.4 8.9 %shard_map.111 = bf16[4,1024,256]{2,1,0:T(8,128)(2,1)} custom-call(bf16[1024,2048]{1,0:T(8,128)(2,1)} %all-gather.4.cloned.1.call-done.a_ref.b_ref, bf16[1024,2048]{1,0:T(8,128)(2,1)} %bitcast.34), custom_call_target="tpu_custom_call" | custom-call | flops 4294967296 | bytes 8388608 | tf_op jit(solution)/shard_map/pallas_call | solution.py:288
  183.6 39.5 %all-to-all-done.2 = bf16[4,1024,256]{2,1,0:T(8,128)(2,1)S(1)} async-done(((bf16[4,1024,256]{2,1,0:T(8,128)(2,1)}), bf16[4,1024,256]{2,1,0:T(8,128)(2,1)S(1)}, u32[]{:S(2)}, u32[]{:S(2)}) %all-to-all-start.2) | async-done | bytes 2097184 | tf_op jit(solution)/shard_map/all_to_all | solution.py:399
  224.4 3.9 all-to-all-start.3
  228.3 70.0 %attend_bwd.2 = (bf16[4,384,512]{2,1,0:T(8,128)(2,1)}, f32[4,64,512]{2,1,0:T(8,128)}, f32[4,512,64]{2,1,0:T(8,128)}) custom-call(bf16[4,512,384]{2,1,0:T(8,128)(2,1)} %copy-done.3, bf16[4,512,384]{2,1,0:T(8,128)(2,1)} %all_to_all.35.refs_1_.refs_3_, bf16[4,512,384]{2,1,0:T(8,128)(2,1)} %copy-done.3, bf16[4,512,384]{2,1,0:T(8,128)(2,1)} %all_to_all.35.refs_1_.refs_3_, ...), custom_call_target="tpu_custom_call" | custom-call | flops 69793218560 | bytes 4194304 | tf_op jit(solution)/shard_map/attend_bwd/pallas_call | solution.py:261
  298.3 28.2 %attend_bwd.3 = bf16[4,384,512]{2,1,0:T(8,128)(2,1)} custom-call(bf16[4,512,384]{2,1,0:T(8,128)(2,1)} %copy-done.3, bf16[4,512,384]{2,1,0:T(8,128)(2,1)} %all_to_all.35.refs_1_.refs_3_, bf16[4,512,384]{2,1,0:T(8,128)(2,1)} %copy-done.3, bf16[4,512,384]{2,1,0:T(8,128)(2,1)} %all_to_all.35.refs_1_.refs_3_, bf16[8,512,256]{2,1,0:T(8,128)(2,1)} %bitcast.30, ...), custom_call_target="tpu_custom_call" | custom-call | flops 26843545600 | bytes 4194304 | tf_op jit(solution)/shard_map/attend_bwd/pallas_call | solution.py:261
  326.6 4.4 %all-to-all-start.4 = ((bf16[4,384,512]{2,1,0:T(8,128)(2,1)}), bf16[4,384,512]{2,1,0:T(8,128)(2,1)}, u32[]{:S(2)}, u32[]{:S(2)}) async-start(bf16[4,384,512]{2,1,0:T(8,128)(2,1)} %attend_bwd.3), calls=%async_computation.4 | async-start | bytes 3145728 | tf_op jit(solution)/shard_map/all_to_all | solution.py:399
  331.0 20.1 %all-to-all-done.4 = bf16[4,384,512]{2,1,0:T(8,128)(2,1)} async-done(((bf16[4,384,512]{2,1,0:T(8,128)(2,1)}), bf16[4,384,512]{2,1,0:T(8,128)(2,1)}, u32[]{:S(2)}, u32[]{:S(2)}) %all-to-all-start.4) | async-done | bytes 1572896 | tf_op jit(solution)/shard_map/all_to_all | solution.py:399
  351.1 4.3 all-to-all-start.5
  360.7 8.6 %shard_map.115 = bf16[1024,2048]{1,0:T(8,128)(2,1)} custom-call(bf16[1024,1024]{1,0:T(8,128)(2,1)} %bitcast.28, bf16[1024,2048]{1,0:T(8,128)(2,1)} %all-gather.4.cloned.1.call-done.a_ref.b_ref), custom_call_target="tpu_custom_call" | custom-call | flops 4294967296 | bytes 6291456 | tf_op jit(solution)/shard_map/pallas_call | solution.py:288
  369.2 14.0 %collective-permute-done.4 = bf16[4,256,512]{2,1,0:T(8,128)(2,1)} collective-permute-done((bf16[4,256,512]{2,1,0:T(8,128)(2,1)S(1)}, bf16[4,256,512]{2,1,0:T(8,128)(2,1)}, u32[]{:S(2)}, u32[]{:S(2)}) %collective-permute-start.4) | collective-permute-done | bytes 1048608 | tf_op jit(solution)/shard_map/ppermute | solution.py:396
  383.2 4.5 %all-to-all-start.6 = ((bf16[4,256,512]{2,1,0:T(8,128)(2,1)}), bf16[4,256,512]{2,1,0:T(8,128)(2,1)}, u32[]{:S(2)}, u32[]{:S(2)}) async-start(bf16[4,256,512]{2,1,0:T(8,128)(2,1)} %collective-permute-done.4), calls=%async_computation.6 | async-start | bytes 2097152 | tf_op jit(solution)/shard_map/all_to_all | solution.py:399
  393.3 10.5 %shard_map.114 = (bf16[1024,2048]{1,0:T(8,128)(2,1)}, bf16[256,2048]{1,0:T(8,128)(2,1)}, bf16[256,2048]{1,0:T(8,128)(2,1)}) custom-call(bf16[4,384,512]{2,1,0:T(8,128)(2,1)} %get-tuple-element.61.refs_0_.g_ref, bf16[512,2048]{1,0:T(8,128)(2,1)} %x_ref.1, bf16[4,384,512]{2,1,0:T(8,128)(2,1)} %copy-done.1, bf16[512,2048]{1,0:T(8,128)(2,1)} %collective-permute-done.a_ref.xp_ref), custom_call_target="tpu_custom_call" | custom-call | flops 6442450944 | bytes 7340032 | tf_op jit(solution)/shard_map/pallas_call | solution.py:288
  405.7 9.3 %shard_map.112 = bf16[512,2048]{1,0:T(8,128)(2,1)} custom-call(bf16[1,1024,512]{2,1,0:T(8,128)(2,1)} %get-tuple-element.63.refs_0_, bf16[1,1024,512]{2,1,0:T(8,128)(2,1)} %bitcast.9.refs_1_, bf16[1024,2048]{1,0:T(8,128)(2,1)} %bitcast.35, bf16[1024,2048]{1,0:T(8,128)(2,1)} %all-gather.6.cloned.1.call-done.refs_3_), custom_call_target="tpu_custom_call" | custom-call | flops 4294967296 | bytes 10485760 | tf_op jit(solution)/shard_map/pallas_call | solution.py:288
  416.4 12.1 %shard_map.113 = bf16[512,2048]{1,0:T(8,128)(2,1)} custom-call(bf16[4,384,512]{2,1,0:T(8,128)(2,1)} %get-tuple-element.61.refs_0_.g_ref, bf16[4,256,512]{2,1,0:T(8,128)(2,1)} %all-to-all-done.6.refs_1_, bf16[4,128,512]{2,1,0:T(8,128)(2,1)} %collective-permute-done.5.refs_2_, bf16[1536,2048]{1,0:T(8,128)(2,1)} %bitcast.26, ...), custom_call_target="tpu_custom_call" | custom-call | flops 6442450944 | bytes 15728640 | tf_op jit(solution)/shard_map/pallas_call | solution.py:288
  (45 shorter events, 36.5 us)
Async XLA Ops:
  7.2 5.9 %copy-start.5 = (bf16[2048,4,64]{0,2,1:T(8,128)(2,1)S(1)}, bf16[2048,4,64]{0,2,1:T(8,128)(2,1)}, u32[]{:S(2)}) copy-start(bf16[2048,4,64]{0,2,1:T(8,128)(2,1)} %param.9) | copy-start | bytes 3145732
  7.2 5.9 %copy-start.6 = (bf16[2048,4,64]{0,2,1:T(8,128)(2,1)S(1)}, bf16[2048,4,64]{0,2,1:T(8,128)(2,1)}, u32[]{:S(2)}) copy-start(bf16[2048,4,64]{0,2,1:T(8,128)(2,1)} %param.8) | copy-start | bytes 3145732
  7.2 49.3 %collective-permute-start = (bf16[512,2048]{1,0:T(8,128)(2,1)}, bf16[512,2048]{1,0:T(8,128)(2,1)}, u32[]{:S(2)}, u32[]{:S(2)}) collective-permute-start(bf16[512,2048]{1,0:T(8,128)(2,1)} %x_ref.1), channel_id=1, source_target_pairs={{0,4},{4,0},{1,5},{5,1},{2,6},{6,2},{3,7},{7,3}} | collective-permute-start | bytes 6291464 | tf_op jit(solution)/shard_map/ppermute | solution.py:396
  27.4 23.6 %all-to-all-start = ((bf16[4,512,384]{2,1,0:T(8,128)(2,1)}), bf16[4,512,384]{2,1,0:T(8,128)(2,1)S(1)}, u32[]{:S(2)}, u32[]{:S(2)}) async-start(bf16[4,512,384]{2,1,0:T(8,128)(2,1)} %shard_map.109), calls=%async_computation | async-start | bytes 3145728 | tf_op jit(solution)/shard_map/all_to_all | solution.py:399
  30.9 80.9 %all-gather.4.cloned.1.call-start = ((), (), s32[]{:S(2)}) async-start(), calls=%async_computation.7 | async-start | bytes 6291456 | tf_op jit(solution)/shard_map/all_gather | solution.py:416
  50.9 14.2 %copy-start.3 = (bf16[4,512,384]{2,1,0:T(8,128)(2,1)}, bf16[4,512,384]{2,1,0:T(8,128)(2,1)S(1)}, u32[]{:S(2)}) copy-start(bf16[4,512,384]{2,1,0:T(8,128)(2,1)S(1)} %all-to-all-done.refs_0_.refs_2_) | copy-start | bytes 4718596
  56.5 349.2 %all-gather.6.cloned.1.call-start = ((), (), s32[]{:S(2)}) async-start(), calls=%async_computation.8 | async-start | bytes 5242880 | tf_op jit(solution)/shard_map/all_gather | solution.py:409
  89.6 22.2 %copy-start.4 = (bf16[384,2048]{1,0:T(8,128)(2,1)S(1)}, bf16[384,2048]{1,0:T(8,128)(2,1)}, u32[]{:S(2)}) copy-start(bf16[384,2048]{1,0:T(8,128)(2,1)} %constant_dynamic-slice_fusion.2) | copy-start | bytes 4718596
  89.6 22.6 %copy-start.7 = (bf16[256,2048]{1,0:T(8,128)(2,1)S(1)}, bf16[256,2048]{1,0:T(8,128)(2,1)}, u32[]{:S(2)}) copy-start(bf16[256,2048]{1,0:T(8,128)(2,1)} %constant_dynamic-slice_fusion.1) | copy-start | bytes 3145732
  111.8 58.5 %collective-permute-start.2 = (bf16[384,2048]{1,0:T(8,128)(2,1)S(1)}, bf16[384,2048]{1,0:T(8,128)(2,1)}, u32[]{:S(2)}, u32[]{:S(2)}) collective-permute-start(bf16[384,2048]{1,0:T(8,128)(2,1)S(1)} %copy-done.4), channel_id=1, source_target_pairs={{0,4},{4,0},{1,5},{5,1},{2,6},{6,2},{3,7},{7,3}} | collective-permute-start | bytes 4718600 | tf_op jit(solution)/shard_map/ppermute | solution.py:396
  112.2 58.2 %collective-permute-start.1 = (bf16[256,2048]{1,0:T(8,128)(2,1)S(1)}, bf16[256,2048]{1,0:T(8,128)(2,1)}, u32[]{:S(2)}, u32[]{:S(2)}) collective-permute-start(bf16[256,2048]{1,0:T(8,128)(2,1)S(1)} %copy-done.7), channel_id=1, source_target_pairs={{0,4},{4,0},{1,5},{5,1},{2,6},{6,2},{3,7},{7,3}} | collective-permute-start | bytes 3145736 | tf_op jit(solution)/shard_map/ppermute | solution.py:396
  179.3 43.8 %all-to-all-start.2 = ((bf16[4,1024,256]{2,1,0:T(8,128)(2,1)}), bf16[4,1024,256]{2,1,0:T(8,128)(2,1)S(1)}, u32[]{:S(2)}, u32[]{:S(2)}) async-start(bf16[4,1024,256]{2,1,0:T(8,128)(2,1)} %shard_map.111), calls=%async_computation.2 | async-start | bytes 4194304 | tf_op jit(solution)/shard_map/all_to_all | solution.py:399
  182.9 233.5 %all-gather.8.cloned.1.call-start = ((), (), s32[]{:S(2)}) async-start(), calls=%async_computation.9 | async-start | bytes 7864320 | tf_op jit(solution)/shard_map/all_gather | solution.py:409
  223.1 1.3 copy-start.2
  224.4 102.1 %all-to-all-start.3 = ((bf16[4,256,1024]{2,1,0:T(8,128)(2,1)}), bf16[4,256,1024]{2,1,0:T(8,128)(2,1)S(1)}, u32[]{:S(2)}, u32[]{:S(2)}) async-start(bf16[4,256,1024]{2,1,0:T(8,128)(2,1)} %get-tuple-element.48.refs_5_), calls=%async_computation.3 | async-start | bytes 4194304 | tf_op jit(solution)/shard_map/all_to_all | solution.py:399
  326.5 32.0 %copy-start = (bf16[4,256,1024]{2,1,0:T(8,128)(2,1)}, bf16[4,256,1024]{2,1,0:T(8,128)(2,1)S(1)}, u32[]{:S(2)}) copy-start(bf16[4,256,1024]{2,1,0:T(8,128)(2,1)S(1)} %all-to-all-done.3) | copy-start | bytes 6291460
  326.6 24.5 %all-to-all-start.4 = ((bf16[4,384,512]{2,1,0:T(8,128)(2,1)}), bf16[4,384,512]{2,1,0:T(8,128)(2,1)}, u32[]{:S(2)}, u32[]{:S(2)}) async-start(bf16[4,384,512]{2,1,0:T(8,128)(2,1)} %attend_bwd.3), calls=%async_computation.4 | async-start | bytes 3145728 | tf_op jit(solution)/shard_map/all_to_all | solution.py:399
  351.1 32.2 %all-to-all-start.5 = ((bf16[4,384,512]{2,1,0:T(8,128)(2,1)}), bf16[4,384,512]{2,1,0:T(8,128)(2,1)}, u32[]{:S(2)}, u32[]{:S(2)}) async-start(bf16[4,384,512]{2,1,0:T(8,128)(2,1)} %get-tuple-element.55), calls=%async_computation.5 | async-start | bytes 3145728 | tf_op jit(solution)/shard_map/all_to_all | solution.py:399
  357.1 26.2 %collective-permute-start.4 = (bf16[4,256,512]{2,1,0:T(8,128)(2,1)S(1)}, bf16[4,256,512]{2,1,0:T(8,128)(2,1)}, u32[]{:S(2)}, u32[]{:S(2)}) collective-permute-start(bf16[4,256,512]{2,1,0:T(8,128)(2,1)S(1)} %slice_select_fusion), channel_id=1, source_target_pairs={{0,4},{4,0},{1,5},{5,1},{2,6},{6,2},{3,7},{7,3}} | collective-permute-start | bytes 3145736 | tf_op jit(solution)/shard_map/ppermute | solution.py:396
  360.1 45.6 %collective-permute-start.3 = (bf16[1024,512]{1,0:T(8,128)(2,1)}, bf16[1024,512]{1,0:T(8,128)(2,1)}, u32[]{:S(2)}, u32[]{:S(2)}) collective-permute-start(bf16[1024,512]{1,0:T(8,128)(2,1)} %get-tuple-element.62), channel_id=1, source_target_pairs={{0,4},{4,0},{1,5},{5,1},{2,6},{6,2},{3,7},{7,3}} | collective-permute-start | bytes 3145736 | tf_op jit(solution)/shard_map/ppermute | solution.py:396
  383.2 33.2 %all-to-all-start.6 = ((bf16[4,256,512]{2,1,0:T(8,128)(2,1)}), bf16[4,256,512]{2,1,0:T(8,128)(2,1)}, u32[]{:S(2)}, u32[]{:S(2)}) async-start(bf16[4,256,512]{2,1,0:T(8,128)(2,1)} %collective-permute-done.4), calls=%async_computation.6 | async-start | bytes 2097152 | tf_op jit(solution)/shard_map/all_to_all | solution.py:399
  391.0 2.4 copy-start.1
  391.9 24.5 %collective-permute-start.5 = (bf16[4,128,512]{2,1,0:T(8,128)(2,1)}, bf16[4,128,512]{2,1,0:T(8,128)(2,1)}, u32[]{:S(2)}, u32[]{:S(2)}) collective-permute-start(bf16[4,128,512]{2,1,0:T(8,128)(2,1)} %slice.13), channel_id=1, source_target_pairs={{0,4},{4,0},{1,5},{5,1},{2,6},{6,2},{3,7},{7,3}} | collective-permute-start | bytes 1572872 | tf_op jit(solution)/shard_map/ppermute | solution.py:396
Sparse Core Ops, SparseCore 0:
  56.6 55.1 all-gather.3
  170.5 46.2 all-gather.5
  218.4 67.2 all-gather.7

commit v6 on v5

--- a/solution.py
+++ b/solution.py
@@ -16,6 +16,7 @@
 VMEM_LIMIT = 60 * 1024 * 1024
 DENSE_LIMIT = 62 * 1024 * 1024
 DENSE_TILES = 4
+FWD_CUT = 5
 FWD_SPLIT, FWD_AHEAD, FWD_BEHIND = 256, 2, 1
 BWD_SPLIT, BWD_AHEAD, BWD_BEHIND = 256, 1, 0
 
@@ -28,39 +29,37 @@
     return jnp.where(pos_blk < n_blk // 2, pos_blk, n_blk - 1 - pos_blk)
 
 
-def stored_block(pos_blk, n_blk):
-    return 2 * shard_of(pos_blk, n_blk) + half_of(pos_blk, n_blk)
-
-
 def keep_mask(shape, col=0):
     return lax.broadcasted_iota(jnp.int32, shape, 0) <= lax.broadcasted_iota(jnp.int32, shape, 1) + col
 
 
-def load_keys(n_blk, own_ref, other_ref, kv_s, kvt_s):
+def load_keys(n_blk, own_ref, head_ref, tail_ref, kv_s, kvt_s):
     own_half = lax.axis_index("tp")
     for b in range(n_blk):
         half, shard = (0, b) if b < n_blk // 2 else (1, n_blk - 1 - b)
-        block = jnp.where(own_half == half, own_ref[shard], other_ref[shard])
+        other = jnp.concatenate([head_ref[shard], tail_ref[shard]], axis=0)
+        block = jnp.where(own_half == half, own_ref[shard], other)
         kv_s[b] = block
         kvt_s[b] = block.T
 
 
-def load_queries(n_blk, pos, own_ref, other_ref):
-    return jnp.where(lax.axis_index("tp") == half_of(pos, n_blk), own_ref[...], other_ref[...])
+def load_rows(n_blk, pos, own_ref, *other_refs):
+    other = jnp.concatenate([ref[...] for ref in other_refs], axis=0)
+    return jnp.where(lax.axis_index("tp") == half_of(pos, n_blk), own_ref[...], other)
 
 
 def fwd_kernel(n_blk, groups, dim, first, *refs):
-    q_own, q_other, kv_own, kv_other = refs[:4]
+    q_refs, key_refs = refs[:3], refs[3:6]
     o_ref, lse_ref, kv_s, kvt_s, rq_s, acc_s, m_s, l_s = refs[-8:]
     pos = first + pl.program_id(0)
-    blk = q_own.shape[0]
+    blk = q_refs[0].shape[0]
 
     @pl.when(pl.program_id(0) == 0)
     def _():
-        load_keys(n_blk, kv_own, kv_other, kv_s, kvt_s)
+        load_keys(n_blk, *key_refs, kv_s, kvt_s)
         rq_s[...] = jnp.zeros_like(rq_s)
 
-    q_t = load_queries(n_blk, pos, q_own, q_other).T
+    q_t = load_rows(n_blk, pos, *q_refs).T
     for h in range(groups):
         rq_s[h, :dim, :] = q_t[h * dim:(h + 1) * dim, :]
 
@@ -116,25 +115,25 @@
 
 
 def bwd_kernel(n_blk, groups, dim, first, count, *refs):
-    q_own, q_other, kv_own, kv_other, do_ref, o_ref, lse_ref = refs[:7]
+    q_refs, key_refs, do_refs, (o_ref, lse_ref) = refs[:3], refs[3:6], refs[6:8], refs[8:10]
     upper = first > 0
-    g_ref = refs[7 if upper else 9]
+    g_ref = refs[10 if upper else 12]
     kv_s, kvt_s, rq_s, rd_s, rdo_s, dot_s, dqt_s, dk_s, dv_s = refs[-9:]
     step = pl.program_id(0)
     pos = first + step
-    blk = do_ref.shape[0]
+    blk = do_refs[0].shape[0]
     cols = groups * dim
 
     @pl.when(step == 0)
     def _():
-        load_keys(n_blk, kv_own, kv_other, kv_s, kvt_s)
+        load_keys(n_blk, *key_refs, kv_s, kvt_s)
         rq_s[...] = jnp.zeros_like(rq_s)
         rd_s[...] = jnp.zeros_like(rd_s)
-        dk_s[...] = jnp.zeros_like(dk_s) if upper else refs[7][...]
-        dv_s[...] = jnp.zeros_like(dv_s) if upper else refs[8][...]
-
-    q = load_queries(n_blk, pos, q_own, q_other)
-    do = do_ref[...]
+        dk_s[...] = jnp.zeros_like(dk_s) if upper else refs[10][...]
+        dv_s[...] = jnp.zeros_like(dv_s) if upper else refs[11][...]
+
+    q = load_rows(n_blk, pos, *q_refs)
+    do = load_rows(n_blk, pos, *do_refs)
     q_t = q.T
     do_t = do.T
     for h in range(groups):
@@ -204,15 +203,16 @@
             g_ref[s, cols:cols + dim, :] = dk_s[b].astype(BF16)
             g_ref[s, cols + dim:, :] = dv_s[b].T.astype(BF16)
         if upper:
-            refs[8][...] = dk_s[:first]
-            refs[9][...] = dv_s[:first]
+            refs[11][...] = dk_s[:first]
+            refs[12][...] = dv_s[:first]
 
 
 def key_specs(n_half, blk, groups, dim, first):
     cols = groups * dim
-    query = pl.BlockSpec((None, blk, cols), lambda i: (shard_of(first + i, 2 * n_half), 0, 0))
-    keys = pl.BlockSpec((n_half, blk, 2 * dim), lambda i: (0, 0, cols // (2 * dim)))
-    return [query, query, keys, keys]
+    sizes = (blk, blk // 2, blk // 2)
+    queries = [pl.BlockSpec((None, n, cols), lambda i: (shard_of(first + i, 2 * n_half), 0, 0)) for n in sizes]
+    keys = [pl.BlockSpec((n_half, n, 2 * dim), lambda i: (0, 0, cols // (2 * dim))) for n in sizes]
+    return queries + keys
 
 
 def feature_spec(n_blk, cols, blk, first):
@@ -231,7 +231,7 @@
         in_specs=key_specs(n_half, blk, groups, dim, first) + [pl.BlockSpec(memory_space=pl.ANY)] * len(prev),
         out_specs=[feature_spec(n_blk, cols, blk, first), pl.BlockSpec((None, groups, blk), lambda i: (first + i, 0, 0))],
         out_shape=out_shape,
-        input_output_aliases={4 + i: i for i in range(len(prev))},
+        input_output_aliases={6 + i: i for i in range(len(prev))},
         scratch_shapes=[
             pltpu.VMEM((n_blk, blk, 2 * dim), BF16),
             pltpu.VMEM((n_blk, 2 * dim, blk), BF16),
@@ -243,7 +243,7 @@
         compiler_params=pltpu.CompilerParams(dimension_semantics=("arbitrary",), vmem_limit_bytes=VMEM_LIMIT),
         cost_estimate=pl.CostEstimate(flops=elems * 4 * 4 * dim, bytes_accessed=count * blk * cols * 4, transcendentals=elems),
         name="attend_fwd",
-    )(own, other, own, other, *prev)
+    )(own, *other, own, *other, *prev)
 
 
 def attend_grad(own, other, do, o, lse, carried, first, count, groups, dim):
@@ -262,7 +262,8 @@
         lambda *refs: bwd_kernel(n_blk, groups, dim, first, count, *refs),
         grid=(count,),
         in_specs=key_specs(n_half, blk, groups, dim, first) + [
-            pl.BlockSpec((None, blk, cols), lambda i: (stored_block(first + i, n_blk), 0, 0)),
+            pl.BlockSpec((None, blk, cols), lambda i: (shard_of(first + i, n_blk), 0, 0)),
+            pl.BlockSpec((None, blk, cols), lambda i: (shard_of(first + i, n_blk), 0, 0)),
             feature_spec(n_blk, cols, blk, first),
             pl.BlockSpec((None, groups, blk), lambda i: (first + i, 0, 0))] + whole * (len(carried) > 0),
         out_specs=out_specs,
@@ -281,7 +282,7 @@
         compiler_params=pltpu.CompilerParams(dimension_semantics=("arbitrary",), vmem_limit_bytes=VMEM_LIMIT),
         cost_estimate=pl.CostEstimate(flops=elems * 10 * 4 * dim, bytes_accessed=count * blk * cols * 8, transcendentals=elems),
         name="attend_bwd",
-    )(own, other, own, other, do, o, lse, *carried)
+    )(own, *other, own, *other, *do, o, lse, *carried)
 
 
 def dense_call(kernel, grid, in_specs, out_specs, out_shape, scratch, flops, args):
@@ -305,16 +306,19 @@
                       jax.ShapeDtypeStruct((parts, count, width), BF16), [], 2 * count * depth * width * parts, (rows, weight))
 
 
-def product(a, b, tiles):
+def product(a, b, a_peer, b_peer, tiles):
     count = a.shape[0] // tiles
 
-    def kernel(a_ref, b_ref, o_ref):
-        o_ref[...] = jnp.dot(a_ref[...], b_ref[...], preferred_element_type=F32).astype(BF16)
-
-    return dense_call(kernel, tiles,
-                      [pl.BlockSpec((count, a.shape[1]), lambda i: (i, 0)), pl.BlockSpec(b.shape, lambda i: (0, 0))],
+    def kernel(a_ref, b_ref, ap_ref, bp_ref, o_ref):
+        total = jnp.dot(a_ref[...], b_ref[...], preferred_element_type=F32)
+        o_ref[...] = (total + jnp.dot(ap_ref[...], bp_ref[...], preferred_element_type=F32)).astype(BF16)
+
+    a_spec = pl.BlockSpec((count, a.shape[1]), lambda i: (i, 0))
+    b_spec = pl.BlockSpec(b.shape, lambda i: (0, 0))
+    return dense_call(kernel, tiles, [a_spec, b_spec, a_spec, b_spec],
                       pl.BlockSpec((count, b.shape[1]), lambda i: (i, 0)),
-                      jax.ShapeDtypeStruct((a.shape[0], b.shape[1]), BF16), [], 2 * a.size * b.shape[1], (a, b))
+                      jax.ShapeDtypeStruct((a.shape[0], b.shape[1]), BF16), [], 4 * a.size * b.shape[1],
+                      (a, b, a_peer, b_peer))
 
 
 def combine(own, w, peer, w_peer, tiles):
@@ -347,14 +351,15 @@
                       4 * count * depth * w.shape[1], (*pieces, w, w_peer))
 
 
-def weight_grads(g, x, g_peer, x_peer, cols, dim, scale):
+def weight_grads(g, x, g_peer, x_peers, cols, dim, scale):
     heads, feats, count = g.shape
     model = x.shape[1]
 
-    def kernel(g_ref, x_ref, gp_ref, xp_ref, q_ref, k_ref, v_ref):
+    def kernel(g_ref, x_ref, gp_ref, xa_ref, xb_ref, q_ref, k_ref, v_ref):
         def part(lo, hi):
             total = jnp.dot(g_ref[lo:hi, :], x_ref[...], preferred_element_type=F32)
-            return total + jnp.dot(gp_ref[lo:hi, :], xp_ref[...], preferred_element_type=F32)
+            total += jnp.dot(gp_ref[lo:hi, :count // 2], xa_ref[...], preferred_element_type=F32)
+            return total + jnp.dot(gp_ref[lo:hi, count // 2:], xb_ref[...], preferred_element_type=F32)
 
         q_ref[...] = (part(0, cols) * scale).astype(BF16)
         both = part(cols, feats).astype(BF16)
@@ -363,11 +368,12 @@
 
     g_spec = pl.BlockSpec((None, feats, count), lambda i: (i, 0, 0))
     x_spec = pl.BlockSpec((count, model), lambda i: (0, 0))
+    half_spec = pl.BlockSpec((count // 2, model), lambda i: (0, 0))
     sizes = (cols, dim, dim)
-    return dense_call(kernel, heads, [g_spec, x_spec, g_spec, x_spec],
+    return dense_call(kernel, heads, [g_spec, x_spec, g_spec, half_spec, half_spec],
                       [pl.BlockSpec((n, model), lambda i: (i, 0)) for n in sizes],
                       [jax.ShapeDtypeStruct((heads * n, model), BF16) for n in sizes], [],
-                      4 * heads * feats * count * model, (g, x, g_peer, x_peer))
+                      4 * heads * feats * count * model, (g, x, g_peer, *x_peers))
 
 
 def solution(mesh):
@@ -408,29 +414,44 @@
         def spread(w):
             return lax.all_gather(w, "cp", axis=0, tiled=True)
 
-        x_peer = exchange(x_blk)
-        own = switch(project(x_blk, w_flat, kv_heads))
+        half = half_rows // 2
+        x_head = exchange(x_blk[:half])
+        x_tail = exchange(x_blk[half:])
+        own = project(x_blk, w_flat, kv_heads)
+        x_head, own = after(x_head, own)
+        own = switch(own)
+        head = project(x_head, w_flat, kv_heads)
+        head, own = after(head, own)
+        dy_first, head = after(dy_blk, head)
+        do_own = project(dy_first, wo, kv_heads)
+        head = switch(head)
         pieces = (quarter_of(w_flat), quarter_of(wo))
-        (x_peer, pieces), own = after((x_peer, pieces), own)
-        dy_late, x_peer = after(dy_blk, x_peer)
-        dy_rows = lax.all_gather(dy_late, "tp", axis=0, tiled=True)
-        other = switch(project(x_peer, w_flat, kv_heads))
-
-        partial = attend(own, other, (), 0, n_half, groups, dim)
-        dy_rows, pieces = after(dy_rows, pieces)
-        wo_quarter, w_quarter = exchange(pieces[1]), exchange(pieces[0])
-        dy_ready, partial = after(dy_rows, partial)
-        do_own = project(dy_ready, wo, kv_heads)
-        do_all = switch(do_own).reshape(n_blk, half_rows, cols)
-        o_all, lse = attend(own, other, partial, n_half, n_half, groups, dim)
-        (wo_quarter, w_quarter), o_all = after((wo_quarter, w_quarter), o_all)
-        wo_peer, w_peer = spread(wo_quarter), spread(w_quarter)
+        x_tail, (do_own, pieces) = after(x_tail, (do_own, pieces))
+        dy_late, x_tail = after(dy_blk, x_tail)
+        dy_peer = exchange(dy_late)
+        tail = project(x_tail, w_flat, kv_heads)
+        tail, head = after(tail, head)
+        other = (head, switch(tail))
+        do_own = switch(after(do_own, other[1])[0])
+
+        partial = attend(own, other, (), 0, FWD_CUT, groups, dim)
+        (dy_peer, pieces), partial = after((dy_peer, pieces), partial)
+        w_quarter, wo_quarter = exchange(pieces[0]), exchange(pieces[1])
+        do_other = project(dy_peer, wo, kv_heads)
+        do_other, do_own = after(do_other, do_own)
+        do_all = (do_own, switch(do_other))
+        o_all, lse = attend(own, other, partial, FWD_CUT, n_blk - FWD_CUT, groups, dim)
+        w_quarter, o_all = after(w_quarter, o_all)
+        w_peer = spread(w_quarter)
 
         o_own = switch(o_all).reshape(q_cols, 2 * half_rows)
         g_upper, *carried = attend_grad(own, other, do_all, o_all, lse, (), n_half, n_half, groups, dim)
         g_upper, o_own = after(g_upper, o_own)
+        (wo_quarter, w_peer), g_upper = after((wo_quarter, w_peer), g_upper)
+        wo_peer = spread(wo_quarter)
         o_mine = lax.dynamic_slice_in_dim(o_own, mine * half_rows, half_rows, axis=1)
-        o_peer = exchange(lax.dynamic_slice_in_dim(o_own, (1 - mine) * half_rows, half_rows, axis=1))
+        o_other = lax.dynamic_slice_in_dim(o_own, (1 - mine) * half_rows, half_rows, axis=1)
+        o_peer = exchange(o_other)
         raw_upper = g_upper
         g_upper = switch(raw_upper)
         raw_lower, = attend_grad(own, other, do_all, o_all, lse, tuple(carried), 0, n_half, groups, dim)
@@ -447,8 +468,8 @@
             return g.reshape(1, -1, dim, model_dim).transpose(0, 3, 1, 2)
 
         y_blk = combine([o_mine[None]], wo, [o_peer[None]], wo_peer, DENSE_TILES)
-        grad_wo = product(o_own, dy_rows, DENSE_TILES).reshape(1, q_heads, dim, model_dim)
-        grad_wq, grad_wk, grad_wv = map(heads_last, weight_grads(g_mine, x_blk, g_other, x_peer, cols, dim, scale))
+        grad_wo = product(o_mine, dy_blk, o_other, dy_peer, DENSE_TILES).reshape(1, q_heads, dim, model_dim)
+        grad_wq, grad_wk, grad_wv = map(heads_last, weight_grads(g_mine, x_blk, g_other, (x_head, x_tail), cols, dim, scale))
         dx_blk = combine([g_mine], w_flat, [relay, g_tail], w_peer, DENSE_TILES)
         return y_blk, dx_blk, grad_wq, grad_wk, grad_wv, grad_wo
 

time: 436 us -> 451 us (1.034)
  blocking collectives: 24.5 us -> 0 us
  waiting for transfers between devices: 116 us -> 131 us
  starting transfers between devices: 33.3 us -> 46.8 us
  Pallas kernels: 225 us -> 233 us
  local copies, waits for them, and re-layouts: 8.83 us -> 13.9 us
    all_to_all x1 -> x0, blocking collectives: 24.5 us -> none  [switch(): return lax.all_to_all(a, 'cp', split_axis=0, concat_axis=0, tiled=True)]
    all_to_all x6 -> x9, starting transfers between devices: 24.3 us -> 36 us  [switch(): return lax.all_to_all(a, 'cp', split_axis=0, concat_axis=0, tiled=True)]
    ppermute x6 -> x8, waiting for transfers between devices: 36.2 us -> 47 us  [exchange(): return lax.ppermute(a, 'tp', swap)]
    all_to_all x6 -> x9, waiting for transfers between devices: 74.5 us -> 83.5 us  [switch(): return lax.all_to_all(a, 'cp', split_axis=0, concat_axis=0, tiled=True)]
    pallas_call x7 -> x9, Pallas kernels: 66.2 us -> 74.2 us  [dense_call(): pl.pallas_call(kernel, grid=(grid,), in_specs=in_specs, out_specs=out_spe...]
    all_gather x1 -> x0, waiting for transfers between devices: 4.79 us -> none  [device_fn(): dy_rows = lax.all_gather(dy_late, 'tp', axis=0, tiled=True)]
    ppermute x6 -> x8, starting transfers between devices: 8.89 us -> 10.7 us  [exchange(): return lax.ppermute(a, 'tp', swap)]
  transfers between devices with their start and end apart: 15 -> 19, of which waited for: 9 -> 9; matrix products, arithmetic and copies ran while one was open for 5% -> 4% of each run, Pallas kernels for 49% -> 50%
where the time goes in v6:
time: 451 us; the launch traced here: 450 us
  Pallas kernels  233 us (52%)
  waiting for transfers between devices  131 us (29%)
  starting transfers between devices  46.8 us (10%)
  between operations  14.2 us (3%)
  local copies, waits for them, and re-layouts  13.9 us (3%)
  other arithmetic  11.3 us (3%)
    pallas_call x2, Pallas kernels, attend_grad(): pl.pallas_call(lambda *refs: bwd_kernel(n_blk, groups, dim, first, count,...  98.4 us
    all_to_all x9, waiting for transfers between devices, switch(): return lax.all_to_all(a, 'cp', split_axis=0, concat_axis=0, tiled=True)  83.5 us
    pallas_call x9, Pallas kernels, dense_call(): pl.pallas_call(kernel, grid=(grid,), in_specs=in_specs, out_specs=out_spe...  74.2 us
    pallas_call x2, Pallas kernels, attend(): pl.pallas_call(lambda *refs: fwd_kernel(n_blk, groups, dim, first, *refs)...  60.4 us
    ppermute x8, waiting for transfers between devices, exchange(): return lax.ppermute(a, 'tp', swap)  47 us
    all_to_all x9, starting transfers between devices, switch(): return lax.all_to_all(a, 'cp', split_axis=0, concat_axis=0, tiled=True)  36 us
    ppermute x8, starting transfers between devices, exchange(): return lax.ppermute(a, 'tp', swap)  10.7 us
  transfers between devices with their start and end apart: 19, of which 9 were waited for; matrix products, arithmetic and copies ran while one was open for 4% of the time, Pallas kernels for 50%

profile of v6, /device:TPU:0, one launch (start us, length us, event | category | flops | bytes accessed | tf_op | source)
XLA Modules:
  0.0 449.8 jit_solution(16292819844893376491)
XLA Ops:
  13.8 6.0 %pad_maximum_fusion = bf16[4,384,2048]{2,1,0:T(8,128)(2,1)} fusion(bf16[4,64,2048]{2,1,0:T(8,128)(2,1)S(1)} %bitcast.27, bf16[4,64,2048]{2,1,0:T(8,128)(2,1)S(1)} %bitcast.28, bf16[4,256,2048]{2,1,0:T(8,128)(2,1)S(1)} %bitcast.25), kind=kLoop, calls=%fused_computation | loop fusion | flops 18874368 | bytes 12582912 | tf_op jit(solution)/shard_map/concatenate | solution.py:397
  19.8 8.3 %shard_map.109 = bf16[4,512,384]{2,1,0:T(8,128)(2,1)} custom-call(bf16[512,2048]{1,0:T(8,128)(2,1)} %x_ref.1, bf16[1536,2048]{1,0:T(8,128)(2,1)} %bitcast.20), custom_call_target="tpu_custom_call" | custom-call | flops 3221225472 | bytes 8388608 | tf_op jit(solution)/shard_map/pallas_call | solution.py:289
  28.1 8.6 %collective-permute-done.a_ref.xa_ref = bf16[256,2048]{1,0:T(8,128)(2,1)} collective-permute-done((bf16[256,2048]{1,0:T(8,128)(2,1)S(1)}, bf16[256,2048]{1,0:T(8,128)(2,1)}, u32[]{:S(2)}, u32[]{:S(2)}) %collective-permute-start) | collective-permute-done | bytes 1048608 | tf_op jit(solution)/shard_map/ppermute | solution.py:402
  44.8 6.2 %shard_map.110 = bf16[4,256,384]{2,1,0:T(8,128)(2,1)} custom-call(bf16[256,2048]{1,0:T(8,128)(2,1)} %collective-permute-done.a_ref.xa_ref, bf16[1536,2048]{1,0:T(8,128)(2,1)} %bitcast.22), custom_call_target="tpu_custom_call" | custom-call | flops 1610612736 | bytes 7340032 | tf_op jit(solution)/shard_map/pallas_call | solution.py:289
  50.9 9.3 %all-to-all-done.refs_0_.refs_3_ = bf16[4,512,384]{2,1,0:T(8,128)(2,1)S(1)} async-done(((bf16[4,512,384]{2,1,0:T(8,128)(2,1)}), bf16[4,512,384]{2,1,0:T(8,128)(2,1)S(1)}, u32[]{:S(2)}, u32[]{:S(2)}) %all-to-all-start) | async-done | bytes 1572896 | tf_op jit(solution)/shard_map/all_to_all | solution.py:405
  66.8 6.3 %shard_map.111 = bf16[4,512,256]{2,1,0:T(8,128)(2,1)} custom-call(bf16[512,2048]{1,0:T(8,128)(2,1)} %b_ref.1, bf16[1024,2048]{1,0:T(8,128)(2,1)} %bitcast.31), custom_call_target="tpu_custom_call" | custom-call | flops 2147483648 | bytes 6291456 | tf_op jit(solution)/shard_map/pallas_call | solution.py:289
  73.1 6.2 %shard_map.112 = bf16[4,256,384]{2,1,0:T(8,128)(2,1)} custom-call(bf16[256,2048]{1,0:T(8,128)(2,1)} %collective-permute-done.1.a_ref.xb_ref, bf16[1536,2048]{1,0:T(8,128)(2,1)} %bitcast.23), custom_call_target="tpu_custom_call" | custom-call | flops 1610612736 | bytes 7340032 | tf_op jit(solution)/shard_map/pallas_call | solution.py:289
  84.6 9.8 %all-to-all-done.2.refs_2_.refs_5_ = bf16[4,256,384]{2,1,0:T(8,128)(2,1)S(1)} async-done(((bf16[4,256,384]{2,1,0:T(8,128)(2,1)}), bf16[4,256,384]{2,1,0:T(8,128)(2,1)S(1)}, u32[]{:S(2)}, u32[]{:S(2)}) %all-to-all-start.2) | async-done | bytes 786464 | tf_op jit(solution)/shard_map/all_to_all | solution.py:405
  95.3 25.0 %attend_fwd.2 = (bf16[4,256,1024]{2,1,0:T(8,128)(2,1)}, f32[8,4,512]{2,1,0:T(4,128)}) custom-call(bf16[4,512,384]{2,1,0:T(8,128)(2,1)} %copy-done.2, bf16[4,256,384]{2,1,0:T(8,128)(2,1)} %all-to-all-done.1.refs_1_.refs_4_, bf16[4,256,384]{2,1,0:T(8,128)(2,1)} %copy-done.9, bf16[4,512,384]{2,1,0:T(8,128)(2,1)} %copy-done.2, ...), custom_call_target="tpu_custom_call" | custom-call | flops 16106127360 | bytes 2621440 | tf_op jit(solution)/shard_map/attend_fwd/pallas_call | solution.py:228
  120.3 10.9 %collective-permute-done.2.a_ref.bp_ref = bf16[512,2048]{1,0:T(8,128)(2,1)} collective-permute-done((bf16[512,2048]{1,0:T(8,128)(2,1)}, bf16[512,2048]{1,0:T(8,128)(2,1)}, u32[]{:S(2)}, u32[]{:S(2)}) %collective-permute-start.2) | collective-permute-done | bytes 2097184 | tf_op jit(solution)/shard_map/ppermute | solution.py:402
  132.9 35.4 %attend_fwd.3 = (bf16[4,256,1024]{2,1,0:T(8,128)(2,1)}, f32[8,4,512]{2,1,0:T(4,128)}) custom-call(bf16[4,512,384]{2,1,0:T(8,128)(2,1)} %copy-done.2, bf16[4,256,384]{2,1,0:T(8,128)(2,1)} %all-to-all-done.1.refs_1_.refs_4_, bf16[4,256,384]{2,1,0:T(8,128)(2,1)} %copy-done.9, ...), custom_call_target="tpu_custom_call", output_to_operand_aliasing={{0}: (6, {}), {1}: (7, {})} | custom-call | flops 22548578304 | bytes 1572864 | tf_op jit(solution)/shard_map/attend_fwd/pallas_call | solution.py:228
  174.0 6.8 %shard_map.113 = bf16[4,512,256]{2,1,0:T(8,128)(2,1)} custom-call(bf16[512,2048]{1,0:T(8,128)(2,1)} %collective-permute-done.2.a_ref.bp_ref, bf16[1024,2048]{1,0:T(8,128)(2,1)} %bitcast.32), custom_call_target="tpu_custom_call" | custom-call | flops 2147483648 | bytes 6291456 | tf_op jit(solution)/shard_map/pallas_call | solution.py:289
  180.8 18.2 %all-to-all-done.3.refs_6_ = bf16[4,512,256]{2,1,0:T(8,128)(2,1)} async-done(((bf16[4,512,256]{2,1,0:T(8,128)(2,1)}), bf16[4,512,256]{2,1,0:T(8,128)(2,1)}, u32[]{:S(2)}, u32[]{:S(2)}) %all-to-all-start.3) | async-done | bytes 1048608 | tf_op jit(solution)/shard_map/all_to_all | solution.py:405
  202.6 26.0 %all-to-all-done.4.refs_7_ = bf16[4,512,256]{2,1,0:T(8,128)(2,1)S(1)} async-done(((bf16[4,512,256]{2,1,0:T(8,128)(2,1)}), bf16[4,512,256]{2,1,0:T(8,128)(2,1)S(1)}, u32[]{:S(2)}, u32[]{:S(2)}) %all-to-all-start.4) | async-done | bytes 1048608 | tf_op jit(solution)/shard_map/all_to_all | solution.py:405
  233.2 70.2 %attend_bwd.2 = (bf16[4,384,512]{2,1,0:T(8,128)(2,1)}, f32[4,64,512]{2,1,0:T(8,128)}, f32[4,512,64]{2,1,0:T(8,128)}) custom-call(bf16[4,512,384]{2,1,0:T(8,128)(2,1)} %copy-done.2, bf16[4,256,384]{2,1,0:T(8,128)(2,1)} %all-to-all-done.1.refs_1_.refs_4_, bf16[4,256,384]{2,1,0:T(8,128)(2,1)} %copy-done.9, bf16[4,512,384]{2,1,0:T(8,128)(2,1)} %copy-done.2, ...), custom_call_target="tpu_custom_call" | custom-call | flops 69793218560 | bytes 4194304 | tf_op jit(solution)/shard_map/attend_bwd/pallas_call | solution.py:261
  303.5 28.2 %attend_bwd.3 = bf16[4,384,512]{2,1,0:T(8,128)(2,1)} custom-call(bf16[4,512,384]{2,1,0:T(8,128)(2,1)} %copy-done.2, bf16[4,256,384]{2,1,0:T(8,128)(2,1)} %all-to-all-done.1.refs_1_.refs_4_, bf16[4,256,384]{2,1,0:T(8,128)(2,1)} %copy-done.9, bf16[4,512,384]{2,1,0:T(8,128)(2,1)} %copy-done.2, bf16[4,256,384]{2,1,0:T(8,128)(2,1)} %all-to-all-done.1.refs_1_.refs_4_, ...), custom_call_target="tpu_custom_call" | custom-call | flops 26843545600 | bytes 4194304 | tf_op jit(solution)/shard_map/attend_bwd/pallas_call | solution.py:261
  336.1 20.1 %all-to-all-done.6 = bf16[4,384,512]{2,1,0:T(8,128)(2,1)} async-done(((bf16[4,384,512]{2,1,0:T(8,128)(2,1)}), bf16[4,384,512]{2,1,0:T(8,128)(2,1)}, u32[]{:S(2)}, u32[]{:S(2)}) %all-to-all-start.6) | async-done | bytes 1572896 | tf_op jit(solution)/shard_map/all_to_all | solution.py:405
  356.2 4.6 %all-to-all-start.7 = ((bf16[4,384,512]{2,1,0:T(8,128)(2,1)}), bf16[4,384,512]{2,1,0:T(8,128)(2,1)}, u32[]{:S(2)}, u32[]{:S(2)}) async-start(bf16[4,384,512]{2,1,0:T(8,128)(2,1)} %get-tuple-element.79), calls=%async_computation.7 | async-start | bytes 3145728 | tf_op jit(solution)/shard_map/all_to_all | solution.py:405
  366.1 8.6 %shard_map.117 = bf16[1024,2048]{1,0:T(8,128)(2,1)} custom-call(bf16[1024,512]{1,0:T(8,128)(2,1)} %get-tuple-element.87.a_ref, bf16[512,2048]{1,0:T(8,128)(2,1)} %b_ref.1, bf16[1024,512]{1,0:T(8,128)(2,1)} %get-tuple-element.86.ap_ref, bf16[512,2048]{1,0:T(8,128)(2,1)} %collective-permute-done.2.a_ref.bp_ref), custom_call_target="tpu_custom_call" | custom-call | flops 4294967296 | bytes 6291456 | tf_op jit(solution)/shard_map/pallas_call | solution.py:289
  374.7 13.9 %collective-permute-done.6 = bf16[4,256,512]{2,1,0:T(8,128)(2,1)} collective-permute-done((bf16[4,256,512]{2,1,0:T(8,128)(2,1)S(1)}, bf16[4,256,512]{2,1,0:T(8,128)(2,1)}, u32[]{:S(2)}, u32[]{:S(2)}) %collective-permute-start.6) | collective-permute-done | bytes 1048608 | tf_op jit(solution)/shard_map/ppermute | solution.py:402
  397.4 10.5 %shard_map.116 = (bf16[1024,2048]{1,0:T(8,128)(2,1)}, bf16[256,2048]{1,0:T(8,128)(2,1)}, bf16[256,2048]{1,0:T(8,128)(2,1)}) custom-call(bf16[4,384,512]{2,1,0:T(8,128)(2,1)} %get-tuple-element.85.refs_0_.g_ref, bf16[512,2048]{1,0:T(8,128)(2,1)} %x_ref.1, bf16[4,384,512]{2,1,0:T(8,128)(2,1)} %copy-done.1, ...), custom_call_target="tpu_custom_call" | custom-call | flops 6442450944 | bytes 7340032 | tf_op jit(solution)/shard_map/pallas_call | solution.py:289
  407.9 13.6 %collective-permute-done.7.refs_2_ = bf16[4,128,512]{2,1,0:T(8,128)(2,1)} collective-permute-done((bf16[4,128,512]{2,1,0:T(8,128)(2,1)}, bf16[4,128,512]{2,1,0:T(8,128)(2,1)}, u32[]{:S(2)}, u32[]{:S(2)}) %collective-permute-start.7) | collective-permute-done | bytes 524320 | tf_op jit(solution)/shard_map/ppermute | solution.py:402
  421.6 12.1 %shard_map.115 = bf16[512,2048]{1,0:T(8,128)(2,1)} custom-call(bf16[4,384,512]{2,1,0:T(8,128)(2,1)} %get-tuple-element.85.refs_0_.g_ref, bf16[4,256,512]{2,1,0:T(8,128)(2,1)} %all-to-all-done.8.refs_1_, bf16[4,128,512]{2,1,0:T(8,128)(2,1)} %collective-permute-done.7.refs_2_, bf16[1536,2048]{1,0:T(8,128)(2,1)} %bitcast.24, ...), custom_call_target="tpu_custom_call" | custom-call | flops 6442450944 | bytes 15728640 | tf_op jit(solution)/shard_map/pallas_call | solution.py:289
  433.7 9.3 %shard_map.114 = bf16[512,2048]{1,0:T(8,128)(2,1)} custom-call(bf16[1,1024,512]{2,1,0:T(8,128)(2,1)} %bitcast.29, bf16[1,1024,512]{2,1,0:T(8,128)(2,1)} %bitcast.8.refs_1_, bf16[1024,2048]{1,0:T(8,128)(2,1)} %bitcast.33, bf16[1024,2048]{1,0:T(8,128)(2,1)} %all-gather.5.cloned.1.call-done.refs_3_), custom_call_target="tpu_custom_call" | custom-call | flops 4294967296 | bytes 10485760 | tf_op jit(solution)/shard_map/pallas_call | solution.py:289
  (58 shorter events, 61.4 us)
Async XLA Ops:
  7.2 6.3 %copy-start = (bf16[2048,16,64]{0,2,1:T(8,128)(2,1)S(1)}, bf16[2048,16,64]{0,2,1:T(8,128)(2,1)}, u32[]{:S(2)}) copy-start(bf16[2048,16,64]{0,2,1:T(8,128)(2,1)} %param.7) | copy-start | bytes 12582916
  10.1 3.7 copy-start.6
  10.1 26.6 %collective-permute-start = (bf16[256,2048]{1,0:T(8,128)(2,1)S(1)}, bf16[256,2048]{1,0:T(8,128)(2,1)}, u32[]{:S(2)}, u32[]{:S(2)}) collective-permute-start(bf16[256,2048]{1,0:T(8,128)(2,1)S(1)} %get-tuple-element.89), channel_id=1, source_target_pairs={{0,4},{4,0},{1,5},{5,1},{2,6},{6,2},{3,7},{7,3}} | collective-permute-start | bytes 3145736 | tf_op jit(solution)/shard_map/ppermute | solution.py:402
  36.7 23.6 %all-to-all-start = ((bf16[4,512,384]{2,1,0:T(8,128)(2,1)}), bf16[4,512,384]{2,1,0:T(8,128)(2,1)S(1)}, u32[]{:S(2)}, u32[]{:S(2)}) async-start(bf16[4,512,384]{2,1,0:T(8,128)(2,1)} %shard_map.109), calls=%async_computation | async-start | bytes 3145728 | tf_op jit(solution)/shard_map/all_to_all | solution.py:405
  40.3 32.8 %collective-permute-start.1 = (bf16[256,2048]{1,0:T(8,128)(2,1)}, bf16[256,2048]{1,0:T(8,128)(2,1)}, u32[]{:S(2)}, u32[]{:S(2)}) collective-permute-start(bf16[256,2048]{1,0:T(8,128)(2,1)} %get-tuple-element.88), channel_id=1, source_target_pairs={{0,4},{4,0},{1,5},{5,1},{2,6},{6,2},{3,7},{7,3}} | collective-permute-start | bytes 3145736 | tf_op jit(solution)/shard_map/ppermute | solution.py:402
  60.3 12.8 %copy-start.2 = (bf16[4,512,384]{2,1,0:T(8,128)(2,1)}, bf16[4,512,384]{2,1,0:T(8,128)(2,1)S(1)}, u32[]{:S(2)}) copy-start(bf16[4,512,384]{2,1,0:T(8,128)(2,1)S(1)} %all-to-all-done.refs_0_.refs_3_) | copy-start | bytes 4718596
  60.3 19.0 %all-to-all-start.1 = ((bf16[4,256,384]{2,1,0:T(8,128)(2,1)}), bf16[4,256,384]{2,1,0:T(8,128)(2,1)}, u32[]{:S(2)}, u32[]{:S(2)}) async-start(bf16[4,256,384]{2,1,0:T(8,128)(2,1)} %shard_map.110), calls=%async_computation.1 | async-start | bytes 1572864 | tf_op jit(solution)/shard_map/all_to_all | solution.py:405
  79.3 15.1 %all-to-all-start.2 = ((bf16[4,256,384]{2,1,0:T(8,128)(2,1)}), bf16[4,256,384]{2,1,0:T(8,128)(2,1)S(1)}, u32[]{:S(2)}, u32[]{:S(2)}) async-start(bf16[4,256,384]{2,1,0:T(8,128)(2,1)} %shard_map.112), calls=%async_computation.2 | async-start | bytes 1572864 | tf_op jit(solution)/shard_map/all_to_all | solution.py:405
  82.8 48.4 %copy-start.4 = (bf16[384,2048]{1,0:T(8,128)(2,1)S(1)}, bf16[384,2048]{1,0:T(8,128)(2,1)}, u32[]{:S(2)}) copy-start(bf16[384,2048]{1,0:T(8,128)(2,1)} %constant_dynamic-slice_fusion.3) | copy-start | bytes 4718596
  82.8 220.6 %all-gather.3.cloned.1.call-start = ((), (), s32[]{:S(2)}) async-start(), calls=%async_computation.9 | async-start | bytes 7864320 | tf_op jit(solution)/shard_map/all_gather | solution.py:415
  82.8 48.3 %collective-permute-start.2 = (bf16[512,2048]{1,0:T(8,128)(2,1)}, bf16[512,2048]{1,0:T(8,128)(2,1)}, u32[]{:S(2)}, u32[]{:S(2)}) collective-permute-start(bf16[512,2048]{1,0:T(8,128)(2,1)} %b_ref.1), channel_id=1, source_target_pairs={{0,4},{4,0},{1,5},{5,1},{2,6},{6,2},{3,7},{7,3}} | collective-permute-start | bytes 6291464 | tf_op jit(solution)/shard_map/ppermute | solution.py:402
  131.2 37.2 %collective-permute-start.3 = (bf16[384,2048]{1,0:T(8,128)(2,1)S(1)}, bf16[384,2048]{1,0:T(8,128)(2,1)S(1)}, u32[]{:S(2)}, u32[]{:S(2)}) collective-permute-start(bf16[384,2048]{1,0:T(8,128)(2,1)S(1)} %copy-done.4), channel_id=1, source_target_pairs={{0,4},{4,0},{1,5},{5,1},{2,6},{6,2},{3,7},{7,3}} | collective-permute-start | bytes 4718600 | tf_op jit(solution)/shard_map/ppermute | solution.py:402
  169.5 29.5 %all-to-all-start.3 = ((bf16[4,512,256]{2,1,0:T(8,128)(2,1)}), bf16[4,512,256]{2,1,0:T(8,128)(2,1)}, u32[]{:S(2)}, u32[]{:S(2)}) async-start(bf16[4,512,256]{2,1,0:T(8,128)(2,1)} %shard_map.111), calls=%async_computation.3 | async-start | bytes 2097152 | tf_op jit(solution)/shard_map/all_to_all | solution.py:405
  180.8 21.8 %copy-start.7 = (bf16[256,2048]{1,0:T(8,128)(2,1)S(1)}, bf16[256,2048]{1,0:T(8,128)(2,1)}, u32[]{:S(2)}) copy-start(bf16[256,2048]{1,0:T(8,128)(2,1)} %constant_dynamic-slice_fusion.2) | copy-start | bytes 3145732
  199.0 29.6 %all-to-all-start.4 = ((bf16[4,512,256]{2,1,0:T(8,128)(2,1)}), bf16[4,512,256]{2,1,0:T(8,128)(2,1)S(1)}, u32[]{:S(2)}, u32[]{:S(2)}) async-start(bf16[4,512,256]{2,1,0:T(8,128)(2,1)} %shard_map.113), calls=%async_computation.4 | async-start | bytes 2097152 | tf_op jit(solution)/shard_map/all_to_all | solution.py:405
  202.5 100.9 %collective-permute-start.5 = (bf16[256,2048]{1,0:T(8,128)(2,1)S(1)}, bf16[256,2048]{1,0:T(8,128)(2,1)}, u32[]{:S(2)}, u32[]{:S(2)}) collective-permute-start(bf16[256,2048]{1,0:T(8,128)(2,1)S(1)} %copy-done.7), channel_id=1, source_target_pairs={{0,4},{4,0},{1,5},{5,1},{2,6},{6,2},{3,7},{7,3}} | collective-permute-start | bytes 3145736 | tf_op jit(solution)/shard_map/ppermute | solution.py:402
  229.5 73.9 %all-to-all-start.5 = ((bf16[4,256,1024]{2,1,0:T(8,128)(2,1)}), bf16[4,256,1024]{2,1,0:T(8,128)(2,1)S(1)}, u32[]{:S(2)}, u32[]{:S(2)}) async-start(bf16[4,256,1024]{2,1,0:T(8,128)(2,1)} %get-tuple-element.69.refs_8_), calls=%async_computation.5 | async-start | bytes 4194304 | tf_op jit(solution)/shard_map/all_to_all | solution.py:405
  233.2 200.5 %all-gather.5.cloned.1.call-start = ((), (), s32[]{:S(2)}) async-start(), calls=%async_computation.10 | async-start | bytes 5242880 | tf_op jit(solution)/shard_map/all_gather | solution.py:415
  331.7 24.5 %all-to-all-start.6 = ((bf16[4,384,512]{2,1,0:T(8,128)(2,1)}), bf16[4,384,512]{2,1,0:T(8,128)(2,1)}, u32[]{:S(2)}, u32[]{:S(2)}) async-start(bf16[4,384,512]{2,1,0:T(8,128)(2,1)} %attend_bwd.3), calls=%async_computation.6 | async-start | bytes 3145728 | tf_op jit(solution)/shard_map/all_to_all | solution.py:405
  356.2 32.4 %all-to-all-start.7 = ((bf16[4,384,512]{2,1,0:T(8,128)(2,1)}), bf16[4,384,512]{2,1,0:T(8,128)(2,1)}, u32[]{:S(2)}, u32[]{:S(2)}) async-start(bf16[4,384,512]{2,1,0:T(8,128)(2,1)} %get-tuple-element.79), calls=%async_computation.7 | async-start | bytes 3145728 | tf_op jit(solution)/shard_map/all_to_all | solution.py:405
  362.4 26.2 %collective-permute-start.6 = (bf16[4,256,512]{2,1,0:T(8,128)(2,1)S(1)}, bf16[4,256,512]{2,1,0:T(8,128)(2,1)}, u32[]{:S(2)}, u32[]{:S(2)}) collective-permute-start(bf16[4,256,512]{2,1,0:T(8,128)(2,1)S(1)} %slice_select_fusion), channel_id=1, source_target_pairs={{0,4},{4,0},{1,5},{5,1},{2,6},{6,2},{3,7},{7,3}} | collective-permute-start | bytes 3145736 | tf_op jit(solution)/shard_map/ppermute | solution.py:402
  364.1 69.6 %collective-permute-start.4 = (bf16[1024,512]{1,0:T(8,128)(2,1)}, bf16[1024,512]{1,0:T(8,128)(2,1)}, u32[]{:S(2)}, u32[]{:S(2)}) collective-permute-start(bf16[1024,512]{1,0:T(8,128)(2,1)} %get-tuple-element.86.ap_ref), channel_id=1, source_target_pairs={{0,4},{4,0},{1,5},{5,1},{2,6},{6,2},{3,7},{7,3}} | collective-permute-start | bytes 3145736 | tf_op jit(solution)/shard_map/ppermute | solution.py:402
  388.6 33.0 %all-to-all-start.8 = ((bf16[4,256,512]{2,1,0:T(8,128)(2,1)}), bf16[4,256,512]{2,1,0:T(8,128)(2,1)}, u32[]{:S(2)}, u32[]{:S(2)}) async-start(bf16[4,256,512]{2,1,0:T(8,128)(2,1)} %collective-permute-done.6), calls=%async_computation.8 | async-start | bytes 2097152 | tf_op jit(solution)/shard_map/all_to_all | solution.py:405
  397.0 24.6 %collective-permute-start.7 = (bf16[4,128,512]{2,1,0:T(8,128)(2,1)}, bf16[4,128,512]{2,1,0:T(8,128)(2,1)}, u32[]{:S(2)}, u32[]{:S(2)}) collective-permute-start(bf16[4,128,512]{2,1,0:T(8,128)(2,1)} %slice.21), channel_id=1, source_target_pairs={{0,4},{4,0},{1,5},{5,1},{2,6},{6,2},{3,7},{7,3}} | collective-permute-start | bytes 1572872 | tf_op jit(solution)/shard_map/ppermute | solution.py:402
  (5 other events, 8.0 us)
Sparse Core Ops, SparseCore 0:
  169.6 65.4 all-gather.2
  303.6 32.0 all-gather.4
